TPU v7x, 32 devices: a 4x4x1 block of a 4x4x8 slice. The times are simulated.
32 devices in a mesh: data: 1 (over z), dap: 32 (over y, x, core).
Axes of the slice: x: 4, y: 4, z: 1, core: 2. Of those that a mesh axis runs over, the one named last changes fastest.
The devices are a block of a 4x4x8 slice.
Arguments:
- msa_act: bfloat16 [4096, 128, 64], P(('data', 'dap'))
- pair_act: bfloat16 [128, 128, 128], P(('data', 'dap'))
- msa_mask: int32 [4096, 128], P('data')
- res_mask: int32 [128], P('data')
- row_bias_w: bfloat16 [128, 8], replicated
- row_qkvg_w: bfloat16 [64, 4, 8, 8], replicated
- row_out_w: bfloat16 [8, 8, 64], replicated
- col_query_w: bfloat16 [64, 8, 8], replicated
- col_kv_w: bfloat16 [64, 2, 8], replicated
- col_gate_w: bfloat16 [64, 8, 8], replicated
- col_out_w: bfloat16 [8, 8, 64], replicated
- opm_proj_w: bfloat16 [64, 2, 32], replicated
- opm_out_w: bfloat16 [32, 32, 128], replicated
- start_bias_w: bfloat16 [128, 4], replicated
- start_qkvg_w: bfloat16 [128, 4, 4, 32], replicated
- start_out_w: bfloat16 [4, 32, 128], replicated
- end_bias_w: bfloat16 [128, 4], replicated
- end_qkvg_w: bfloat16 [128, 4, 4, 32], replicated
- end_out_w: bfloat16 [4, 32, 128], replicated
Outputs:
- output 1: bfloat16 [4096, 128, 64], P(('data', 'dap'))
- output 2: bfloat16 [128, 128, 128], P(('data', 'dap'))
All inputs are finite; a program needn't handle non-finite values.
Results may differ from a plain program's by a relative error of at most 0.0149318.
Values are sent between devices in bfloat16 or wider.
A program may use at most 768 MiB of HBM per device.

v0:
```python
import jax
import jax.numpy as jnp
from jax import lax
from jax.sharding import PartitionSpec as P


def layer_norm(values):
    widened = values.astype(jnp.float32)
    mean_val = jnp.mean(widened, axis=-1, keepdims=True)
    centered = widened - mean_val
    variance = jnp.mean(centered * centered, axis=-1, keepdims=True)
    return (centered * lax.rsqrt(variance + 1e-5)).astype(jnp.bfloat16)


def mask_bias(mask_vals):
    return (mask_vals.astype(jnp.float32) - 1.0) * 1e4


def matmul_bf(einsum_form, left_arr, right_arr):
    return jnp.einsum(einsum_form, left_arr, right_arr, preferred_element_type=jnp.float32).astype(jnp.bfloat16)


def gated_out(einsum_form, gate_proj, attended, out_w):
    gated_vals = (jax.nn.sigmoid(gate_proj.astype(jnp.float32)) * attended).astype(jnp.bfloat16)
    return jnp.einsum(einsum_form, gated_vals, out_w, preferred_element_type=jnp.float32)


def row_attention(value_a7, bias_full, seq_mask, qkvg_w, out_w):
    projected = matmul_bf('sic,cahd->asihd', layer_norm(value_a7), qkvg_w)
    logits = jnp.einsum('sihd,sjhd->shij', projected[0], projected[1], preferred_element_type=jnp.float32) * (qkvg_w.shape[-1] ** -0.5) + bias_full[None] + mask_bias(seq_mask)[:, None, None, :]
    attn_probs = jax.nn.softmax(logits, axis=-1).astype(jnp.bfloat16)
    attended = jnp.einsum('shij,sjhd->sihd', attn_probs, projected[2], preferred_element_type=jnp.float32)
    return (value_a7 + gated_out('sihd,hdc->sic', projected[3], attended, out_w)).astype(jnp.bfloat16)


def column_attention(value_a7, col_mask, query_w, kv_w, gate_w, out_w):
    value_a6 = layer_norm(value_a7)
    mask_count = jnp.sum(col_mask, axis=0).astype(jnp.float32) + 1e-10
    mean_query = (jnp.einsum('sr,src->rc', col_mask.astype(jnp.bfloat16), value_a6, preferred_element_type=jnp.float32) / mask_count[:, None]).astype(jnp.bfloat16)
    query_proj = matmul_bf('rc,chd->rhd', mean_query, query_w)
    key_val = matmul_bf('src,cad->asrd', value_a6, kv_w)
    gate_proj = matmul_bf('src,chd->srhd', value_a6, gate_w)
    logits = jnp.einsum('rhd,srd->rhs', query_proj, key_val[0], preferred_element_type=jnp.float32) * (kv_w.shape[-1] ** -0.5) + mask_bias(col_mask).T[:, None, :]
    attn_probs = jax.nn.softmax(logits, axis=-1).astype(jnp.bfloat16)
    attended = jnp.einsum('rhs,srd->rhd', attn_probs, key_val[1], preferred_element_type=jnp.float32)
    return (value_a7 + gated_out('srhd,hdc->src', gate_proj, attended[None], out_w)).astype(jnp.bfloat16)


def outer_update(pair_act, left_proj, right_full, counts, out_w):
    outer_sum = matmul_bf('sie,sjf->ijef', left_proj, right_full)
    update = jnp.einsum('ijef,efc->ijc', outer_sum, out_w, preferred_element_type=jnp.float32) / (1e-3 + counts)[:, :, None]
    return (pair_act + update).astype(jnp.bfloat16)


def triangle_rows(pair_act, pair_ln, bias_full, res_mask, qkvg_w, out_w):
    projected = matmul_bf('ijc,cahd->aijhd', pair_ln, qkvg_w)
    logits = jnp.einsum('ijhd,ikhd->ihjk', projected[0], projected[1], preferred_element_type=jnp.float32) * (qkvg_w.shape[-1] ** -0.5) + bias_full[None] + mask_bias(res_mask)[None, None, None, :]
    attn_probs = jax.nn.softmax(logits, axis=-1).astype(jnp.bfloat16)
    attended = jnp.einsum('ihjk,ikhd->ijhd', attn_probs, projected[2], preferred_element_type=jnp.float32)
    return (pair_act + gated_out('ijhd,hdc->ijc', projected[3], attended, out_w)).astype(jnp.bfloat16)


def triangle_cols(pair_cols, pair_ln, bias_full, res_mask, qkvg_w, out_w):
    projected = matmul_bf('ijc,cahd->aijhd', pair_ln, qkvg_w)
    logits = jnp.einsum('ijhd,kjhd->jhik', projected[0], projected[1], preferred_element_type=jnp.float32) * (qkvg_w.shape[-1] ** -0.5) + bias_full[None] + mask_bias(res_mask)[None, None, None, :]
    attn_probs = jax.nn.softmax(logits, axis=-1).astype(jnp.bfloat16)
    attended = jnp.einsum('jhik,kjhd->ijhd', attn_probs, projected[2], preferred_element_type=jnp.float32)
    return (pair_cols + gated_out('ijhd,hdc->ijc', projected[3], attended, out_w)).astype(jnp.bfloat16)


def solution(mesh):
    def evoformer_block(value_a7, pair_act, array_b8, res_mask, row_bias_w, row_qkvg_w, row_out_w, col_query_w, col_kv_w, col_gate_w, col_out_w, opm_proj_w, opm_out_w, start_bias_w, start_qkvg_w, start_out_w, end_bias_w, end_qkvg_w, end_out_w):
        seq_local = value_a7.shape[0]
        res_local = pair_act.shape[0]
        dev_index = lax.axis_index('dap')
        seq_mask = lax.dynamic_slice_in_dim(array_b8, dev_index * seq_local, seq_local, axis=0)
        col_mask = lax.dynamic_slice_in_dim(array_b8, dev_index * res_local, res_local, axis=1)

        row_bias = matmul_bf('ijc,ch->hij', layer_norm(pair_act), row_bias_w)
        row_bias_full = lax.all_gather(row_bias, 'dap', axis=1, tiled=True)
        value_a7 = row_attention(value_a7, row_bias_full, seq_mask, row_qkvg_w, row_out_w)

        value_a8 = lax.all_to_all(value_a7, 'dap', 1, 0, tiled=True)
        value_a8 = column_attention(value_a8, col_mask, col_query_w, col_kv_w, col_gate_w, col_out_w)

        projected = matmul_bf('src,cae->asre', layer_norm(value_a8), opm_proj_w) * col_mask.astype(jnp.bfloat16)[None, :, :, None]
        right_full = lax.all_gather(projected[1], 'dap', axis=1, tiled=True)
        counts = jnp.einsum('si,sj->ij', col_mask.astype(jnp.bfloat16), array_b8.astype(jnp.bfloat16), preferred_element_type=jnp.float32)
        pair_act = outer_update(pair_act, projected[0], right_full, counts, opm_out_w)
        array_b7 = lax.all_to_all(value_a8, 'dap', 0, 1, tiled=True)

        pair_ln = layer_norm(pair_act)
        start_full = lax.all_gather(matmul_bf('ijc,ch->hij', pair_ln, start_bias_w), 'dap', axis=1, tiled=True)
        pair_act = triangle_rows(pair_act, pair_ln, start_full, res_mask, start_qkvg_w, start_out_w)

        pair_cols = lax.all_to_all(pair_act, 'dap', 1, 0, tiled=True)
        cols_ln = layer_norm(pair_cols)
        end_full = lax.all_gather(matmul_bf('ijc,ch->hji', cols_ln, end_bias_w), 'dap', axis=1, tiled=True)
        pair_cols = triangle_cols(pair_cols, cols_ln, end_full, res_mask, end_qkvg_w, end_out_w)
        pair_out = lax.all_to_all(pair_cols, 'dap', 0, 1, tiled=True)
        return array_b7, pair_out

    row_spec = P(('data', 'dap'), None, None)
    in_specs = (row_spec, row_spec, P('data', None), P('data')) + (P(),) * 15
    return jax.shard_map(evoformer_block, mesh=mesh, in_specs=in_specs, out_specs=(row_spec, row_spec), check_vma=False)
```

profile of v0, /device:TPU:97, one launch (start us, length us, event | category | flops | bytes accessed | tf_op | source)
XLA Modules:
  0.0 453.7 jit_solution(4095918111355887711)
XLA Ops:
  7.2 1.2 copy.156
  9.4 32.5 %all_gather.12 = bf16[8,128,128]{2,0,1:T(8,128)(2,1)S(1)} all-gather(bf16[8,4,128]{2,0,1:T(8,128)(2,1)S(1)} %fusion.83), channel_id=1, replica_groups=mesh['data'=1,'dap'=32] {'dap'}, dimensions={1}, use_global_device_ids=true | all-gather | bytes 270336 | tf_op jit(solution)/shard_map/all_gather | solution.py:80
  42.1 2.2 convert_reduce_fusion
  46.2 5.5 %convert_bitcast_fusion = bf16[4,128,128,8,8]{2,4,3,0,1:T(8,128)(2,1)} fusion(bf16[128,128,64]{1,2,0:T(8,128)(2,1)S(1)} %copy-done.1, f32[128,128]{1,0:T(8,128)S(1)} %add_rsqrt_fusion.2, f32[128,128]{1,0:T(8,128)S(1)} %broadcast_multiply_fusion.3, bf16[64,4,8,8]{0,3,2,1:T(8,128)(2,1)S(1)} %copy-done.9), kind=kOutput, calls=%fused_computation.14 | convolution fusion | flops 545259520 | bytes 10649600 | tf_op jit(solution)/shard_map/sic,cahd->asihd/dot_general | solution.py:20
  51.7 32.8 %fusion.163 = (f32[128,8,128]{2,1,0:T(8,128)}, f32[128,8,128,128]{2,3,1,0:T(8,128)}) fusion(f32[128,128]{1,0:T(8,128)S(1)} %add_multiply_fusion, f32[8,128,128]{1,2,0:T(8,128)S(1)} %copy.158, bf16[4,128,128,8,8]{2,4,3,0,1:T(8,128)(2,1)} %convert_bitcast_fusion), kind=kOutput, calls=%fused_computation.220 | convolution fusion | flops 352321664 | bytes 72417280 | tf_op jit(solution)/shard_map/sub | solution.py:31
  84.5 25.8 %fusion.40 = bf16[128,128,64]{1,2,0:T(8,128)(2,1)} fusion(bf16[128,128,64]{1,2,0:T(8,128)(2,1)S(1)} %copy-done.1, f32[128,8,128,128]{2,3,1,0:T(8,128)} %get-tuple-element.17, f32[128,8,128]{2,1,0:T(8,128)} %get-tuple-element.16, bf16[4,128,128,8,8]{2,4,3,0,1:T(8,128)(2,1)} %convert_bitcast_fusion, bf16[8,8,64]{2,1,0:T(8,128)(2,1)S(1)} %copy-done.13), kind=kOutput, calls=%fused_computation.55 | convolution fusion | flops 445644800 | bytes 76029952 | tf_op jit(solution)/shard_map/sihd,hdc->sic/dot_general | solution.py:25
  110.3 4.6 %copy.160 = bf16[128,128,64]{0,2,1:T(8,128)(2,1)} copy(bf16[128,128,64]{1,2,0:T(8,128)(2,1)} %fusion.40) | data formatting | bytes 4194304 | tf_op jit(solution)/shard_map/convert_element_type | solution.py:33
  114.9 9.5 %all-to-all-start = ((bf16[128,128,64]{0,2,1:T(8,128)(2,1)}), bf16[128,128,64]{0,2,1:T(8,128)(2,1)S(1)}, u32[]{:S(2)}, u32[]{:S(2)}) async-start(bf16[128,128,64]{0,2,1:T(8,128)(2,1)} %copy.160), calls=%async_computation | async-start | bytes 4194304 | tf_op jit(solution)/shard_map/all_to_all | solution.py:83
  124.7 3.5 fusion.162
  128.3 2.2 copy.215
  130.6 21.6 %all-to-all-done = bf16[128,128,64]{0,2,1:T(8,128)(2,1)S(1)} async-done(((bf16[128,128,64]{0,2,1:T(8,128)(2,1)}), bf16[128,128,64]{0,2,1:T(8,128)(2,1)S(1)}, u32[]{:S(2)}, u32[]{:S(2)}) %all-to-all-start) | async-done | bytes 2097184 | tf_op jit(solution)/shard_map/all_to_all | solution.py:83
  156.4 3.3 convert_reduce_fusion.1
  159.7 2.3 fusion.36
  162.0 2.6 fusion.29
  164.6 1.3 copy-done.6
  167.3 108.0 %all-gather.3.cloned.1.call-done = bf16[1,4096,128,32]{1,3,0,2:T(8,128)(2,1)} async-done(((bf16[1,4096,4,32]{1,3,0,2:T(8,128)(2,1)}), bf16[1,4096,128,32]{1,3,0,2:T(8,128)(2,1)}) %all-gather.3.cloned.1.call-update) | async-done | bytes 33554448 | tf_op jit(solution)/shard_map/all_gather | solution.py:87
  275.3 22.6 %convert_bitcast_fusion.3 = bf16[4,128,32,32]{2,3,0,1:T(8,128)(2,1)} fusion(bf16[1,4096,128,32]{1,3,0,2:T(8,128)(2,1)} %all-gather.3.cloned.1.call-done, bf16[2,4096,4,32]{1,3,0,2:T(8,128)(2,1)} %copy-done.6), kind=kOutput, calls=%fused_computation.61 | convolution fusion | flops 4295491584 | bytes 35651584 | tf_op jit(solution)/shard_map/sie,sjf->ijef/dot_general | solution.py:20
  297.9 7.0 %copy.170 = bf16[4,128,32,32]{1,3,2,0:T(8,128)(2,1)S(1)} copy(bf16[4,128,32,32]{2,3,0,1:T(8,128)(2,1)} %convert_bitcast_fusion.3) | data formatting | bytes 2097152 | tf_op jit(solution)/shard_map/convert_element_type | solution.py:20
  305.9 27.7 %all_gather.14 = bf16[4,128,128]{2,0,1:T(4,128)(2,1)S(1)} all-gather(bf16[4,4,128]{2,0,1:T(4,128)(2,1)S(1)} %fusion.84), channel_id=1, replica_groups=mesh['data'=1,'dap'=32] {'dap'}, dimensions={1}, use_global_device_ids=true | all-gather | bytes 135168 | tf_op jit(solution)/shard_map/all_gather | solution.py:93
  334.4 2.5 fusion.172
  336.9 1.6 fusion.76
  339.4 9.8 %all-to-all-start.2 = ((bf16[4,128,128]{2,0,1:T(4,128)(2,1)}), bf16[4,128,128]{2,0,1:T(4,128)(2,1)S(1)}, u32[]{:S(2)}, u32[]{:S(2)}) async-start(bf16[4,128,128]{2,0,1:T(4,128)(2,1)} %copy.177), calls=%async_computation.2 | async-start | bytes 262144 | tf_op jit(solution)/shard_map/all_to_all | solution.py:96
  349.2 4.7 %copy.167 = bf16[4096,4,64]{2,1,0:T(4,128)(2,1)} copy(bf16[4096,4,64]{0,2,1:T(8,128)(2,1)S(1)} %copy-done.3) | data formatting | bytes 4194304 | tf_op jit(solution)/shard_map/convert_element_type | solution.py:46
  353.9 8.6 %reshape.203 = bf16[32,2,16384]{2,1,0:T(2,128)(2,1)} reshape(bf16[4096,4,64]{2,1,0:T(4,128)(2,1)} %copy.167) | data formatting | bytes 4194304
  362.5 6.4 %all-to-all-start.1 = ((bf16[32,2,16384]{2,1,0:T(2,128)(2,1)}), bf16[32,2,16384]{2,1,0:T(2,128)(2,1)S(1)}, u32[]{:S(2)}, u32[]{:S(2)}) async-start(bf16[32,2,16384]{2,1,0:T(2,128)(2,1)} %reshape.203), calls=%async_computation.1 | async-start | bytes 4194304 | tf_op jit(solution)/shard_map/all_to_all | solution.py:90
  371.0 46.7 %all_gather.15 = bf16[4,128,128]{2,0,1:T(4,128)(2,1)S(1)} all-gather(bf16[4,4,128]{2,0,1:T(4,128)(2,1)S(1)} %fusion.85), channel_id=1, replica_groups=mesh['data'=1,'dap'=32] {'dap'}, dimensions={1}, use_global_device_ids=true | all-gather | bytes 135168 | tf_op jit(solution)/shard_map/all_gather | solution.py:98
  418.3 1.5 fusion.173
  419.9 1.7 fusion.75
  422.3 10.6 %all-to-all-start.3 = ((bf16[128,4,128]{2,1,0:T(4,128)(2,1)}), bf16[128,4,128]{2,1,0:T(4,128)(2,1)S(1)}, u32[]{:S(2)}, u32[]{:S(2)}) async-start(bf16[128,4,128]{2,1,0:T(4,128)(2,1)} %copy.188), calls=%async_computation.3 | async-start | bytes 262144 | tf_op jit(solution)/shard_map/all_to_all | solution.py:100
  432.9 4.0 reshape.204
  436.9 5.4 %copy.211 = bf16[32,128,4,64]{1,3,2,0:T(8,128)(2,1)S(1)} copy(bf16[32,128,4,64]{3,2,1,0:T(4,128)(2,1)} %bitcast.350) | data formatting | bytes 4194304 | tf_op jit(solution)/shard_map/all_to_all | solution.py:90
  442.4 3.3 copy.190
  (98 shorter events, 15.6 us)
Async XLA Ops:
  7.2 297.7 %copy-start = (bf16[32,32,128]{2,1,0:T(8,128)(2,1)S(1)}, bf16[32,32,128]{2,1,0:T(8,128)(2,1)}, u32[]{:S(2)}) copy-start(bf16[32,32,128]{2,1,0:T(8,128)(2,1)} %param.31) | copy-start | bytes 786436
  7.2 37.1 %copy-start.1 = (bf16[128,128,64]{1,2,0:T(8,128)(2,1)S(1)}, bf16[128,128,64]{1,2,0:T(8,128)(2,1)}, u32[]{:S(2)}) copy-start(bf16[128,128,64]{1,2,0:T(8,128)(2,1)} %param.19) | copy-start | bytes 6291460
  7.2 38.9 %copy-start.9 = (bf16[64,4,8,8]{0,3,2,1:T(8,128)(2,1)S(1)}, bf16[64,4,8,8]{0,3,2,1:T(8,128)(2,1)}, u32[]{:S(2)}) copy-start(bf16[64,4,8,8]{0,3,2,1:T(8,128)(2,1)} %param.24) | copy-start | bytes 98308
  8.4 43.3 %copy-start.4 = (bf16[4,128,128]{1,2,0:T(8,128)(2,1)}, bf16[4,128,128]{1,2,0:T(8,128)(2,1)S(1)}, u32[]{:S(2)}) copy-start(bf16[4,128,128]{1,2,0:T(8,128)(2,1)S(1)} %copy.156) | copy-start | bytes 393220
  51.7 32.8 %copy-start.13 = (bf16[8,8,64]{2,1,0:T(8,128)(2,1)S(1)}, bf16[8,8,64]{2,1,0:T(8,128)(2,1)}, u32[]{:S(2)}) copy-start(bf16[8,8,64]{2,1,0:T(8,128)(2,1)} %param.25) | copy-start | bytes 24580
  114.9 37.2 %all-to-all-start = ((bf16[128,128,64]{0,2,1:T(8,128)(2,1)}), bf16[128,128,64]{0,2,1:T(8,128)(2,1)S(1)}, u32[]{:S(2)}, u32[]{:S(2)}) async-start(bf16[128,128,64]{0,2,1:T(8,128)(2,1)} %copy.160), calls=%async_computation | async-start | bytes 4194304 | tf_op jit(solution)/shard_map/all_to_all | solution.py:83
  124.4 150.8 %all-gather.3.cloned.1.call-start = ((), (), s32[]{:S(2)}) async-start(), calls=%async_computation.4 | async-start | bytes 34603008 | tf_op jit(solution)/shard_map/all_gather | solution.py:87
  152.1 2.4 copy-start.14
  152.1 2.6 copy-start.18
  154.7 1.6 copy-start.15
  154.7 1.6 copy-start.16
  156.4 5.6 %copy-start.17 = (bf16[64,2,32]{0,2,1:T(8,128)(2,1)S(1)}, bf16[64,2,32]{0,2,1:T(8,128)(2,1)}, u32[]{:S(2)}) copy-start(bf16[64,2,32]{0,2,1:T(8,128)(2,1)} %param.30) | copy-start | bytes 24580
  162.0 5.1 %copy-start.19 = (s32[128]{0:T(128)S(1)}, s32[128]{0:T(128)}, u32[]{:S(2)}) copy-start(s32[128]{0:T(128)} %param.22) | copy-start | bytes 1540
  162.0 5.1 %copy-start.2 = (s32[4096,128]{1,0:T(8,128)S(1)}, s32[4096,128]{1,0:T(8,128)}, u32[]{:S(2)}) copy-start(s32[4096,128]{1,0:T(8,128)} %param.21) | copy-start | bytes 6291460
  164.6 1.3 copy-start.6
  297.9 7.0 %copy-start.5 = (bf16[4,128,128]{1,2,0:T(8,128)(2,1)S(1)}, bf16[4,128,128]{1,2,0:T(8,128)(2,1)}, u32[]{:S(2)}) copy-start(bf16[4,128,128]{1,2,0:T(8,128)(2,1)} %copy-done.4) | copy-start | bytes 393220
  297.9 7.5 %copy-start.7 = (bf16[128,4,4,32]{0,3,2,1:T(8,128)(2,1)S(1)}, bf16[128,4,4,32]{0,3,2,1:T(8,128)(2,1)}, u32[]{:S(2)}) copy-start(bf16[128,4,4,32]{0,3,2,1:T(8,128)(2,1)} %param.33) | copy-start | bytes 393220
  297.9 7.8 %copy-start.10 = (bf16[128,4]{0,1:T(4,128)(2,1)S(1)}, bf16[128,4]{0,1:T(4,128)(2,1)}, u32[]{:S(2)}) copy-start(bf16[128,4]{0,1:T(4,128)(2,1)} %param.32) | copy-start | bytes 3076
  304.9 32.0 %copy-start.12 = (bf16[4,32,128]{2,1,0:T(8,128)(2,1)S(1)}, bf16[4,32,128]{2,1,0:T(8,128)(2,1)}, u32[]{:S(2)}) copy-start(bf16[4,32,128]{2,1,0:T(8,128)(2,1)} %param.34) | copy-start | bytes 98308
  333.6 15.6 %copy-start.3 = (bf16[4096,4,64]{0,2,1:T(8,128)(2,1)S(1)}, bf16[4096,4,64]{0,2,1:T(8,128)(2,1)}, u32[]{:S(2)}) copy-start(bf16[4096,4,64]{0,2,1:T(8,128)(2,1)} %get-tuple-element.19) | copy-start | bytes 6291460
  339.4 23.1 %all-to-all-start.2 = ((bf16[4,128,128]{2,0,1:T(4,128)(2,1)}), bf16[4,128,128]{2,0,1:T(4,128)(2,1)S(1)}, u32[]{:S(2)}, u32[]{:S(2)}) async-start(bf16[4,128,128]{2,0,1:T(4,128)(2,1)} %copy.177), calls=%async_computation.2 | async-start | bytes 262144 | tf_op jit(solution)/shard_map/all_to_all | solution.py:96
  362.5 8.1 %copy-start.11 = (bf16[128,4]{0,1:T(4,128)(2,1)S(1)}, bf16[128,4]{0,1:T(4,128)(2,1)}, u32[]{:S(2)}) copy-start(bf16[128,4]{0,1:T(4,128)(2,1)} %param.35) | copy-start | bytes 3076
  362.5 55.4 %copy-start.8 = (bf16[128,4,4,32]{0,3,2,1:T(8,128)(2,1)S(1)}, bf16[128,4,4,32]{0,3,2,1:T(8,128)(2,1)}, u32[]{:S(2)}) copy-start(bf16[128,4,4,32]{0,3,2,1:T(8,128)(2,1)} %param.36) | copy-start | bytes 393220
  362.5 59.8 %all-to-all-start.1 = ((bf16[32,2,16384]{2,1,0:T(2,128)(2,1)}), bf16[32,2,16384]{2,1,0:T(2,128)(2,1)S(1)}, u32[]{:S(2)}, u32[]{:S(2)}) async-start(bf16[32,2,16384]{2,1,0:T(2,128)(2,1)} %reshape.203), calls=%async_computation.1 | async-start | bytes 4194304 | tf_op jit(solution)/shard_map/all_to_all | solution.py:90
  422.3 23.4 %all-to-all-start.3 = ((bf16[128,4,128]{2,1,0:T(4,128)(2,1)}), bf16[128,4,128]{2,1,0:T(4,128)(2,1)S(1)}, u32[]{:S(2)}, u32[]{:S(2)}) async-start(bf16[128,4,128]{2,1,0:T(4,128)(2,1)} %copy.188), calls=%async_computation.3 | async-start | bytes 262144 | tf_op jit(solution)/shard_map/all_to_all | solution.py:100
Sparse Core Ops, SparseCore 0:
  167.1 108.0 all-gather.2
where the time goes:
time: 460 us; the launch traced here: 454 us
  waiting for transfers between devices  130 us (28%)
  blocking collectives  107 us (23%)
  matrix products  105 us (23%)
  local copies, waits for them, and re-layouts  47.9 us (10%)
  starting transfers between devices  36.6 us (8%)
  between operations  15 us (3%)
  other arithmetic  12.5 us (3%)
    all_gather x1, waiting for transfers between devices, evoformer_block(): right_full = lax.all_gather(projected[1], 'dap', axis=1, tiled=True)  108 us
    all_gather x1, blocking collectives, evoformer_block(): lax.all_gather(matmul_bf('ijc,ch->hji', cols_ln, end_bias_w), 'dap', axis...  46.7 us
    dot_general x10, matrix products, matmul_bf(): jnp.einsum(einsum_form, left_arr, right_arr, preferred_element_type=jnp.f...  33.6 us
    sub x1, matrix products, row_attention(): attn_probs = jax.nn.softmax(logits, axis=-1).astype(jnp.bfloat16)  32.8 us
    all_gather x1, blocking collectives, evoformer_block(): row_bias_full = lax.all_gather(row_bias, 'dap', axis=1, tiled=True)  32.5 us
    dot_general x4, matrix products, gated_out(): jnp.einsum(einsum_form, gated_vals, out_w, preferred_element_type=jnp.flo...  32.4 us
    all_gather x1, blocking collectives, evoformer_block(): lax.all_gather(matmul_bf('ijc,ch->hij', pair_ln, start_bias_w), 'dap', ax...  27.7 us
    all_to_all x1, waiting for transfers between devices, evoformer_block(): value_a8 = lax.all_to_all(value_a7, 'dap', 1, 0, tiled=True)  21.6 us
  transfers between devices with their start and end apart: 5, of which 2 were waited for; matrix products, arithmetic and copies ran while one was open for 9% of the time, Pallas kernels for 0%

commit v1 on v0

v1 whole, which is shorter than its diff:
```python
import functools
import math

import jax
import jax.numpy as jnp
from jax import lax
from jax.experimental import pallas as pl
from jax.experimental.pallas import tpu as pltpu
from jax.sharding import PartitionSpec as P

MESH = pl.DeviceIdType.MESH
F32 = jnp.float32
BF16 = jnp.bfloat16


def layer_norm(values):
    widened = values.astype(F32)
    mean_val = jnp.mean(widened, axis=-1, keepdims=True)
    centered = widened - mean_val
    variance = jnp.mean(centered * centered, axis=-1, keepdims=True)
    return (centered * lax.rsqrt(variance + 1e-5)).astype(BF16)


def mask_bias(mask_vals):
    return (mask_vals.astype(F32) - 1.0) * 1e4


def matmul_bf(einsum_form, left_arr, right_arr):
    return jnp.einsum(einsum_form, left_arr, right_arr, preferred_element_type=F32).astype(BF16)


def gated_out(einsum_form, gate_proj, attended, out_w):
    gated_vals = (jax.nn.sigmoid(gate_proj.astype(F32)) * attended).astype(BF16)
    return jnp.einsum(einsum_form, gated_vals, out_w, preferred_element_type=F32)


def row_attention(msa, bias_full, seq_mask, qkvg_w, out_w):
    projected = matmul_bf('sic,cahd->asihd', layer_norm(msa), qkvg_w)
    logits = jnp.einsum('sihd,sjhd->shij', projected[0], projected[1], preferred_element_type=F32) * (qkvg_w.shape[-1] ** -0.5) + bias_full[None] + mask_bias(seq_mask)[:, None, None, :]
    attn_probs = jax.nn.softmax(logits, axis=-1).astype(BF16)
    attended = jnp.einsum('shij,sjhd->sihd', attn_probs, projected[2], preferred_element_type=F32)
    return (msa + gated_out('sihd,hdc->sic', projected[3], attended, out_w)).astype(BF16)


def triangle_rows(pair_act, pair_ln, bias_full, res_mask, qkvg_w, out_w):
    projected = matmul_bf('ijc,cahd->aijhd', pair_ln, qkvg_w)
    logits = jnp.einsum('ijhd,ikhd->ihjk', projected[0], projected[1], preferred_element_type=F32) * (qkvg_w.shape[-1] ** -0.5) + bias_full[None] + mask_bias(res_mask)[None, None, None, :]
    attn_probs = jax.nn.softmax(logits, axis=-1).astype(BF16)
    attended = jnp.einsum('ihjk,ikhd->ijhd', attn_probs, projected[2], preferred_element_type=F32)
    return (pair_act + gated_out('ijhd,hdc->ijc', projected[3], attended, out_w)).astype(BF16)


def remote(src, dst, send_sem, recv_sem, dev):
    return pltpu.make_async_remote_copy(src_ref=src, dst_ref=dst, send_sem=send_sem, recv_sem=recv_sem,
                                        device_id={'dap': dev}, device_id_type=MESH)


def greet_all(me, n):
    barrier = pltpu.get_barrier_semaphore()
    for k in range(1, n):
        pl.semaphore_signal(barrier, inc=1, device_id={'dap': lax.rem(me + k, n)}, device_id_type=MESH)
    pl.semaphore_wait(barrier, n - 1)


def vmem():
    return pl.BlockSpec(memory_space=pltpu.VMEM)


def params(cid, limit=None):
    return pltpu.CompilerParams(collective_id=cid, has_side_effects=True, vmem_limit_bytes=limit)


def position(me, side):
    return me // (2 * side), (me // 2) % side, me % 2


def rows_to_block(me, side, rows_ref, block_ref, send_sem, recv_sem):
    y, x, c = position(me, side)
    half = side // 2
    slot = (x % half) * 2 + c
    core = x // half
    for t in range(side):
        dst = y * 2 * side + t * 2 + core

        @pl.when(dst != me)
        def _():
            remote(rows_ref.at[:, t], block_ref.at[slot], send_sem.at[t], recv_sem.at[slot], dst).start()

        @pl.when(dst == me)
        def _():
            block_ref[slot] = rows_ref[:, t]


def rows_to_block_wait(me, side, rows_ref, block_ref, send_sem, recv_sem):
    y, x, c = position(me, side)
    half = side // 2
    core = x // half
    for t in range(side):
        dst = y * 2 * side + t * 2 + core
        src = y * 2 * side + (c * half + t // 2) * 2 + t % 2

        @pl.when(dst != me)
        def _():
            remote(rows_ref.at[:, t], block_ref.at[t], send_sem.at[t], recv_sem.at[t], dst).wait_send()

        @pl.when(src != me)
        def _():
            remote(rows_ref.at[:, 0], block_ref.at[t], send_sem.at[t], recv_sem.at[t], dst).wait_recv()


def entry_kernel(n, side, bias_ref, rows_ref, bias_out, block_out, send_sem, recv_sem, bsend, brecv):
    me = lax.axis_index('dap')
    greet_all(me, n)
    copies = []
    for k in range(1, n):
        cp = remote(bias_ref, bias_out.at[me], send_sem.at[k], recv_sem.at[k], lax.rem(me + k, n))
        cp.start()
        copies.append(cp)
    rows_to_block(me, side, rows_ref, block_out, bsend, brecv)
    bias_out[me] = bias_ref[...]
    rows_to_block_wait(me, side, rows_ref, block_out, bsend, brecv)
    for cp in copies:
        cp.wait()


def entry_exchange(n, side, bias, rows):
    r, sides, w, ch = rows.shape
    return pl.pallas_call(
        functools.partial(entry_kernel, n, side),
        out_shape=[jax.ShapeDtypeStruct((n,) + bias.shape, bias.dtype),
                   jax.ShapeDtypeStruct((side, r, w, ch), rows.dtype)],
        in_specs=[vmem(), vmem()], out_specs=[vmem(), vmem()],
        scratch_shapes=[pltpu.SemaphoreType.DMA((n,)), pltpu.SemaphoreType.DMA((n,)),
                        pltpu.SemaphoreType.DMA((side,)), pltpu.SemaphoreType.DMA((side,))],
        compiler_params=params(0), name='entry_exchange')(bias, rows)


def reduce_kernel(n, combine, part_ref, out_ref, got, mine, send_sem, recv_sem, send2, recv2):
    me = lax.axis_index('dap')
    greet_all(me, n)
    copies = []
    for k in range(1, n):
        dst = lax.rem(me + k, n)
        cp = remote(part_ref.at[dst], got.at[me], send_sem.at[k], recv_sem.at[k], dst)
        cp.start()
        copies.append(cp)
    got[me] = part_ref[me]
    for cp in copies:
        cp.wait()
    total = combine(got[...])
    mine[...] = total
    out_ref[me] = total
    copies = []
    for k in range(1, n):
        cp = remote(mine, out_ref.at[me], send2.at[k], recv2.at[k], lax.rem(me + k, n))
        cp.start()
        copies.append(cp)
    for cp in copies:
        cp.wait()


def all_reduce(n, cid, combine, part, out_block):
    return pl.pallas_call(
        functools.partial(reduce_kernel, n, combine),
        out_shape=jax.ShapeDtypeStruct((n,) + out_block, F32),
        in_specs=[vmem()], out_specs=vmem(),
        scratch_shapes=[pltpu.VMEM(part.shape, F32), pltpu.VMEM(out_block, F32)]
        + [pltpu.SemaphoreType.DMA((n,))] * 4,
        compiler_params=params(cid), name=f'all_reduce{cid}')(part)


def combine_sum(got):
    return jnp.sum(got, axis=0)


def combine_softmax(got):
    acc, top, den = got[:, 0], got[:, 1], got[:, 2]
    scale = jnp.exp(top - jnp.max(top, axis=0, keepdims=True))
    return jnp.sum(acc * scale, axis=0) / jnp.sum(den * scale, axis=0)


def opm_kernel(side, a_ref, c_ref, o_ref, a_buf, c_buf, acc, got, s1, r1, s2, r2, s3, r3):
    me = lax.axis_index('dap')
    y, x, c = position(me, side)
    seq = a_ref.shape[-1]
    half = side // 2
    blk = a_ref.shape[1]

    def dev(yy, xx, cc):
        return (yy * side + xx) * 2 + cc

    barrier = pltpu.get_barrier_semaphore()
    peers = [dev(y, x, 1 - c)]
    for k in range(1, side):
        peers.append(dev(lax.rem(y + k, side), x, c))
        peers.append(dev(y, lax.rem(x + k, side), c))
    for p in peers:
        pl.semaphore_signal(barrier, inc=1, device_id={'dap': p}, device_id_type=MESH)
    pl.semaphore_wait(barrier, len(peers))

    def slot(buf, yy, xx):
        return buf.at[yy, xx // 2, :, pl.ds(pl.multiple_of((xx % 2) * seq, seq), seq)]

    first = []
    for k in range(1, side):
        ty = lax.rem(y + k, side)
        cp = remote(a_ref.at[ty], slot(a_buf, y, x), s1.at[0, k], r1.at[0, k], dev(ty, x, c))
        cp.start()
        tx = lax.rem(x + k, side)
        cq = remote(c_ref.at[tx], slot(c_buf, y, x), s1.at[1, k], r1.at[1, k], dev(y, tx, c))
        cq.start()
        first.append((cp, cq))
    second = []
    for k in range(1, side):
        cp = remote(a_ref.at[y], slot(a_buf, y, x), s2.at[0, 0, k], r2.at[0, 0, k], dev(y, lax.rem(x + k, side), c))
        cp.start()
        cq = remote(c_ref.at[x], slot(c_buf, y, x), s2.at[1, 0, k], r2.at[1, 0, k], dev(lax.rem(y + k, side), x, c))
        cq.start()
        second += [cp, cq]
    lanes = pl.ds(pl.multiple_of((x % 2) * seq, seq), seq)
    a_buf[y, x // 2, :, lanes] = a_ref[y]
    c_buf[y, x // 2, :, lanes] = c_ref[x]
    order = [1, side - 1] + list(range(2, side - 1))
    for k in order:
        cp, cq = first[k - 1]
        cp.wait_recv()
        sy = lax.rem(y - k + side, side)
        for q in range(1, side):
            f = remote(slot(a_buf, sy, x), slot(a_buf, sy, x), s2.at[0, k, q], r2.at[0, k, q], dev(y, lax.rem(x + q, side), c))
            f.start()
            second.append(f)
        cq.wait_recv()
        sx = lax.rem(x - k + side, side)
        for q in range(1, side):
            f = remote(slot(c_buf, y, sx), slot(c_buf, y, sx), s2.at[1, k, q], r2.at[1, k, q], dev(lax.rem(y + q, side), x, c))
            f.start()
            second.append(f)
    for cp, cq in first:
        cp.wait_send()
        cq.wait_send()
    for f in second:
        f.wait()
    rows = blk // 2

    def product(base, dst):
        def tile(t, _):
            r0 = pl.multiple_of(base + t * 128, 128)
            total = jnp.zeros((128, blk), F32)
            for yy in range(side):
                for xx in range(half):
                    total += lax.dot_general(a_buf[yy, xx, pl.ds(r0, 128), :], c_buf[yy, xx], (((1,), (1,)), ((), ())),
                                             preferred_element_type=F32)
            dst[pl.ds(pl.multiple_of(t * 128, 128), 128), :] = total
            return 0
        lax.fori_loop(0, rows // 128, tile, 0)

    product((1 - c) * rows, acc.at[0])
    swap = remote(acc.at[0], got, s3, r3, dev(y, x, 1 - c))
    swap.start()
    product(c * rows, acc.at[1])
    swap.wait()
    o_ref[...] = (acc[1] + got[...]).astype(BF16)


def opm_exchange(side, a, c):
    blk, seq = a.shape[1:]
    buf = pltpu.VMEM((side, side // 2, blk, 2 * seq), BF16)
    dma = pltpu.SemaphoreType.DMA
    return pl.pallas_call(
        functools.partial(opm_kernel, side),
        out_shape=jax.ShapeDtypeStruct((blk // 2, blk), BF16),
        in_specs=[vmem(), vmem()], out_specs=vmem(),
        scratch_shapes=[buf, buf, pltpu.VMEM((2, blk // 2, blk), F32), pltpu.VMEM((blk // 2, blk), F32),
                        dma((2, side)), dma((2, side)), dma((2, side, side)), dma((2, side, side)), dma, dma],
        compiler_params=params(3, 60 * 1024 * 1024), name='opm_exchange')(a, c)


def block_to_rows_kernel(side, block_ref, rows_out, send_sem, recv_sem):
    me = lax.axis_index('dap')
    y, x, c = position(me, side)
    half = side // 2
    core = x // half
    my_slot = (x % half) * 2 + c
    barrier = pltpu.get_barrier_semaphore()
    for t in range(2 * side):
        peer = y * 2 * side + t

        @pl.when(peer != me)
        def _():
            pl.semaphore_signal(barrier, inc=1, device_id={'dap': peer}, device_id_type=MESH)
    pl.semaphore_wait(barrier, 2 * side - 1)
    for t in range(side):
        dst = y * 2 * side + (c * half + t // 2) * 2 + t % 2

        @pl.when(dst != me)
        def _():
            remote(block_ref.at[t], rows_out.at[x], send_sem.at[t], recv_sem.at[x], dst).start()

        @pl.when(dst == me)
        def _():
            rows_out[x] = block_ref[t]
    for t in range(side):
        dst = y * 2 * side + (c * half + t // 2) * 2 + t % 2
        src = y * 2 * side + t * 2 + core

        @pl.when(dst != me)
        def _():
            remote(block_ref.at[t], rows_out.at[x], send_sem.at[t], recv_sem.at[x], dst).wait_send()

        @pl.when(src != me)
        def _():
            remote(block_ref.at[t], rows_out.at[t], send_sem.at[t], recv_sem.at[t], dst).wait_recv()


def block_to_rows(side, block):
    slots, r, w, ch = block.shape
    return pl.pallas_call(
        functools.partial(block_to_rows_kernel, side),
        out_shape=jax.ShapeDtypeStruct((side, r, w, ch), block.dtype),
        in_specs=[vmem()], out_specs=vmem(),
        scratch_shapes=[pltpu.SemaphoreType.DMA((side,)), pltpu.SemaphoreType.DMA((side,))],
        compiler_params=params(4), name='block_to_rows')(block)


def exchange_kernel(n, n_gather, n_swap, *refs):
    k_in = n_gather + n_swap
    ins, outs, (send_sem, recv_sem) = refs[:k_in], refs[k_in:2 * k_in], refs[2 * k_in:]
    me = lax.axis_index('dap')
    greet_all(me, n)
    copies = []
    for k in range(1, n):
        dst = lax.rem(me + k, n)
        for a in range(k_in):
            src = ins[a] if a < n_gather else ins[a].at[dst]
            cp = remote(src, outs[a].at[me], send_sem.at[a, k], recv_sem.at[a, k], dst)
            cp.start()
            copies.append(cp)
    for a in range(k_in):
        outs[a][me] = ins[a][...] if a < n_gather else ins[a][me]
    for cp in copies:
        cp.wait()


def exchange(n, cid, gathers, swaps):
    ops = list(gathers) + list(swaps)
    shapes = [jax.ShapeDtypeStruct((n,) + g.shape, g.dtype) for g in gathers] + [jax.ShapeDtypeStruct(s.shape, s.dtype) for s in swaps]
    return pl.pallas_call(
        functools.partial(exchange_kernel, n, len(gathers), len(swaps)),
        out_shape=shapes, in_specs=[vmem()] * len(ops), out_specs=[vmem()] * len(ops),
        scratch_shapes=[pltpu.SemaphoreType.DMA((len(ops), n))] * 2,
        compiler_params=params(cid), name=f'exchange{cid}')(*ops)


def solution(mesh):
    n = mesh.shape['dap']
    side = math.isqrt(n // 2)
    assert 2 * side * side == n

    def block(msa, pair, mask_full, res_mask, row_bias_w, row_qkvg_w, row_out_w, col_query_w, col_kv_w, col_gate_w, col_out_w, opm_proj_w, opm_out_w, start_bias_w, start_qkvg_w, start_out_w, end_bias_w, end_qkvg_w, end_out_w):
        seq, res, ch = msa.shape
        r = pair.shape[0]
        pc = pair.shape[-1]
        w = res // side
        heads, hd = col_gate_w.shape[1:]
        dev_index = lax.axis_index('dap')
        y, x, core = position(dev_index, side)
        seq_mask = lax.dynamic_slice_in_dim(mask_full, dev_index * seq, seq, axis=0)

        row_bias = matmul_bf('ijc,ch->hij', layer_norm(pair), row_bias_w)
        bias_all, pair_blk = entry_exchange(n, side, row_bias, pair.reshape(r, side, w, pc))
        bias_full = bias_all.transpose(1, 0, 2, 3).reshape(row_bias.shape[0], res, res)
        msa = row_attention(msa, bias_full, seq_mask, row_qkvg_w, row_out_w)

        msa_ln = layer_norm(msa)
        part = jnp.einsum('sr,src->rc', seq_mask.astype(BF16), msa_ln, preferred_element_type=F32)
        qsum = all_reduce(n, 1, combine_sum, part.reshape(n, r, ch), (r, ch)).reshape(res, ch)
        mask_count = jnp.sum(mask_full, axis=0).astype(F32) + 1e-10
        query = matmul_bf('rc,chd->rhd', (qsum / mask_count[:, None]).astype(BF16), col_query_w)
        key_val = matmul_bf('src,cad->asrd', msa_ln, col_kv_w)
        gate = matmul_bf('src,chd->srhd', msa_ln, col_gate_w)
        logits = jnp.einsum('rhd,srd->rhs', query, key_val[0], preferred_element_type=F32) * (hd ** -0.5) + mask_bias(seq_mask).T[:, None, :]
        top = jnp.max(logits, axis=-1, keepdims=True)
        weights = jnp.exp(logits - top)
        den = jnp.sum(weights, axis=-1, keepdims=True)
        acc = jnp.einsum('rhs,srd->rhd', weights.astype(BF16), key_val[1], preferred_element_type=F32)
        part = jnp.stack([acc, jnp.broadcast_to(top, acc.shape), jnp.broadcast_to(den, acc.shape)], axis=0)
        part = part.reshape(3, n, r, heads * hd).transpose(1, 0, 2, 3)
        attended = all_reduce(n, 2, combine_softmax, part, (r, heads * hd)).reshape(res, heads, hd)
        msa = (msa + gated_out('srhd,hdc->src', gate, attended[None], col_out_w)).astype(BF16)

        msa_ln = layer_norm(msa)
        proj = matmul_bf('src,cae->ares', msa_ln, opm_proj_w) * seq_mask.astype(BF16).T[None, :, None, :]
        e = opm_proj_w.shape[-1]
        outer = opm_exchange(side, proj[0].reshape(side, w * e, seq), proj[1].reshape(side, w * e, seq))
        rows0 = y * w + core * (w // 2)
        mask_bf = mask_full.astype(BF16)
        mask_i = lax.dynamic_slice_in_dim(mask_bf, rows0, w // 2, axis=1)
        mask_j = lax.dynamic_slice_in_dim(mask_bf, x * w, w, axis=1)
        counts = jnp.einsum('si,sj->ij', mask_i, mask_j, preferred_element_type=F32)
        update = jnp.einsum('iejf,efc->ijc', outer.reshape(w // 2, e, w, e), opm_out_w, preferred_element_type=F32) / (1e-3 + counts)[:, :, None]
        pair_blk = (pair_blk.reshape(w // 2, w, pc) + update).astype(BF16)
        rows = block_to_rows(side, pair_blk.reshape(side, r, w, pc))
        pair = rows.transpose(1, 0, 2, 3).reshape(r, res, pc)

        pair_ln = layer_norm(pair)
        start_all, = exchange(n, 5, [matmul_bf('ijc,ch->hij', pair_ln, start_bias_w)], [])
        start_full = start_all.transpose(1, 0, 2, 3).reshape(-1, res, res)
        pair = triangle_rows(pair, pair_ln, start_full, res_mask, start_qkvg_w, start_out_w)

        end_bias = matmul_bf('ijc,ch->hij', layer_norm(pair), end_bias_w)
        end_all, cols = exchange(n, 6, [end_bias], [pair.reshape(r, n, r, pc).transpose(1, 2, 0, 3)])
        end_full = end_all.transpose(1, 3, 0, 2).reshape(-1, res, res)
        cols = cols.transpose(1, 0, 2, 3).reshape(r, res, pc)
        cols = triangle_rows(cols, layer_norm(cols), end_full, res_mask, end_qkvg_w, end_out_w)
        back, = exchange(n, 7, [], [cols.reshape(r, n, r, pc).transpose(1, 2, 0, 3)])
        pair_out = back.transpose(1, 0, 2, 3).reshape(r, res, pc)
        return msa, pair_out

    row_spec = P(('data', 'dap'), None, None)
    in_specs = (row_spec, row_spec, P('data', None), P('data')) + (P(),) * 15
    return jax.shard_map(block, mesh=mesh, in_specs=in_specs, out_specs=(row_spec, row_spec), check_vma=False)
```

time: 460 us -> 327 us (0.71)
  Pallas kernels: 0 us -> 165 us
  waiting for transfers between devices: 130 us -> 0 us
  blocking collectives: 107 us -> 0 us
  starting transfers between devices: 36.6 us -> 0 us
  other arithmetic: 12.5 us -> 30.9 us
  matrix products: 105 us -> 86.7 us
  between operations: 15 us -> 1.66 us
  local copies, waits for them, and re-layouts: 47.9 us -> 36.9 us
    pallas_call x0 -> x8, Pallas kernels: none -> 165 us  [the longest x1 74.9 us: opm_exchange(): pl.pallas_call(functools.partial(opm_kernel, side), out_shape=jax.ShapeDt...]
    all_gather x1 -> x0, waiting for transfers between devices: 108 us -> none  [evoformer_block(): right_full = lax.all_gather(projected[1], 'dap', axis=1, tiled=True)]
    all_gather x3 -> x0, blocking collectives: 107 us -> none  [the longest x1 46.7 us: evoformer_block(): lax.all_gather(matmul_bf('ijc,ch->hji', cols_ln, end_bias_w), 'dap', axis...]
    all_to_all x4 -> x0, starting transfers between devices: 36.3 us -> none  [the longest x1 10.6 us: evoformer_block(): pair_out = lax.all_to_all(pair_cols, 'dap', 0, 1, tiled=True)]
    all_to_all x4 -> x0, waiting for transfers between devices: 21.6 us -> none  [the longest x1 21.6 us: evoformer_block(): value_a8 = lax.all_to_all(value_a7, 'dap', 1, 0, tiled=True)]
    unnamed x45 -> x35, local copies, waits for them, and re-layouts: 20.7 us -> 0.71 us
    convert_element_type x6 -> x3, local copies, waits for them, and re-layouts: 17.3 us -> 0.95 us  [the longest x1 0.89 us: matmul_bf(): jnp.einsum(einsum_form, left_arr, right_arr, preferred_element_type=F32)]
    dot_general x18 -> x16, matrix products: 67.8 us -> 52 us  [the longest x4 32.1 us: gated_out(): jnp.einsum(einsum_form, gated_vals, out_w, preferred_element_type=F32)]
  transfers between devices with their start and end apart: 5 -> 0, of which waited for: 2 -> 0; matrix products, arithmetic and copies ran while one was open for 9% -> 0% of each run, Pallas kernels for 0% -> 0%
where the time goes in v1:
time: 327 us; the launch traced here: 321 us
  Pallas kernels  165 us (50%)
  matrix products  86.7 us (27%)
  local copies, waits for them, and re-layouts  36.9 us (11%)
  other arithmetic  30.9 us (9%)
    pallas_call x1, Pallas kernels, opm_exchange(): pl.pallas_call(functools.partial(opm_kernel, side), out_shape=jax.ShapeDt...  74.9 us
    sub x1, matrix products, row_attention(): attn_probs = jax.nn.softmax(logits, axis=-1).astype(BF16)  32.7 us
    pallas_call x2, Pallas kernels, all_reduce(): pl.pallas_call(functools.partial(reduce_kernel, n, combine), out_shape=ja...  32.2 us
    dot_general x4, matrix products, gated_out(): jnp.einsum(einsum_form, gated_vals, out_w, preferred_element_type=F32)  32.1 us
    pallas_call x3, Pallas kernels, exchange(): pl.pallas_call(functools.partial(exchange_kernel, n, len(gathers), len(sw...  31.9 us
    pallas_call x1, Pallas kernels, entry_exchange(): pl.pallas_call(functools.partial(entry_kernel, n, side), out_shape=[jax.S...  16.8 us
    dot_general x8, matrix products, matmul_bf(): jnp.einsum(einsum_form, left_arr, right_arr, preferred_element_type=F32)  10.8 us
    reduce_sum x7, other arithmetic, layer_norm(): variance = jnp.mean(centered * centered, axis=-1, keepdims=True)  10.7 us

profile of v1, /device:TPU:97, one launch (start us, length us, event | category | flops | bytes accessed | tf_op | source)
XLA Modules:
  0.0 320.8 jit_solution(9061846660841742968)
XLA Ops:
  1.7 2.2 convert_reduce_fusion.1
  3.9 2.5 fusion.18
  6.5 5.5 %convert_bitcast_fusion = bf16[4,128,128,8,8]{2,4,3,0,1:T(8,128)(2,1)} fusion(bf16[128,128,64]{1,2,0:T(8,128)(2,1)S(1)} %copy-done.1, f32[128,128]{1,0:T(8,128)S(1)} %add_rsqrt_fusion.2, f32[128,128]{1,0:T(8,128)S(1)} %broadcast_multiply_fusion.2, bf16[64,4,8,8]{0,3,2,1:T(8,128)(2,1)S(1)} %copy-done.7), kind=kOutput, calls=%fused_computation.11 | convolution fusion | flops 545259520 | bytes 10649600 | tf_op jit(solution)/shard_map/sic,cahd->asihd/dot_general | solution.py:29
  13.4 16.8 %entry_exchange.1 = (bf16[32,8,4,128]{3,2,1,0:T(4,128)(2,1)}, bf16[4,4,32,128]{3,2,1,0:T(8,128)(2,1)}) custom-call(bf16[8,4,128]{2,1,0:T(4,128)(2,1)} %bitcast.348, bf16[4,4,32,128]{3,2,1,0:T(8,128)(2,1)} %bitcast.332), custom_call_target="tpu_custom_call" | custom-call | tf_op jit(solution)/shard_map/entry_exchange/pallas_call | solution.py:128
  31.5 32.7 %fusion.171 = (f32[128,8,128]{2,1,0:T(8,128)}, f32[128,8,128,128]{2,3,1,0:T(8,128)}) fusion(f32[128,128]{1,0:T(8,128)S(1)} %add_multiply_fusion, f32[8,128,128]{1,2,0:T(8,128)S(1)} %copy.97, bf16[4,128,128,8,8]{2,4,3,0,1:T(8,128)(2,1)} %convert_bitcast_fusion), kind=kOutput, calls=%fused_computation.225 | convolution fusion | flops 352321664 | bytes 72417280 | tf_op jit(solution)/shard_map/sub | solution.py:40
  64.2 26.3 %convert_reduce_fusion = (f32[128,128]{1,0:T(8,128)S(1)}, bf16[128,128,64]{1,2,0:T(8,128)(2,1)}) fusion(bf16[8,8,64]{2,1,0:T(8,128)(2,1)S(1)} %copy-done.12, f32[128,8,128,128]{2,3,1,0:T(8,128)} %get-tuple-element.19, f32[128,8,128]{2,1,0:T(8,128)} %get-tuple-element.18, bf16[4,128,128,8,8]{2,4,3,0,1:T(8,128)(2,1)} %convert_bitcast_fusion, ...), kind=kOutput, calls=%fused_computation.15 | convolution fusion | flops 447725568 | bytes 76095488 | tf_op jit(solution)/shard_map/sihd,hdc->sic/dot_general | solution.py:34
  90.5 2.7 fusion.16
  94.7 2.4 multiply_reduce_fusion
  97.8 16.0 %all_reduce1.1 = f32[32,4,64]{2,1,0:T(4,128)} custom-call(f32[32,4,64]{2,1,0:T(4,128)} %bitcast.344), custom_call_target="tpu_custom_call" | custom-call | tf_op jit(solution)/shard_map/all_reduce1/pallas_call | solution.py:163
  115.3 2.8 fusion.169
  122.0 1.9 copy.102
  125.5 2.1 fusion.172
  127.6 1.9 copy.104
  129.5 2.2 fusion.98
  131.8 1.9 stack.6
  136.1 1.9 stack_broadcast_in_dim.17
  141.8 16.2 %all_reduce2.1 = f32[32,4,64]{2,1,0:T(4,128)} custom-call(f32[32,3,4,64]{3,2,1,0:T(4,128)} %maximum_bitcast_fusion.part_ref), custom_call_target="tpu_custom_call" | custom-call | tf_op jit(solution)/shard_map/all_reduce2/pallas_call | solution.py:163
  158.0 1.8 mul.160
  159.8 1.8 copy.108
  161.6 4.8 %convert_reduce_fusion.2 = (f32[128,128]{1,0:T(8,128)S(1)}, bf16[128,128,64]{1,2,0:T(8,128)(2,1)}) fusion(bf16[8,8,64]{2,1,0:T(8,128)(2,1)S(1)} %copy-done.13, f32[128,8,8]{0,1,2:T(8,128)} %copy.108, bf16[128,128,64]{1,2,0:T(8,128)(2,1)S(1)} %copy-done.2, f32[128,128]{1,0:T(8,128)} %copy-done.4, f32[128,128]{1,0:T(8,128)S(1)} %broadcast_multiply_fusion.1, ...), kind=kOutput, calls=%fused_computation.20 | convolution fusion | flops 285196288 | bytes 4440064 | tf_op jit(solution)/shard_map/srhd,hdc->src/dot_general | solution.py:34
  166.4 2.6 fusion.20
  169.1 2.4 bitcast_multiply_fusion.1
  171.9 2.3 copy.110
  174.2 2.3 copy.111
  176.4 74.9 %opm_exchange.1 = bf16[512,1024]{1,0:T(8,128)(2,1)} custom-call(bf16[4,1024,128]{2,1,0:T(8,128)(2,1)} %bitcast.329, bf16[4,1024,128]{2,1,0:T(8,128)(2,1)} %bitcast.330), custom_call_target="tpu_custom_call" | custom-call | tf_op jit(solution)/shard_map/opm_exchange/pallas_call | solution.py:269
  251.3 6.3 %reshape.228 = bf16[16,32,32,32]{3,2,1,0:T(8,128)(2,1)} reshape(bf16[512,1024]{1,0:T(8,128)(2,1)} %opm_exchange.1) | data formatting | bytes 2097152 | tf_op jit(solution)/shard_map/reshape | solution.py:400
  258.7 3.8 %fusion.77 = bf16[16,32,128]{2,1,0:T(8,128)(2,1)} fusion(bf16[16,32,32,32]{3,2,1,0:T(8,128)(2,1)} %reshape.228, bf16[16,32,128]{2,1,0:T(8,128)(2,1)S(1)} %bitcast.351, bf16[32,32,128]{2,1,0:T(8,128)(2,1)S(1)} %copy-done, f32[16,32]{1,0:T(8,128)S(1)} %convolution_add_fusion), kind=kOutput, calls=%fused_computation.93 | convolution fusion | flops 134479872 | bytes 1574912 | tf_op jit(solution)/shard_map/iejf,efc->ijc/dot_general | solution.py:400
  262.5 8.8 %block_to_rows.1 = bf16[4,4,32,128]{3,2,1,0:T(8,128)(2,1)} custom-call(bf16[4,4,32,128]{3,2,1,0:T(8,128)(2,1)} %bitcast.347), custom_call_target="tpu_custom_call" | custom-call | tf_op jit(solution)/shard_map/block_to_rows/pallas_call | solution.py:317
  275.7 9.9 %exchange5.1 = bf16[32,4,4,128]{3,2,1,0:T(4,128)(2,1)} custom-call(bf16[4,4,128]{2,1,0:T(4,128)(2,1)} %bitcast.350), custom_call_target="tpu_custom_call" | custom-call | tf_op jit(solution)/shard_map/exchange5/pallas_call | solution.py:347
  290.1 11.6 %exchange6.1 = (bf16[32,4,4,128]{3,2,1,0:T(4,128)(2,1)}, bf16[32,4,4,128]{3,2,1,0:T(4,128)(2,1)}) custom-call(bf16[4,4,128]{2,1,0:T(4,128)(2,1)} %bitcast.349, bf16[32,4,4,128]{3,2,1,0:T(4,128)(2,1)} %bitcast.337), custom_call_target="tpu_custom_call" | custom-call | tf_op jit(solution)/shard_map/exchange6/pallas_call | solution.py:347
  308.3 10.4 %exchange7.1 = bf16[32,4,4,128]{3,2,1,0:T(4,128)(2,1)} custom-call(bf16[32,4,4,128]{3,2,1,0:T(4,128)(2,1)} %bitcast.338), custom_call_target="tpu_custom_call" | custom-call | tf_op jit(solution)/shard_map/exchange7/pallas_call | solution.py:347
  318.7 1.6 copy.130
  (111 shorter events, 35.9 us)
Async XLA Ops:
  0.6 258.0 %copy-start = (bf16[32,32,128]{2,1,0:T(8,128)(2,1)S(1)}, bf16[32,32,128]{2,1,0:T(8,128)(2,1)}, u32[]{:S(2)}) copy-start(bf16[32,32,128]{2,1,0:T(8,128)(2,1)} %param.31) | copy-start | bytes 786436
  0.6 5.8 %copy-start.1 = (bf16[128,128,64]{1,2,0:T(8,128)(2,1)S(1)}, bf16[128,128,64]{1,2,0:T(8,128)(2,1)}, u32[]{:S(2)}) copy-start(bf16[128,128,64]{1,2,0:T(8,128)(2,1)} %param.19) | copy-start | bytes 6291460
  0.7 5.8 %copy-start.7 = (bf16[64,4,8,8]{0,3,2,1:T(8,128)(2,1)S(1)}, bf16[64,4,8,8]{0,3,2,1:T(8,128)(2,1)}, u32[]{:S(2)}) copy-start(bf16[64,4,8,8]{0,3,2,1:T(8,128)(2,1)} %param.24) | copy-start | bytes 98308
  6.5 5.6 %copy-start.3 = (bf16[4,128,128]{2,1,0:T(8,128)(2,1)S(1)}, bf16[4,128,128]{2,1,0:T(8,128)(2,1)}, u32[]{:S(2)}) copy-start(bf16[4,128,128]{2,1,0:T(8,128)(2,1)} %param.20) | copy-start | bytes 393220
  6.5 5.9 %copy-start.14 = (bf16[128,8]{0,1:T(8,128)(2,1)S(1)}, bf16[128,8]{0,1:T(8,128)(2,1)}, u32[]{:S(2)}) copy-start(bf16[128,8]{0,1:T(8,128)(2,1)} %param.23) | copy-start | bytes 6148
  31.5 32.7 %copy-start.12 = (bf16[8,8,64]{2,1,0:T(8,128)(2,1)S(1)}, bf16[8,8,64]{2,1,0:T(8,128)(2,1)}, u32[]{:S(2)}) copy-start(bf16[8,8,64]{2,1,0:T(8,128)(2,1)} %param.25) | copy-start | bytes 24580
  90.5 29.4 %copy-start.2 = (bf16[128,128,64]{1,2,0:T(8,128)(2,1)S(1)}, bf16[128,128,64]{1,2,0:T(8,128)(2,1)}, u32[]{:S(2)}) copy-start(bf16[128,128,64]{1,2,0:T(8,128)(2,1)} %get-tuple-element.21) | copy-start | bytes 6291460
  93.2 28.0 %copy-start.4 = (f32[128,128]{1,0:T(8,128)}, f32[128,128]{1,0:T(8,128)S(1)}, u32[]{:S(2)}) copy-start(f32[128,128]{1,0:T(8,128)S(1)} %add_rsqrt_fusion.1) | copy-start | bytes 196612
  125.5 36.1 %copy-start.13 = (bf16[8,8,64]{2,1,0:T(8,128)(2,1)S(1)}, bf16[8,8,64]{2,1,0:T(8,128)(2,1)}, u32[]{:S(2)}) copy-start(bf16[8,8,64]{2,1,0:T(8,128)(2,1)} %param.29) | copy-start | bytes 24580
  251.3 7.3 %copy-start.9 = (bf16[4,4,32,128]{3,2,1,0:T(8,128)(2,1)S(1)}, bf16[4,4,32,128]{3,2,1,0:T(8,128)(2,1)}, u32[]{:S(2)}) copy-start(bf16[4,4,32,128]{3,2,1,0:T(8,128)(2,1)} %get-tuple-element.7) | copy-start | bytes 393220
  258.6 16.3 %copy-start.8 = (bf16[128,4]{0,1:T(4,128)(2,1)S(1)}, bf16[128,4]{0,1:T(4,128)(2,1)}, u32[]{:S(2)}) copy-start(bf16[128,4]{0,1:T(4,128)(2,1)} %param.32) | copy-start | bytes 3076
  258.6 28.0 %copy-start.6 = (bf16[128,4,4,32]{0,3,2,1:T(8,128)(2,1)S(1)}, bf16[128,4,4,32]{0,3,2,1:T(8,128)(2,1)}, u32[]{:S(2)}) copy-start(bf16[128,4,4,32]{0,3,2,1:T(8,128)(2,1)} %param.33) | copy-start | bytes 393220
  258.6 28.3 %copy-start.16 = (s32[128]{0:T(128)S(1)}, s32[128]{0:T(128)}, u32[]{:S(2)}) copy-start(s32[128]{0:T(128)} %param.22) | copy-start | bytes 1540
  262.5 25.1 %copy-start.10 = (bf16[4,32,128]{2,1,0:T(8,128)(2,1)S(1)}, bf16[4,32,128]{2,1,0:T(8,128)(2,1)}, u32[]{:S(2)}) copy-start(bf16[4,32,128]{2,1,0:T(8,128)(2,1)} %param.34) | copy-start | bytes 98308
  286.7 2.5 copy-start.15
  287.6 18.4 %copy-start.5 = (bf16[128,4,4,32]{0,3,2,1:T(8,128)(2,1)S(1)}, bf16[128,4,4,32]{0,3,2,1:T(8,128)(2,1)}, u32[]{:S(2)}) copy-start(bf16[128,4,4,32]{0,3,2,1:T(8,128)(2,1)} %param.36) | copy-start | bytes 393220
  288.1 19.0 %copy-start.11 = (bf16[4,32,128]{2,1,0:T(8,128)(2,1)S(1)}, bf16[4,32,128]{2,1,0:T(8,128)(2,1)}, u32[]{:S(2)}) copy-start(bf16[4,32,128]{2,1,0:T(8,128)(2,1)} %param.37) | copy-start | bytes 98308

commit v2 on v1

--- a/solution.py
+++ b/solution.py
@@ -34,20 +34,203 @@
     return jnp.einsum(einsum_form, gated_vals, out_w, preferred_element_type=F32)
 
 
-def row_attention(msa, bias_full, seq_mask, qkvg_w, out_w):
-    projected = matmul_bf('sic,cahd->asihd', layer_norm(msa), qkvg_w)
-    logits = jnp.einsum('sihd,sjhd->shij', projected[0], projected[1], preferred_element_type=F32) * (qkvg_w.shape[-1] ** -0.5) + bias_full[None] + mask_bias(seq_mask)[:, None, None, :]
-    attn_probs = jax.nn.softmax(logits, axis=-1).astype(BF16)
-    attended = jnp.einsum('shij,sjhd->sihd', attn_probs, projected[2], preferred_element_type=F32)
-    return (msa + gated_out('sihd,hdc->sic', projected[3], attended, out_w)).astype(BF16)
-
-
 def triangle_rows(pair_act, pair_ln, bias_full, res_mask, qkvg_w, out_w):
     projected = matmul_bf('ijc,cahd->aijhd', pair_ln, qkvg_w)
     logits = jnp.einsum('ijhd,ikhd->ihjk', projected[0], projected[1], preferred_element_type=F32) * (qkvg_w.shape[-1] ** -0.5) + bias_full[None] + mask_bias(res_mask)[None, None, None, :]
     attn_probs = jax.nn.softmax(logits, axis=-1).astype(BF16)
     attended = jnp.einsum('ihjk,ikhd->ijhd', attn_probs, projected[2], preferred_element_type=F32)
     return (pair_act + gated_out('ijhd,hdc->ijc', projected[3], attended, out_w)).astype(BF16)
+
+
+LOG2E = 1.4426950408889634
+
+def norm_cols(x):
+    mean = jnp.mean(x, axis=0, keepdims=True)
+    cen = x - mean
+    var = jnp.mean(cen * cen, axis=0, keepdims=True)
+    return (cen * lax.rsqrt(var + 1e-5)).astype(BF16)
+
+
+def row_kernel(heads, hd, m_ref, bias_ref, maskc_ref, maskl_ref, pick_ref, wt_ref, wo_ref, m_out, ln_out, q_out,
+               x_buf, q_buf, v_buf, g_buf, k_buf, att_buf):
+    @pl.when(pl.program_id(0) == 0)
+    def _():
+        q_out[...] = jnp.zeros_like(q_out)
+    seqs, ch, res = m_ref.shape
+    width = heads * hd
+    scale = LOG2E * hd ** -0.5
+    for s in range(seqs):
+        x_buf[:, s * res:(s + 1) * res] = m_ref[s].astype(F32)
+    ln = norm_cols(x_buf[...])
+    proj = jnp.dot(wt_ref[...], ln, preferred_element_type=F32)
+    q_buf[...] = proj[:width].astype(BF16)
+    v_buf[...] = proj[2 * width:3 * width].astype(BF16)
+    g_buf[...] = proj[3 * width:].astype(BF16)
+    for s in range(seqs):
+        k_buf[s] = proj[width:2 * width, s * res:(s + 1) * res].T.astype(BF16)
+
+    units = [(s, p) for s in range(seqs) for p in range(heads // 2)]
+
+    def logits_of(u):
+        s, p = u
+        qt = q_buf[:, s * res:(s + 1) * res]
+        return jnp.dot(k_buf[s], jnp.concatenate([qt, qt], axis=1) * pick_ref[p], preferred_element_type=F32)
+
+    def weights_of(u, raw):
+        s, p = u
+        mcol = jnp.broadcast_to(maskc_ref[0, :, s:s + 1], (res, 2 * res))
+        t = raw * scale + bias_ref[p] + mcol
+        w = jnp.exp2(t - jnp.max(t, axis=0, keepdims=True))
+        return w.astype(BF16), 1.0 / jnp.sum(w, axis=0, keepdims=True)
+
+    def attend(u, w, den):
+        s, p = u
+        o = jnp.dot(v_buf[2 * p * hd:2 * (p + 1) * hd, s * res:(s + 1) * res], w, preferred_element_type=F32) * den
+        lo = 2 * p * hd
+        att_buf[lo:lo + hd, s * res:(s + 1) * res] = o[:hd, :res]
+        att_buf[lo + hd:lo + 2 * hd, s * res:(s + 1) * res] = o[hd:, res:]
+
+    raws = [logits_of(units[0]), logits_of(units[1])]
+    prev = None
+    for i, u in enumerate(units):
+        if i + 2 < len(units):
+            raws.append(logits_of(units[i + 2]))
+        cur = weights_of(u, raws.pop(0))
+        if prev is not None:
+            attend(*prev)
+        prev = (u,) + cur
+    attend(*prev)
+    y = (jax.nn.sigmoid(g_buf[...].astype(F32)) * att_buf[...]).astype(BF16)
+    new = (x_buf[...] + jnp.dot(wo_ref[...], y, preferred_element_type=F32)).astype(BF16)
+    m_out[0] = new
+    ln2 = norm_cols(new.astype(F32))
+    ln_out[0] = ln2
+    masked = ln2.astype(F32) * maskl_ref[0]
+    total = masked[:, :res]
+    for s in range(1, seqs):
+        total += masked[:, s * res:(s + 1) * res]
+    q_out[...] += total
+
+
+def row_attention(msa, bias_full, seq_mask, qkvg_w, out_w, block=8):
+    seq, res, ch = msa.shape
+    heads, hd = out_w.shape[:2]
+    pairs = heads // 2
+    steps = seq // block
+    bias = (bias_full.astype(F32) * LOG2E).transpose(0, 2, 1).reshape(pairs, 2, res, res).transpose(0, 2, 1, 3).reshape(pairs, res, 2 * res)
+    maskf = seq_mask.astype(F32)
+    maskc = ((maskf - 1.0) * (1e4 * LOG2E)).reshape(steps, block, res).transpose(0, 2, 1)
+    maskl = maskf.reshape(steps, 1, block * res)
+    row_head = jnp.arange(heads * hd) // hd
+    lane_head = jnp.arange(2 * res) // res
+    pick = (row_head[None, :, None] == (2 * jnp.arange(pairs)[:, None, None] + lane_head[None, None, :])).astype(BF16)
+    wt = qkvg_w.reshape(ch, -1).T
+    wo = out_w.reshape(heads * hd, ch).T
+    full = lambda a: pl.BlockSpec(a.shape, lambda g: (0,) * a.ndim)
+    wide = jax.ShapeDtypeStruct((steps, ch, block * res), BF16)
+    lanes = block * res
+    return pl.pallas_call(
+        functools.partial(row_kernel, heads, hd),
+        grid=(steps,),
+        out_shape=[wide, wide, jax.ShapeDtypeStruct((ch, res), F32)],
+        in_specs=[pl.BlockSpec((block, ch, res), lambda g: (g, 0, 0)), full(bias), pl.BlockSpec((1, res, block), lambda g: (g, 0, 0)),
+                  pl.BlockSpec((1, 1, lanes), lambda g: (g, 0, 0)), full(pick), full(wt), full(wo)],
+        out_specs=[pl.BlockSpec((1, ch, lanes), lambda g: (g, 0, 0))] * 2 + [pl.BlockSpec((ch, res), lambda g: (0, 0))],
+        scratch_shapes=[pltpu.VMEM((ch, lanes), F32), pltpu.VMEM((heads * hd, lanes), BF16), pltpu.VMEM((heads * hd, lanes), BF16),
+                        pltpu.VMEM((heads * hd, lanes), BF16), pltpu.VMEM((block, res, heads * hd), BF16), pltpu.VMEM((heads * hd, lanes), F32)],
+        compiler_params=pltpu.CompilerParams(dimension_semantics=("arbitrary",), vmem_limit_bytes=48 * 1024 * 1024),
+        name='row_attention')(msa.transpose(0, 2, 1), bias, maskc, maskl, pick, wt, wo)
+
+
+def col_sums_kernel(heads, hd, ln_ref, q_ref, maskb_ref, wkv_ref, part_out, logit_buf, val_buf):
+    steps, ch, lanes = ln_ref.shape
+    res = q_ref.shape[-1]
+    block = lanes // res
+    scale = hd ** -0.5
+    qd = [q_ref[d] for d in range(hd)]
+
+    def first(g, top):
+        kv = jnp.dot(wkv_ref[...], ln_ref[g], preferred_element_type=F32).astype(BF16).astype(F32)
+        bias = maskb_ref[g]
+        for u in range(block):
+            k = kv[:hd, u * res:(u + 1) * res]
+            logit = qd[0] * k[0:1]
+            for d in range(1, hd):
+                logit += qd[d] * k[d:d + 1]
+            logit = logit * scale + bias[u:u + 1]
+            logit_buf[g * block + u] = logit
+            val_buf[g * block + u] = kv[hd:, u * res:(u + 1) * res]
+            top = jnp.maximum(top, logit)
+        return top
+    top = lax.fori_loop(0, steps, first, jnp.full((heads, res), -jnp.inf, F32))
+
+    def second(g, carry):
+        den, acc = carry
+        acc = list(acc)
+        for u in range(block):
+            s = g * block + u
+            w = jnp.exp(logit_buf[s] - top)
+            den = den + w
+            wb = w.astype(BF16).astype(F32)
+            val = val_buf[s]
+            for d in range(hd):
+                acc[d] = acc[d] + wb * val[d:d + 1]
+        return den, tuple(acc)
+    zero = jnp.zeros((heads, res), F32)
+    den, acc = lax.fori_loop(0, steps, second, (zero, (zero,) * hd))
+    for d in range(hd):
+        rows = slice(d * heads, (d + 1) * heads)
+        part_out[0, rows] = acc[d]
+        part_out[1, rows] = top
+        part_out[2, rows] = den
+
+
+def col_sums(ln, query, seq_mask, kv_w, heads, hd):
+    steps, ch, lanes = ln.shape
+    seq, res = seq_mask.shape
+    vm = pl.BlockSpec(memory_space=pltpu.VMEM)
+    maskb = ((seq_mask.astype(F32) - 1.0) * 1e4).reshape(steps, seq // steps, res)
+    return pl.pallas_call(
+        functools.partial(col_sums_kernel, heads, hd),
+        out_shape=jax.ShapeDtypeStruct((3, hd * heads, res), F32),
+        in_specs=[vm] * 4, out_specs=vm,
+        scratch_shapes=[pltpu.VMEM((seq, heads, res), F32), pltpu.VMEM((seq, hd, res), F32)],
+        compiler_params=pltpu.CompilerParams(vmem_limit_bytes=48 * 1024 * 1024),
+        name='col_sums')(ln, query, maskb, kv_w.reshape(ch, -1).T)
+
+
+def col_out_kernel(m_ref, ln_ref, att_ref, maskl_ref, wg_ref, wo_ref, wp_ref, m_out, p_out):
+    seqs, ch, res = m_out.shape
+    att = jnp.concatenate([att_ref[...]] * seqs, axis=1)
+    gate = jnp.dot(wg_ref[...], ln_ref[0], preferred_element_type=F32).astype(BF16).astype(F32)
+    y = (jax.nn.sigmoid(gate) * att).astype(BF16)
+    new = (m_ref[0].astype(F32) + jnp.dot(wo_ref[...], y, preferred_element_type=F32)).astype(BF16)
+    newf = new.astype(F32)
+    for s in range(seqs):
+        m_out[s] = new[:, s * res:(s + 1) * res]
+    proj = jnp.dot(wp_ref[...], norm_cols(newf), preferred_element_type=F32).astype(BF16)
+    proj = (proj.astype(F32) * maskl_ref[0]).astype(BF16)
+    for s in range(seqs):
+        p_out[s] = proj[:, s * res:(s + 1) * res]
+
+
+def col_out(m, ln, att, seq_mask, gate_w, out_w, proj_w):
+    steps, ch, lanes = m.shape
+    seq, res = seq_mask.shape
+    block = seq // steps
+    wg, wo = gate_w.transpose(2, 1, 0).reshape(-1, ch), out_w.transpose(2, 1, 0).reshape(ch, -1)
+    wp = proj_w.reshape(ch, -1).T
+    maskl = seq_mask.astype(F32).reshape(steps, 1, lanes)
+    full = lambda a: pl.BlockSpec(a.shape, lambda g: (0,) * a.ndim)
+    blk = pl.BlockSpec((1, ch, lanes), lambda g: (g, 0, 0))
+    m_new, proj = pl.pallas_call(
+        col_out_kernel, grid=(steps,),
+        out_shape=[jax.ShapeDtypeStruct((seq, ch, res), BF16), jax.ShapeDtypeStruct((seq, wp.shape[0], res), BF16)],
+        in_specs=[blk, blk, full(att), pl.BlockSpec((1, 1, lanes), lambda g: (g, 0, 0)), full(wg), full(wo), full(wp)],
+        out_specs=[pl.BlockSpec((block, ch, res), lambda g: (g, 0, 0)), pl.BlockSpec((block, wp.shape[0], res), lambda g: (g, 0, 0))],
+        compiler_params=pltpu.CompilerParams(dimension_semantics=("arbitrary",), vmem_limit_bytes=48 * 1024 * 1024),
+        name='col_out')(m, ln, att, maskl, wg, wo, wp)
+    return m_new.transpose(0, 2, 1), proj
 
 
 def remote(src, dst, send_sem, recv_sem, dev):
@@ -135,48 +318,73 @@
         compiler_params=params(0), name='entry_exchange')(bias, rows)
 
 
-def reduce_kernel(n, combine, part_ref, out_ref, got, mine, send_sem, recv_sem, send2, recv2):
+def reduce_kernel(n, combine, finish, n_extra, *refs):
+    part_ref, extra, out_ref = refs[0], refs[1:1 + n_extra], refs[1 + n_extra]
+    cut, got, mine, back, send_sem, recv_sem, send2, recv2 = refs[2 + n_extra:]
     me = lax.axis_index('dap')
+    terms, width, res = part_ref.shape
+    own = res // n
+    for t in range(terms):
+        flat = part_ref[t].T
+        for p in range(n):
+            cut[p, t] = flat[p * own:(p + 1) * own]
     greet_all(me, n)
     copies = []
     for k in range(1, n):
         dst = lax.rem(me + k, n)
-        cp = remote(part_ref.at[dst], got.at[me], send_sem.at[k], recv_sem.at[k], dst)
+        cp = remote(cut.at[dst], got.at[me], send_sem.at[k], recv_sem.at[k], dst)
         cp.start()
         copies.append(cp)
-    got[me] = part_ref[me]
+    got[me] = cut[me]
     for cp in copies:
         cp.wait()
     total = combine(got[...])
     mine[...] = total
-    out_ref[me] = total
+    back[me] = total
     copies = []
     for k in range(1, n):
-        cp = remote(mine, out_ref.at[me], send2.at[k], recv2.at[k], lax.rem(me + k, n))
+        cp = remote(mine, back.at[me], send2.at[k], recv2.at[k], lax.rem(me + k, n))
         cp.start()
         copies.append(cp)
     for cp in copies:
         cp.wait()
-
-
-def all_reduce(n, cid, combine, part, out_block):
+    whole = jnp.concatenate([back[p] for p in range(n)], axis=0)
+    finish(whole.T, extra, out_ref)
+
+
+def all_reduce(n, cid, combine, finish, part, extra, out_shape):
+    terms, width, res = part.shape
+    own = res // n
     return pl.pallas_call(
-        functools.partial(reduce_kernel, n, combine),
-        out_shape=jax.ShapeDtypeStruct((n,) + out_block, F32),
-        in_specs=[vmem()], out_specs=vmem(),
-        scratch_shapes=[pltpu.VMEM(part.shape, F32), pltpu.VMEM(out_block, F32)]
+        functools.partial(reduce_kernel, n, combine, finish, len(extra)),
+        out_shape=jax.ShapeDtypeStruct(out_shape, F32),
+        in_specs=[vmem()] * (1 + len(extra)), out_specs=vmem(),
+        scratch_shapes=[pltpu.VMEM((n, terms, own, width), F32)] * 2 + [pltpu.VMEM((own, width), F32), pltpu.VMEM((n, own, width), F32)]
         + [pltpu.SemaphoreType.DMA((n,))] * 4,
-        compiler_params=params(cid), name=f'all_reduce{cid}')(part)
+        compiler_params=params(cid), name=f'all_reduce{cid}')(part, *extra)
 
 
 def combine_sum(got):
-    return jnp.sum(got, axis=0)
+    return jnp.sum(got[:, 0], axis=0)
 
 
 def combine_softmax(got):
     acc, top, den = got[:, 0], got[:, 1], got[:, 2]
     scale = jnp.exp(top - jnp.max(top, axis=0, keepdims=True))
     return jnp.sum(acc * scale, axis=0) / jnp.sum(den * scale, axis=0)
+
+
+def finish_query(total, extra, out_ref):
+    count_ref, w_ref = extra
+    hd, heads, res = out_ref.shape
+    mean = (total / count_ref[...]).astype(BF16)
+    query = jnp.dot(w_ref[...], mean, preferred_element_type=F32).astype(BF16).astype(F32)
+    for d in range(hd):
+        out_ref[d] = query[d * heads:(d + 1) * heads]
+
+
+def finish_plain(total, extra, out_ref):
+    out_ref[...] = total
 
 
 def opm_kernel(side, a_ref, c_ref, o_ref, a_buf, c_buf, acc, got, s1, r1, s2, r2, s3, r3):
@@ -369,28 +577,16 @@
         row_bias = matmul_bf('ijc,ch->hij', layer_norm(pair), row_bias_w)
         bias_all, pair_blk = entry_exchange(n, side, row_bias, pair.reshape(r, side, w, pc))
         bias_full = bias_all.transpose(1, 0, 2, 3).reshape(row_bias.shape[0], res, res)
-        msa = row_attention(msa, bias_full, seq_mask, row_qkvg_w, row_out_w)
-
-        msa_ln = layer_norm(msa)
-        part = jnp.einsum('sr,src->rc', seq_mask.astype(BF16), msa_ln, preferred_element_type=F32)
-        qsum = all_reduce(n, 1, combine_sum, part.reshape(n, r, ch), (r, ch)).reshape(res, ch)
-        mask_count = jnp.sum(mask_full, axis=0).astype(F32) + 1e-10
-        query = matmul_bf('rc,chd->rhd', (qsum / mask_count[:, None]).astype(BF16), col_query_w)
-        key_val = matmul_bf('src,cad->asrd', msa_ln, col_kv_w)
-        gate = matmul_bf('src,chd->srhd', msa_ln, col_gate_w)
-        logits = jnp.einsum('rhd,srd->rhs', query, key_val[0], preferred_element_type=F32) * (hd ** -0.5) + mask_bias(seq_mask).T[:, None, :]
-        top = jnp.max(logits, axis=-1, keepdims=True)
-        weights = jnp.exp(logits - top)
-        den = jnp.sum(weights, axis=-1, keepdims=True)
-        acc = jnp.einsum('rhs,srd->rhd', weights.astype(BF16), key_val[1], preferred_element_type=F32)
-        part = jnp.stack([acc, jnp.broadcast_to(top, acc.shape), jnp.broadcast_to(den, acc.shape)], axis=0)
-        part = part.reshape(3, n, r, heads * hd).transpose(1, 0, 2, 3)
-        attended = all_reduce(n, 2, combine_softmax, part, (r, heads * hd)).reshape(res, heads, hd)
-        msa = (msa + gated_out('srhd,hdc->src', gate, attended[None], col_out_w)).astype(BF16)
-
-        msa_ln = layer_norm(msa)
-        proj = matmul_bf('src,cae->ares', msa_ln, opm_proj_w) * seq_mask.astype(BF16).T[None, :, None, :]
+        msa_t, ln_t, qsum = row_attention(msa, bias_full, seq_mask, row_qkvg_w, row_out_w)
+
+        count = (jnp.sum(mask_full, axis=0).astype(F32) + 1e-10)[None, :]
+        query = all_reduce(n, 1, combine_sum, finish_query, qsum[None], [count, col_query_w.transpose(2, 1, 0).reshape(-1, ch)], (hd, heads, res))
+        part = col_sums(ln_t, query, seq_mask, col_kv_w, heads, hd)
+        attended = all_reduce(n, 2, combine_softmax, finish_plain, part, [], part.shape[1:])
+        msa, proj = col_out(msa_t, ln_t, attended, seq_mask, col_gate_w, col_out_w, opm_proj_w)
+
         e = opm_proj_w.shape[-1]
+        proj = proj.reshape(seq, 2, e, res).transpose(1, 3, 2, 0)
         outer = opm_exchange(side, proj[0].reshape(side, w * e, seq), proj[1].reshape(side, w * e, seq))
         rows0 = y * w + core * (w // 2)
         mask_bf = mask_full.astype(BF16)

time: 327 us -> 286 us (0.87); the launches traced: 321 us -> 285 us
  matrix products: 86.7 us -> 9.94 us
  Pallas kernels: 165 us -> 223 us
  other arithmetic: 30.9 us -> 17.6 us
  local copies, waits for them, and re-layouts: 36.9 us -> 32.5 us
    pallas_call x2 -> x5, Pallas kernels: 32.2 us -> 90.7 us  [the longest x1 41.5 us: row_attention(): pl.pallas_call(functools.partial(row_kernel, heads, hd), grid=(steps,), o...]
    sub x1 -> x0, matrix products: 32.7 us -> none  [row_attention(): attn_probs = jax.nn.softmax(logits, axis=-1).astype(BF16)]
    dot_general x4 -> x2, matrix products: 32.1 us -> 0.99 us  [gated_out(): jnp.einsum(einsum_form, gated_vals, out_w, preferred_element_type=F32)]
    unnamed x35 -> x52, local copies, waits for them, and re-layouts: 0.71 us -> 9.12 us
    dot_general x8 -> x5, matrix products: 10.8 us -> 2.44 us  [matmul_bf(): jnp.einsum(einsum_form, left_arr, right_arr, preferred_element_type=F32)]
    another operation x5 -> x0, local copies, waits for them, and re-layouts: 6.96 us -> none  [block(): jnp.stack([acc, jnp.broadcast_to(top, acc.shape), jnp.broadcast_to(den, a...]
    reduce_sum x7 -> x4, other arithmetic: 10.7 us -> 3.85 us  [layer_norm(): variance = jnp.mean(centered * centered, axis=-1, keepdims=True)]
    reshape x1 -> x5, local copies, waits for them, and re-layouts: 1.54 us -> 7.56 us  [the longest x1 4.29 us: block(): proj = proj.reshape(seq, 2, e, res).transpose(1, 3, 2, 0)]
where the time goes in v2:
time: 286 us; the launch traced here: 285 us
  Pallas kernels  223 us (78%)
  local copies, waits for them, and re-layouts  32.5 us (11%)
  other arithmetic  17.6 us (6%)
  matrix products  9.94 us (3%)
    pallas_call x1, Pallas kernels, opm_exchange(): pl.pallas_call(functools.partial(opm_kernel, side), out_shape=jax.ShapeDt...  74.9 us
    pallas_call x1, Pallas kernels, row_attention(): pl.pallas_call(functools.partial(row_kernel, heads, hd), grid=(steps,), o...  41.5 us
    pallas_call x2, Pallas kernels, all_reduce(): pl.pallas_call(functools.partial(reduce_kernel, n, combine, finish, len(e...  33.2 us
    pallas_call x3, Pallas kernels, exchange(): pl.pallas_call(functools.partial(exchange_kernel, n, len(gathers), len(sw...  31.9 us
    pallas_call x1, Pallas kernels, entry_exchange(): pl.pallas_call(functools.partial(entry_kernel, n, side), out_shape=[jax.S...  16.8 us
    pallas_call x1, Pallas kernels, col_out(): pl.pallas_call(col_out_kernel, grid=(steps,), out_shape=[jax.ShapeDtypeSt...  12.9 us
    unnamed x52, local copies, waits for them, and re-layouts  9.12 us
    pallas_call x1, Pallas kernels, block_to_rows(): pl.pallas_call(functools.partial(block_to_rows_kernel, side), out_shape=j...  8.82 us

profile of v2, /device:TPU:97, one launch (start us, length us, event | category | flops | bytes accessed | tf_op | source)
XLA Modules:
  0.0 284.5 jit_solution(4261819329568441157)
XLA Ops:
  0.7 1.3 add_multiply_fusion
  2.0 1.0 convert_reduce_fusion.1
  3.0 1.1 fusion.35
  4.3 1.2 convolution_convert_fusion.2
  6.1 1.4 copy.86
  7.5 1.3 copy.134
  12.6 16.8 %entry_exchange.1 = (bf16[32,8,4,128]{3,2,1,0:T(4,128)(2,1)}, bf16[4,4,32,128]{3,2,1,0:T(8,128)(2,1)}) custom-call(bf16[8,4,128]{2,1,0:T(4,128)(2,1)} %bitcast.268, bf16[4,4,32,128]{3,2,1,0:T(8,128)(2,1)} %bitcast.255), custom_call_target="tpu_custom_call" | custom-call | tf_op jit(solution)/shard_map/entry_exchange/pallas_call | solution.py:311
  29.4 1.1 multiply_bitcast_fusion
  32.0 2.8 fusion.87
  34.8 1.6 convolution_add_fusion
  37.0 41.5 %row_attention.1 = (bf16[16,64,1024]{2,1,0:T(8,128)(2,1)S(1)}, bf16[16,64,1024]{2,1,0:T(8,128)(2,1)S(1)}, f32[64,128]{1,0:T(8,128)S(1)}) custom-call(bf16[128,64,128]{2,1,0:T(8,128)(2,1)} %bitcast.254, f32[4,128,256]{2,1,0:T(8,128)S(1)} %bitcast.239, f32[16,128,8]{2,1,0:T(8,128)S(1)} %bitcast.238, f32[16,1,1024]{2,1,0:T(1,128)S(1)} %bitcast.241, ...), custom_call_target="tpu_custom_call" | custom-call | tf_op jit(solution)/shard_map/row_attention/pallas_call | solution.py:132
  78.6 1.3 copy-done.3
  80.5 16.5 %all_reduce1.1.q_ref = f32[8,8,128]{2,1,0:T(8,128)} custom-call(f32[1,64,128]{2,1,0:T(8,128)} %bitcast.246, f32[1,128]{1,0:T(1,128)} %add_bitcast_fusion.refs_1_, bf16[64,64]{1,0:T(8,128)(2,1)} %bitcast.266), custom_call_target="tpu_custom_call" | custom-call | tf_op jit(solution)/shard_map/all_reduce1/pallas_call | solution.py:358
  98.5 3.2 %col_sums.1.refs_0_ = f32[3,64,128]{2,1,0:T(8,128)S(1)} custom-call(bf16[16,64,1024]{2,1,0:T(8,128)(2,1)S(1)} %get-tuple-element.13.ln_ref, f32[8,8,128]{2,1,0:T(8,128)S(1)} %copy-done.8, f32[16,8,128]{2,1,0:T(8,128)S(1)} %get-tuple-element.20.maskb_ref, bf16[16,64]{1,0:T(8,128)(2,1)S(1)} %bitcast.248), custom_call_target="tpu_custom_call" | custom-call | tf_op jit(solution)/shard_map/col_sums/pallas_call | solution.py:193
  102.3 16.7 %all_reduce2.1.att_ref = f32[64,128]{1,0:T(8,128)} custom-call(f32[3,64,128]{2,1,0:T(8,128)} %copy-done.7), custom_call_target="tpu_custom_call" | custom-call | tf_op jit(solution)/shard_map/all_reduce2/pallas_call | solution.py:358
  119.0 1.6 copy-done.4
  121.3 12.9 %col_out.1 = (bf16[128,64,128]{2,1,0:T(8,128)(2,1)}, bf16[128,64,128]{2,1,0:T(8,128)(2,1)S(1)}) custom-call(bf16[16,64,1024]{2,1,0:T(8,128)(2,1)S(1)} %copy-done.4, bf16[16,64,1024]{2,1,0:T(8,128)(2,1)} %copy-done.1, f32[64,128]{1,0:T(8,128)S(1)} %copy-done.9, f32[16,1,1024]{2,1,0:T(1,128)S(1)} %bitcast.242, bf16[64,64]{1,0:T(8,128)(2,1)S(1)} %bitcast.244, ...), custom_call_target="tpu_custom_call" | custom-call | tf_op jit(solution)/shard_map/col_out/pallas_call | solution.py:226
  134.2 1.3 copy-done.5
  135.6 4.3 %copy.91 = bf16[128,2,32,128]{0,2,3,1:T(8,128)(2,1)S(1)} copy(bf16[128,2,32,128]{3,2,1,0:T(8,128)(2,1)} %bitcast.240) | data formatting | bytes 4194304 | tf_op jit(solution)/shard_map/reshape | solution.py:589
  139.9 1.7 fusion.88
  141.6 74.9 %opm_exchange.1 = bf16[512,1024]{1,0:T(8,128)(2,1)} custom-call(bf16[4,1024,128]{2,1,0:T(8,128)(2,1)} %bitcast.251, bf16[4,1024,128]{2,1,0:T(8,128)(2,1)} %bitcast.250), custom_call_target="tpu_custom_call" | custom-call | tf_op jit(solution)/shard_map/opm_exchange/pallas_call | solution.py:477
  216.6 6.3 %reshape.279 = bf16[16,32,32,32]{3,2,1,0:T(8,128)(2,1)} reshape(bf16[512,1024]{1,0:T(8,128)(2,1)} %opm_exchange.1) | data formatting | bytes 2097152 | tf_op jit(solution)/shard_map/reshape | solution.py:596
  222.9 3.8 %fusion.22 = bf16[16,32,128]{2,1,0:T(8,128)(2,1)} fusion(bf16[16,32,32,32]{3,2,1,0:T(8,128)(2,1)} %reshape.279, bf16[16,32,128]{2,1,0:T(8,128)(2,1)S(1)} %bitcast.275, bf16[32,32,128]{2,1,0:T(8,128)(2,1)S(1)} %copy-done, f32[16,32]{1,0:T(8,128)S(1)} %copy-done.18), kind=kOutput, calls=%fused_computation.31 | convolution fusion | flops 134479872 | bytes 1574912 | tf_op jit(solution)/shard_map/iejf,efc->ijc/dot_general | solution.py:596
  226.6 8.8 %block_to_rows.1 = bf16[4,4,32,128]{3,2,1,0:T(8,128)(2,1)} custom-call(bf16[4,4,32,128]{3,2,1,0:T(8,128)(2,1)} %bitcast.265), custom_call_target="tpu_custom_call" | custom-call | tf_op jit(solution)/shard_map/block_to_rows/pallas_call | solution.py:525
  235.5 1.0 fusion.54
  236.6 1.2 multiply_reduce_fusion.1
  239.9 9.9 %exchange5.1 = bf16[32,4,4,128]{3,2,1,0:T(4,128)(2,1)} custom-call(bf16[4,4,128]{2,1,0:T(4,128)(2,1)} %bitcast.270), custom_call_target="tpu_custom_call" | custom-call | tf_op jit(solution)/shard_map/exchange5/pallas_call | solution.py:555
  254.3 11.6 %exchange6.1 = (bf16[32,4,4,128]{3,2,1,0:T(4,128)(2,1)}, bf16[32,4,4,128]{3,2,1,0:T(4,128)(2,1)}) custom-call(bf16[4,4,128]{2,1,0:T(4,128)(2,1)} %bitcast.269, bf16[32,4,4,128]{3,2,1,0:T(4,128)(2,1)} %bitcast.260), custom_call_target="tpu_custom_call" | custom-call | tf_op jit(solution)/shard_map/exchange6/pallas_call | solution.py:555
  265.9 1.1 fusion.55
  267.3 1.3 multiply_reduce_fusion
  272.5 10.4 %exchange7.1 = bf16[32,4,4,128]{3,2,1,0:T(4,128)(2,1)} custom-call(bf16[32,4,4,128]{3,2,1,0:T(4,128)(2,1)} %bitcast.261), custom_call_target="tpu_custom_call" | custom-call | tf_op jit(solution)/shard_map/exchange7/pallas_call | solution.py:555
  282.9 1.6 copy.110
  (104 shorter events, 20.6 us)
Async XLA Ops:
  0.6 222.2 %copy-start = (bf16[32,32,128]{2,1,0:T(8,128)(2,1)S(1)}, bf16[32,32,128]{2,1,0:T(8,128)(2,1)}, u32[]{:S(2)}) copy-start(bf16[32,32,128]{2,1,0:T(8,128)(2,1)} %param.31) | copy-start | bytes 786436
  32.0 5.1 %copy-start.2 = (f32[4,2,16,8,128]{4,3,1,2,0:T(8,128)S(1)}, f32[4,2,16,8,128]{4,3,1,2,0:T(8,128)}, u32[]{:S(2)}) copy-start(f32[4,2,16,8,128]{4,3,1,2,0:T(8,128)} %copy.131) | copy-start | bytes 1572868
  32.0 5.1 %copy-start.6 = (bf16[4,64,256]{2,1,0:T(8,128)(2,1)S(1)}, bf16[4,64,256]{2,1,0:T(8,128)(2,1)}, u32[]{:S(2)}) copy-start(bf16[4,64,256]{2,1,0:T(8,128)(2,1)} %compare_convert_fusion.pick_ref) | copy-start | bytes 393220
  32.0 5.0 %copy-start.10 = (bf16[64,4,8,8]{0,3,2,1:T(8,128)(2,1)S(1)}, bf16[64,4,8,8]{0,3,2,1:T(8,128)(2,1)}, u32[]{:S(2)}) copy-start(bf16[64,4,8,8]{0,3,2,1:T(8,128)(2,1)} %param.24) | copy-start | bytes 98308
  32.0 5.0 %copy-start.12 = (bf16[64,64]{0,1:T(8,128)(2,1)S(1)}, bf16[64,64]{0,1:T(8,128)(2,1)}, u32[]{:S(2)}) copy-start(bf16[64,64]{0,1:T(8,128)(2,1)} %copy.86) | copy-start | bytes 24580
  78.6 1.3 copy-start.3
  79.9 0.6 copy-start.13
  80.5 38.4 %copy-start.1 = (bf16[16,64,1024]{2,1,0:T(8,128)(2,1)}, bf16[16,64,1024]{2,1,0:T(8,128)(2,1)S(1)}, u32[]{:S(2)}) copy-start(bf16[16,64,1024]{2,1,0:T(8,128)(2,1)S(1)} %get-tuple-element.13.ln_ref) | copy-start | bytes 6291460
  80.5 38.5 %copy-start.11 = (bf16[64,64]{1,0:T(8,128)(2,1)S(1)}, bf16[64,64]{1,0:T(8,128)(2,1)}, u32[]{:S(2)}) copy-start(bf16[64,64]{1,0:T(8,128)(2,1)} %copy.90.wo_ref) | copy-start | bytes 24580
  80.5 38.5 %copy-start.14 = (bf16[64,2,32]{0,2,1:T(8,128)(2,1)S(1)}, bf16[64,2,32]{0,2,1:T(8,128)(2,1)}, u32[]{:S(2)}) copy-start(bf16[64,2,32]{0,2,1:T(8,128)(2,1)} %param.30) | copy-start | bytes 24580
  97.0 0.8 copy-start.8
  97.8 0.7 copy-start.15
  101.6 0.6 copy-start.7
  119.0 1.6 copy-start.4
  120.6 0.8 copy-start.9
  134.2 1.4 copy-start.5
  216.5 6.3 %copy-start.18 = (f32[16,32]{1,0:T(8,128)S(1)}, f32[16,32]{1,0:T(8,128)}, u32[]{:S(2)}) copy-start(f32[16,32]{1,0:T(8,128)} %convolution_add_fusion) | copy-start | bytes 6148
  216.5 6.3 %copy-start.20 = (bf16[4,4,32,128]{3,2,1,0:T(8,128)(2,1)S(1)}, bf16[4,4,32,128]{3,2,1,0:T(8,128)(2,1)}, u32[]{:S(2)}) copy-start(bf16[4,4,32,128]{3,2,1,0:T(8,128)(2,1)} %get-tuple-element.16) | copy-start | bytes 393220
  222.9 16.2 %copy-start.19 = (bf16[128,4]{0,1:T(4,128)(2,1)S(1)}, bf16[128,4]{0,1:T(4,128)(2,1)}, u32[]{:S(2)}) copy-start(bf16[128,4]{0,1:T(4,128)(2,1)} %param.32) | copy-start | bytes 3076
  226.6 24.2 %copy-start.17 = (bf16[128,4,4,32]{0,3,2,1:T(8,128)(2,1)S(1)}, bf16[128,4,4,32]{0,3,2,1:T(8,128)(2,1)}, u32[]{:S(2)}) copy-start(bf16[128,4,4,32]{0,3,2,1:T(8,128)(2,1)} %param.33) | copy-start | bytes 393220
  235.5 15.7 %copy-start.24 = (f32[128]{0:T(128)S(1)}, f32[128]{0:T(128)}, u32[]{:S(2)}) copy-start(f32[128]{0:T(128)} %add_multiply_fusion) | copy-start | bytes 1540
  249.7 2.0 copy-start.21
  251.7 0.8 copy-start.23
  252.3 18.0 %copy-start.16 = (bf16[128,4,4,32]{0,3,2,1:T(8,128)(2,1)S(1)}, bf16[128,4,4,32]{0,3,2,1:T(8,128)(2,1)}, u32[]{:S(2)}) copy-start(bf16[128,4,4,32]{0,3,2,1:T(8,128)(2,1)} %param.36) | copy-start | bytes 393220
  270.1 1.2 copy-start.22

commit v3 on v2

--- a/solution.py
+++ b/solution.py
@@ -32,14 +32,6 @@
 def gated_out(einsum_form, gate_proj, attended, out_w):
     gated_vals = (jax.nn.sigmoid(gate_proj.astype(F32)) * attended).astype(BF16)
     return jnp.einsum(einsum_form, gated_vals, out_w, preferred_element_type=F32)
-
-
-def triangle_rows(pair_act, pair_ln, bias_full, res_mask, qkvg_w, out_w):
-    projected = matmul_bf('ijc,cahd->aijhd', pair_ln, qkvg_w)
-    logits = jnp.einsum('ijhd,ikhd->ihjk', projected[0], projected[1], preferred_element_type=F32) * (qkvg_w.shape[-1] ** -0.5) + bias_full[None] + mask_bias(res_mask)[None, None, None, :]
-    attn_probs = jax.nn.softmax(logits, axis=-1).astype(BF16)
-    attended = jnp.einsum('ihjk,ikhd->ijhd', attn_probs, projected[2], preferred_element_type=F32)
-    return (pair_act + gated_out('ijhd,hdc->ijc', projected[3], attended, out_w)).astype(BF16)
 
 
 LOG2E = 1.4426950408889634
@@ -387,7 +379,46 @@
     out_ref[...] = total
 
 
-def opm_kernel(side, a_ref, c_ref, o_ref, a_buf, c_buf, acc, got, s1, r1, s2, r2, s3, r3):
+def norm_rows(x):
+    mean = jnp.mean(x, axis=-1, keepdims=True)
+    cen = x - mean
+    var = jnp.mean(cen * cen, axis=-1, keepdims=True)
+    return (cen * lax.rsqrt(var + 1e-5)).astype(BF16)
+
+
+def triangle(z_ref, bias_ref, maskb, qkvg_ref, out_w_ref, heads):
+    rows, res, ch = z_ref.shape
+    width = qkvg_ref.shape[-1] // 4
+    hd = width // heads
+    lane_head = lax.broadcasted_iota(jnp.int32, (res, width), 1) // hd
+    picks = [(lane_head == h).astype(F32) for h in range(heads)]
+    pick_bf = jnp.concatenate(picks, axis=0).astype(BF16)
+    bias = bias_ref[...].reshape(heads * res, res) + maskb
+    projs = [jnp.dot(norm_rows(z_ref[i]), qkvg_ref[...], preferred_element_type=F32) for i in range(rows)]
+    raws = []
+    for i in range(rows):
+        q = projs[i][:, :width].astype(BF16)
+        k = projs[i][:, width:2 * width].astype(BF16)
+        raws.append(lax.dot_general(jnp.concatenate([q] * heads, axis=0) * pick_bf, k, (((1,), (1,)), ((), ())), preferred_element_type=F32))
+    outs = []
+    for i in range(rows):
+        t = raws[i] * hd ** -0.5 + bias
+        w = jnp.exp(t - jnp.max(t, axis=-1, keepdims=True))
+        den = 1.0 / jnp.sum(w, axis=-1, keepdims=True)
+        v = projs[i][:, 2 * width:3 * width].astype(BF16)
+        outs.append(jnp.dot(w.astype(BF16), v, preferred_element_type=F32) * den)
+    for i in range(rows):
+        att = outs[i][:res] * picks[0]
+        for h in range(1, heads):
+            att += outs[i][h * res:(h + 1) * res] * picks[h]
+        gate = projs[i][:, 3 * width:].astype(BF16).astype(F32)
+        y = (jax.nn.sigmoid(gate) * att).astype(BF16)
+        z_ref[i] = (z_ref[i] + jnp.dot(y, out_w_ref[...], preferred_element_type=F32)).astype(BF16).astype(F32)
+
+
+def pair_kernel(n, side, heads, a_ref, c_ref, zblk_ref, count_ref, w_ref, maskb_ref, sb_ref, sq_ref, so_ref, eb_ref, eq_ref, eo_ref, z_out,
+                a_buf, c_buf, acc, got, terms, zsend, zrows, z_f, bias, msg, inbox, flat,
+                s1, r1, s2, r2, s3, r3, s4, r4, s5, r5, s6, r6, s7, r7, s8, r8):
     me = lax.axis_index('dap')
     y, x, c = position(me, side)
     seq = a_ref.shape[-1]
@@ -397,166 +428,214 @@
     def dev(yy, xx, cc):
         return (yy * side + xx) * 2 + cc
 
-    barrier = pltpu.get_barrier_semaphore()
-    peers = [dev(y, x, 1 - c)]
-    for k in range(1, side):
-        peers.append(dev(lax.rem(y + k, side), x, c))
-        peers.append(dev(y, lax.rem(x + k, side), c))
-    for p in peers:
-        pl.semaphore_signal(barrier, inc=1, device_id={'dap': p}, device_id_type=MESH)
-    pl.semaphore_wait(barrier, len(peers))
-
-    def slot(buf, yy, xx):
-        return buf.at[yy, xx // 2, :, pl.ds(pl.multiple_of((xx % 2) * seq, seq), seq)]
-
-    first = []
-    for k in range(1, side):
-        ty = lax.rem(y + k, side)
+    def slot(buf, yy, xx, rows=None):
+        rows = pl.ds(0, blk) if rows is None else rows
+        return buf.at[yy, xx // 2, rows, pl.ds(pl.multiple_of((xx % 2) * seq, seq), seq)]
+
+    greet_all(me, n)
+    order = [0, 1, side - 1] + list(range(2, side - 1))
+    first = {}
+    for k in [1, side - 1] + list(range(2, side - 1)):
+        ty, tx = lax.rem(y + k, side), lax.rem(x + k, side)
         cp = remote(a_ref.at[ty], slot(a_buf, y, x), s1.at[0, k], r1.at[0, k], dev(ty, x, c))
+        cq = remote(c_ref.at[tx], slot(c_buf, y, x), s1.at[1, k], r1.at[1, k], dev(y, tx, c))
         cp.start()
-        tx = lax.rem(x + k, side)
-        cq = remote(c_ref.at[tx], slot(c_buf, y, x), s1.at[1, k], r1.at[1, k], dev(y, tx, c))
         cq.start()
-        first.append((cp, cq))
-    second = []
-    for k in range(1, side):
-        cp = remote(a_ref.at[y], slot(a_buf, y, x), s2.at[0, 0, k], r2.at[0, 0, k], dev(y, lax.rem(x + k, side), c))
-        cp.start()
-        cq = remote(c_ref.at[x], slot(c_buf, y, x), s2.at[1, 0, k], r2.at[1, 0, k], dev(lax.rem(y + k, side), x, c))
-        cq.start()
-        second += [cp, cq]
+        first[k] = (cp, cq)
+    started = []
+    hop = {}
+    halves = [pl.ds(0, blk // 2), pl.ds(blk // 2, blk // 2)]
+    xn, yn = [lax.rem(x + 1, side), lax.rem(x + side - 1, side)], [lax.rem(y + 1, side), lax.rem(y + side - 1, side)]
+
+    def spread(k):
+        sy, sx = lax.rem(y - k + side, side), lax.rem(x - k + side, side)
+        for d in range(2):
+            src = a_ref.at[y] if k == 0 else slot(a_buf, sy, x)
+            cp = remote(src, slot(a_buf, sy, x), s2.at[0, k, d], r2.at[0, k, d], dev(y, xn[d], c))
+            src = c_ref.at[x] if k == 0 else slot(c_buf, y, sx)
+            cq = remote(src, slot(c_buf, y, sx), s2.at[1, k, d], r2.at[1, k, d], dev(yn[d], x, c))
+            cp.start()
+            cq.start()
+            hop[k, d] = (cp, cq)
+
+    def relay(k):
+        sy, sx = lax.rem(y - k + side, side), lax.rem(x - k + side, side)
+        for d in range(2):
+            hop[k, d][0].wait_recv()
+            fx = xn[1 - d]
+            f = remote(slot(a_buf, sy, fx, halves[d]), slot(a_buf, sy, fx, halves[d]), s3.at[0, k, d], r3.at[0, k, d], dev(y, xn[d], c))
+            f.start()
+            hop[k, d][1].wait_recv()
+            fy = yn[1 - d]
+            g = remote(slot(c_buf, fy, sx, halves[d]), slot(c_buf, fy, sx, halves[d]), s3.at[1, k, d], r3.at[1, k, d], dev(yn[d], x, c))
+            g.start()
+            started.extend([f, g])
+
     lanes = pl.ds(pl.multiple_of((x % 2) * seq, seq), seq)
-    a_buf[y, x // 2, :, lanes] = a_ref[y]
-    c_buf[y, x // 2, :, lanes] = c_ref[x]
-    order = [1, side - 1] + list(range(2, side - 1))
-    for k in order:
-        cp, cq = first[k - 1]
-        cp.wait_recv()
-        sy = lax.rem(y - k + side, side)
-        for q in range(1, side):
-            f = remote(slot(a_buf, sy, x), slot(a_buf, sy, x), s2.at[0, k, q], r2.at[0, k, q], dev(y, lax.rem(x + q, side), c))
-            f.start()
-            second.append(f)
-        cq.wait_recv()
-        sx = lax.rem(x - k + side, side)
-        for q in range(1, side):
-            f = remote(slot(c_buf, y, sx), slot(c_buf, y, sx), s2.at[1, k, q], r2.at[1, k, q], dev(lax.rem(y + q, side), x, c))
-            f.start()
-            second.append(f)
-    for cp, cq in first:
-        cp.wait_send()
-        cq.wait_send()
-    for f in second:
+    for pos, k in enumerate(order):
+        if k:
+            first[k][0].wait_recv()
+            first[k][1].wait_recv()
+        spread(k)
+        if pos == 0:
+            a_buf[y, x // 2, :, lanes] = a_ref[y]
+            c_buf[y, x // 2, :, lanes] = c_ref[x]
+        else:
+            relay(order[pos - 1])
+    relay(order[-1])
+    for k in order[1:]:
+        first[k][0].wait_send()
+        first[k][1].wait_send()
+    for pair in hop.values():
+        pair[0].wait_send()
+        pair[1].wait_send()
+    for f in started:
         f.wait()
-    rows = blk // 2
+
+    cols = blk // 2
 
     def product(base, dst):
-        def tile(t, _):
-            r0 = pl.multiple_of(base + t * 128, 128)
-            total = jnp.zeros((128, blk), F32)
-            for yy in range(side):
-                for xx in range(half):
-                    total += lax.dot_general(a_buf[yy, xx, pl.ds(r0, 128), :], c_buf[yy, xx], (((1,), (1,)), ((), ())),
-                                             preferred_element_type=F32)
-            dst[pl.ds(pl.multiple_of(t * 128, 128), 128), :] = total
+        def chunk(t, _):
+            yy, xx = t // half, t % half
+            part = lax.dot_general(c_buf[yy, xx], a_buf[yy, xx, pl.ds(pl.multiple_of(base, cols), cols), :], (((1,), (1,)), ((), ())),
+                                   preferred_element_type=F32)
+
+            @pl.when(t == 0)
+            def _():
+                dst[...] = part
+
+            @pl.when(t > 0)
+            def _():
+                dst[...] += part
             return 0
-        lax.fori_loop(0, rows // 128, tile, 0)
-
-    product((1 - c) * rows, acc.at[0])
-    swap = remote(acc.at[0], got, s3, r3, dev(y, x, 1 - c))
+        lax.fori_loop(0, side * half, chunk, 0)
+
+    product((1 - c) * cols, acc.at[0])
+    swap = remote(acc.at[0], got, s4, r4, dev(y, x, 1 - c))
     swap.start()
-    product(c * rows, acc.at[1])
+    product(c * cols, acc.at[1])
     swap.wait()
-    o_ref[...] = (acc[1] + got[...]).astype(BF16)
-
-
-def opm_exchange(side, a, c):
+
+    w = zblk_ref.shape[2]
+    e = blk // w
+    per = 128 // e
+    lane_i = lax.broadcasted_iota(jnp.int32, (w, 128), 1) // e
+    keep = [(lane_i == i).astype(F32) for i in range(per)]
+
+    def place(f, _):
+        for g in range(cols // 128):
+            rows = pl.ds(pl.multiple_of(f * w, w), w)
+            both = acc[1, rows, g * 128:(g + 1) * 128] + got[rows, g * 128:(g + 1) * 128]
+            for i in range(per):
+                r0 = (g * per + i) * w
+                terms[r0:r0 + w, pl.ds(pl.multiple_of(f * 128, 128), 128)] = (both * keep[i]).astype(BF16)
+        return 0
+    lax.fori_loop(0, blk // w, place, 0)
+    update = jnp.dot(terms[...], w_ref[...], preferred_element_type=F32) / count_ref[...]
+    slots, r, _, ch = zblk_ref.shape
+    fresh = (zblk_ref[...].reshape(slots * r * w, ch).astype(F32) + update).astype(BF16)
+    zsend[...] = fresh.reshape(slots, r, w, ch)
+
+    my_core = x // half
+    for t in range(side):
+        dst = y * 2 * side + (c * half + t // 2) * 2 + t % 2
+
+        @pl.when(dst != me)
+        def _():
+            remote(zsend.at[t], zrows.at[x], s5.at[t], r5.at[x], dst).start()
+
+        @pl.when(dst == me)
+        def _():
+            zrows[x] = zsend[t]
+    for t in range(side):
+        dst = y * 2 * side + (c * half + t // 2) * 2 + t % 2
+        src = y * 2 * side + t * 2 + my_core
+
+        @pl.when(dst != me)
+        def _():
+            remote(zsend.at[t], zrows.at[x], s5.at[t], r5.at[x], dst).wait_send()
+
+        @pl.when(src != me)
+        def _():
+            remote(zsend.at[t], zrows.at[t], s5.at[t], r5.at[t], dst).wait_recv()
+    for t in range(side):
+        z_f[:, t * w:(t + 1) * w, :] = zrows[t].astype(F32)
+
+    res = side * w
+    nh = r * heads
+
+    def bias_rows(wb_ref):
+        parts = [lax.dot_general(wb_ref[...], norm_rows(z_f[i]), (((1,), (1,)), ((), ())), preferred_element_type=F32)[:heads] for i in range(r)]
+        return jnp.concatenate(parts, axis=0).astype(BF16)
+
+    def gather_bias(turn):
+        for h in range(heads):
+            plane = flat[pl.ds(h, res, stride=heads), :]
+            bias[h] = plane.T if turn else plane
+
+    def exchange_all(box, src_of, send_sem, recv_sem):
+        copies = []
+        for k in range(1, n):
+            dst = lax.rem(me + k, n)
+            cp = remote(src_of(dst), box.at[me], send_sem.at[k], recv_sem.at[k], dst)
+            cp.start()
+            copies.append(cp)
+        box[me] = src_of(me)[...]
+        for cp in copies:
+            cp.wait()
+
+    msg[0, 0, :nh] = bias_rows(sb_ref)
+    exchange_all(inbox.at[0, :, :nh], lambda p: msg.at[0, 0, :nh], s6, r6)
+    flat[...] = inbox[0, :, :nh].astype(F32).reshape(n * nh, res)
+    gather_bias(False)
+    triangle(z_f, bias, maskb_ref[...], sq_ref, so_ref, heads)
+
+    rr = r * r
+
+    def pack(slot_id):
+        for p in range(n):
+            msg[slot_id, p, :rr] = jnp.concatenate([z_f[i, p * r:(p + 1) * r, :] for i in range(r)], axis=0).astype(BF16)
+
+    def unpack(slot_id):
+        flat[...] = inbox[slot_id, :, :rr].astype(F32).reshape(n * rr, ch)
+        for i in range(r):
+            z_f[i] = flat[pl.ds(i, res, stride=r), :]
+
+    pack(1)
+    rows_b = bias_rows(eb_ref)
+    for p in range(n):
+        msg[1, p, rr:] = rows_b
+    exchange_all(inbox.at[1], lambda p: msg.at[1, p], s7, r7)
+    flat[...] = inbox[1, :, rr:].astype(F32).reshape(n * nh, res)
+    gather_bias(True)
+    unpack(1)
+    triangle(z_f, bias, maskb_ref[...], eq_ref, eo_ref, heads)
+    pack(2)
+    exchange_all(inbox.at[2, :, :rr], lambda p: msg.at[2, p, :rr], s8, r8)
+    unpack(2)
+    z_out[...] = z_f[...].astype(BF16)
+
+
+def pair_steps(n, side, heads, a, c, zblk, count, w, maskb, weights):
     blk, seq = a.shape[1:]
+    slots, r, wd, ch = zblk.shape
+    res = side * wd
+    assert r * r == r * heads and res == 128 and seq == 128
     buf = pltpu.VMEM((side, side // 2, blk, 2 * seq), BF16)
     dma = pltpu.SemaphoreType.DMA
+    box = pltpu.VMEM((3, n, 2 * r * r, ch), BF16)
+    half = pltpu.VMEM((blk, blk // 2), F32)
+    ops = [a, c, zblk, count, w, maskb] + weights
     return pl.pallas_call(
-        functools.partial(opm_kernel, side),
-        out_shape=jax.ShapeDtypeStruct((blk // 2, blk), BF16),
-        in_specs=[vmem(), vmem()], out_specs=vmem(),
-        scratch_shapes=[buf, buf, pltpu.VMEM((2, blk // 2, blk), F32), pltpu.VMEM((blk // 2, blk), F32),
-                        dma((2, side)), dma((2, side)), dma((2, side, side)), dma((2, side, side)), dma, dma],
-        compiler_params=params(3, 60 * 1024 * 1024), name='opm_exchange')(a, c)
-
-
-def block_to_rows_kernel(side, block_ref, rows_out, send_sem, recv_sem):
-    me = lax.axis_index('dap')
-    y, x, c = position(me, side)
-    half = side // 2
-    core = x // half
-    my_slot = (x % half) * 2 + c
-    barrier = pltpu.get_barrier_semaphore()
-    for t in range(2 * side):
-        peer = y * 2 * side + t
-
-        @pl.when(peer != me)
-        def _():
-            pl.semaphore_signal(barrier, inc=1, device_id={'dap': peer}, device_id_type=MESH)
-    pl.semaphore_wait(barrier, 2 * side - 1)
-    for t in range(side):
-        dst = y * 2 * side + (c * half + t // 2) * 2 + t % 2
-
-        @pl.when(dst != me)
-        def _():
-            remote(block_ref.at[t], rows_out.at[x], send_sem.at[t], recv_sem.at[x], dst).start()
-
-        @pl.when(dst == me)
-        def _():
-            rows_out[x] = block_ref[t]
-    for t in range(side):
-        dst = y * 2 * side + (c * half + t // 2) * 2 + t % 2
-        src = y * 2 * side + t * 2 + core
-
-        @pl.when(dst != me)
-        def _():
-            remote(block_ref.at[t], rows_out.at[x], send_sem.at[t], recv_sem.at[x], dst).wait_send()
-
-        @pl.when(src != me)
-        def _():
-            remote(block_ref.at[t], rows_out.at[t], send_sem.at[t], recv_sem.at[t], dst).wait_recv()
-
-
-def block_to_rows(side, block):
-    slots, r, w, ch = block.shape
-    return pl.pallas_call(
-        functools.partial(block_to_rows_kernel, side),
-        out_shape=jax.ShapeDtypeStruct((side, r, w, ch), block.dtype),
-        in_specs=[vmem()], out_specs=vmem(),
-        scratch_shapes=[pltpu.SemaphoreType.DMA((side,)), pltpu.SemaphoreType.DMA((side,))],
-        compiler_params=params(4), name='block_to_rows')(block)
-
-
-def exchange_kernel(n, n_gather, n_swap, *refs):
-    k_in = n_gather + n_swap
-    ins, outs, (send_sem, recv_sem) = refs[:k_in], refs[k_in:2 * k_in], refs[2 * k_in:]
-    me = lax.axis_index('dap')
-    greet_all(me, n)
-    copies = []
-    for k in range(1, n):
-        dst = lax.rem(me + k, n)
-        for a in range(k_in):
-            src = ins[a] if a < n_gather else ins[a].at[dst]
-            cp = remote(src, outs[a].at[me], send_sem.at[a, k], recv_sem.at[a, k], dst)
-            cp.start()
-            copies.append(cp)
-    for a in range(k_in):
-        outs[a][me] = ins[a][...] if a < n_gather else ins[a][me]
-    for cp in copies:
-        cp.wait()
-
-
-def exchange(n, cid, gathers, swaps):
-    ops = list(gathers) + list(swaps)
-    shapes = [jax.ShapeDtypeStruct((n,) + g.shape, g.dtype) for g in gathers] + [jax.ShapeDtypeStruct(s.shape, s.dtype) for s in swaps]
-    return pl.pallas_call(
-        functools.partial(exchange_kernel, n, len(gathers), len(swaps)),
-        out_shape=shapes, in_specs=[vmem()] * len(ops), out_specs=[vmem()] * len(ops),
-        scratch_shapes=[pltpu.SemaphoreType.DMA((len(ops), n))] * 2,
-        compiler_params=params(cid), name=f'exchange{cid}')(*ops)
+        functools.partial(pair_kernel, n, side, heads),
+        out_shape=jax.ShapeDtypeStruct((r, res, ch), BF16),
+        in_specs=[vmem()] * len(ops), out_specs=vmem(),
+        scratch_shapes=[buf, buf, pltpu.VMEM((2, blk, blk // 2), F32), half, pltpu.VMEM((slots * r * wd, blk * 128 // wd), BF16),
+                        pltpu.VMEM(zblk.shape, BF16), pltpu.VMEM((side, r, wd, ch), BF16), pltpu.VMEM((r, res, ch), F32),
+                        pltpu.VMEM((heads, res, res), F32), box, box, pltpu.VMEM((n * r * r, ch), F32),
+                        dma((2, side)), dma((2, side)), dma((2, side, 2)), dma((2, side, 2)), dma((2, side, 2)), dma((2, side, 2)),
+                        dma, dma, dma((side,)), dma((side,))] + [dma((n,))] * 6,
+        compiler_params=params(3, 60 * 1024 * 1024), name='pair_steps')(*ops)
 
 
 def solution(mesh):
@@ -586,30 +665,19 @@
         msa, proj = col_out(msa_t, ln_t, attended, seq_mask, col_gate_w, col_out_w, opm_proj_w)
 
         e = opm_proj_w.shape[-1]
-        proj = proj.reshape(seq, 2, e, res).transpose(1, 3, 2, 0)
-        outer = opm_exchange(side, proj[0].reshape(side, w * e, seq), proj[1].reshape(side, w * e, seq))
+        a = proj[:, :e].transpose(2, 1, 0).reshape(side, w * e, seq)
+        c = proj[:, e:].reshape(seq, e, side, w).transpose(2, 1, 3, 0).reshape(side, e * w, seq)
         rows0 = y * w + core * (w // 2)
         mask_bf = mask_full.astype(BF16)
         mask_i = lax.dynamic_slice_in_dim(mask_bf, rows0, w // 2, axis=1)
         mask_j = lax.dynamic_slice_in_dim(mask_bf, x * w, w, axis=1)
-        counts = jnp.einsum('si,sj->ij', mask_i, mask_j, preferred_element_type=F32)
-        update = jnp.einsum('iejf,efc->ijc', outer.reshape(w // 2, e, w, e), opm_out_w, preferred_element_type=F32) / (1e-3 + counts)[:, :, None]
-        pair_blk = (pair_blk.reshape(w // 2, w, pc) + update).astype(BF16)
-        rows = block_to_rows(side, pair_blk.reshape(side, r, w, pc))
-        pair = rows.transpose(1, 0, 2, 3).reshape(r, res, pc)
-
-        pair_ln = layer_norm(pair)
-        start_all, = exchange(n, 5, [matmul_bf('ijc,ch->hij', pair_ln, start_bias_w)], [])
-        start_full = start_all.transpose(1, 0, 2, 3).reshape(-1, res, res)
-        pair = triangle_rows(pair, pair_ln, start_full, res_mask, start_qkvg_w, start_out_w)
-
-        end_bias = matmul_bf('ijc,ch->hij', layer_norm(pair), end_bias_w)
-        end_all, cols = exchange(n, 6, [end_bias], [pair.reshape(r, n, r, pc).transpose(1, 2, 0, 3)])
-        end_full = end_all.transpose(1, 3, 0, 2).reshape(-1, res, res)
-        cols = cols.transpose(1, 0, 2, 3).reshape(r, res, pc)
-        cols = triangle_rows(cols, layer_norm(cols), end_full, res_mask, end_qkvg_w, end_out_w)
-        back, = exchange(n, 7, [], [cols.reshape(r, n, r, pc).transpose(1, 2, 0, 3)])
-        pair_out = back.transpose(1, 0, 2, 3).reshape(r, res, pc)
+        counts = 1e-3 + jnp.einsum('si,sj->ij', mask_i, mask_j, preferred_element_type=F32)
+        counts = jnp.broadcast_to(counts[:, :, None], (w // 2, w, pc)).reshape(-1, pc)
+        spread_w = jnp.broadcast_to(opm_out_w.transpose(1, 0, 2)[:, None], (e, 128 // e, e, pc)).reshape(-1, pc)
+        tri_heads = start_bias_w.shape[-1]
+        maskb = mask_bias(res_mask)[None, :]
+        weights = [start_bias_w.T, start_qkvg_w.reshape(pc, -1), start_out_w.reshape(-1, pc), end_bias_w.T, end_qkvg_w.reshape(pc, -1), end_out_w.reshape(-1, pc)]
+        pair_out = pair_steps(n, side, tri_heads, a, c, pair_blk, counts, spread_w, maskb, weights)
         return msa, pair_out
 
     row_spec = P(('data', 'dap'), None, None)

time: 286 us -> 236 us (0.83)
  Pallas kernels: 223 us -> 202 us
  local copies, waits for them, and re-layouts: 32.5 us -> 19.6 us
  matrix products: 9.94 us -> 2.23 us
  other arithmetic: 17.6 us -> 9.96 us
    pallas_call x5 -> x1, Pallas kernels: 116 us -> 94 us  [pair_steps(): pl.pallas_call(functools.partial(pair_kernel, n, side, heads), out_shape=...]
    reshape x2, local copies, waits for them, and re-layouts: 10.6 us -> 1.54 us  [the longest x1 0.77 us: block(): start_qkvg_w.reshape(pc, -1)]
    dot_general x4 -> x1, matrix products: 6.38 us -> 1.01 us  [block(): jnp.einsum('si,sj->ij', mask_i, mask_j, preferred_element_type=F32)]
    convert_element_type x4 -> x0, other arithmetic: 3.06 us -> none  [the longest x2 1.94 us: triangle_rows(): jnp.einsum('ijhd,ikhd->ihjk', projected[0], projected[1], preferred_eleme...]
    unnamed x52 -> x45, local copies, waits for them, and re-layouts: 9.12 us -> 8.94 us
where the time goes in v3:
time: 236 us; the launch traced here: 235 us
  Pallas kernels  202 us (86%)
  local copies, waits for them, and re-layouts  19.6 us (8%)
  other arithmetic  9.96 us (4%)
    pallas_call x1, Pallas kernels, pair_steps(): pl.pallas_call(functools.partial(pair_kernel, n, side, heads), out_shape=...  94 us
    pallas_call x1, Pallas kernels, row_attention(): pl.pallas_call(functools.partial(row_kernel, heads, hd), grid=(steps,), o...  42.1 us
    pallas_call x2, Pallas kernels, all_reduce(): pl.pallas_call(functools.partial(reduce_kernel, n, combine, finish, len(e...  33.1 us
    pallas_call x1, Pallas kernels, entry_exchange(): pl.pallas_call(functools.partial(entry_kernel, n, side), out_shape=[jax.S...  16.9 us
    pallas_call x1, Pallas kernels, col_out(): pl.pallas_call(col_out_kernel, grid=(steps,), out_shape=[jax.ShapeDtypeSt...  12.9 us
    unnamed x45, local copies, waits for them, and re-layouts  8.94 us

profile of v3, /device:TPU:97, one launch (start us, length us, event | category | flops | bytes accessed | tf_op | source)
XLA Modules:
  0.0 234.9 jit_solution(94272102112042266)
XLA Ops:
  0.6 0.9 multiply_bitcast_fusion.1
  1.9 1.0 convert_reduce_fusion
  2.9 1.1 fusion.4
  4.1 1.2 convolution_convert_fusion
  5.3 0.6 copy.58
  5.9 16.9 %entry_exchange.1 = (bf16[32,8,4,128]{3,2,1,0:T(4,128)(2,1)}, bf16[4,4,32,128]{3,2,1,0:T(8,128)(2,1)}) custom-call(bf16[8,4,128]{2,1,0:T(4,128)(2,1)} %bitcast.96, bf16[4,4,32,128]{3,2,1,0:T(8,128)(2,1)} %bitcast.88), custom_call_target="tpu_custom_call" | custom-call | tf_op jit(solution)/shard_map/entry_exchange/pallas_call | solution.py:303
  22.8 1.1 multiply_bitcast_fusion
  24.2 0.8 copy.54
  25.3 1.0 copy-done.2
  26.4 42.1 %row_attention.1 = (bf16[16,64,1024]{2,1,0:T(8,128)(2,1)S(1)}, bf16[16,64,1024]{2,1,0:T(8,128)(2,1)S(1)}, f32[64,128]{1,0:T(8,128)S(1)}) custom-call(bf16[128,64,128]{2,1,0:T(8,128)(2,1)} %bitcast.87, f32[4,128,256]{2,1,0:T(8,128)S(1)} %bitcast.72, f32[16,128,8]{2,1,0:T(8,128)S(1)} %bitcast.71, f32[16,1,1024]{2,1,0:T(1,128)S(1)} %bitcast.73, ...), custom_call_target="tpu_custom_call" | custom-call | tf_op jit(solution)/shard_map/row_attention/pallas_call | solution.py:124
  68.5 1.3 copy-done.3
  69.9 0.6 copy-done.9
  70.5 4.4 %fusion.11 = (bf16[4096,128]{1,0:T(8,128)(2,1)}, s32[128]{0:T(128)S(1)}) fusion(s32[4096,128]{1,0:T(8,128)} %param.21), kind=kLoop, calls=%fused_computation.39 | loop fusion | flops 1048448 | bytes 3146240 | tf_op jit(solution)/shard_map/convert_element_type | solution.py:671
  75.5 0.6 copy.57
  76.1 16.4 %all_reduce1.1.q_ref = f32[8,8,128]{2,1,0:T(8,128)} custom-call(f32[1,64,128]{2,1,0:T(8,128)} %bitcast.78, f32[1,128]{1,0:T(1,128)} %add_bitcast_fusion.refs_1_, bf16[64,64]{1,0:T(8,128)(2,1)} %bitcast.92), custom_call_target="tpu_custom_call" | custom-call | tf_op jit(solution)/shard_map/all_reduce1/pallas_call | solution.py:350
  92.5 0.7 copy-done.6
  93.3 3.2 %col_sums.1.refs_0_ = f32[3,64,128]{2,1,0:T(8,128)S(1)} custom-call(bf16[16,64,1024]{2,1,0:T(8,128)(2,1)S(1)} %get-tuple-element.11.ln_ref, f32[8,8,128]{2,1,0:T(8,128)S(1)} %copy-done.6, f32[16,8,128]{2,1,0:T(8,128)S(1)} %get-tuple-element.16.maskb_ref, bf16[16,64]{1,0:T(8,128)(2,1)S(1)} %bitcast.80), custom_call_target="tpu_custom_call" | custom-call | tf_op jit(solution)/shard_map/col_sums/pallas_call | solution.py:185
  96.5 0.6 copy-done.5
  97.1 16.7 %all_reduce2.1.att_ref = f32[64,128]{1,0:T(8,128)} custom-call(f32[3,64,128]{2,1,0:T(8,128)} %copy-done.5), custom_call_target="tpu_custom_call" | custom-call | tf_op jit(solution)/shard_map/all_reduce2/pallas_call | solution.py:350
  113.9 1.6 copy-done.4
  115.5 0.8 copy-done.7
  116.3 12.9 %col_out.1 = (bf16[128,64,128]{2,1,0:T(8,128)(2,1)}, bf16[128,64,128]{2,1,0:T(8,128)(2,1)S(1)}) custom-call(bf16[16,64,1024]{2,1,0:T(8,128)(2,1)S(1)} %copy-done.4, bf16[16,64,1024]{2,1,0:T(8,128)(2,1)} %copy-done.1, f32[64,128]{1,0:T(8,128)S(1)} %copy-done.7, f32[16,1,1024]{2,1,0:T(1,128)S(1)} %bitcast.74, bf16[64,64]{1,0:T(8,128)(2,1)S(1)} %bitcast.76, ...), custom_call_target="tpu_custom_call" | custom-call | tf_op jit(solution)/shard_map/col_out/pallas_call | solution.py:218
  129.6 1.0 copy.42
  130.6 1.1 copy.43
  131.7 2.3 copy.41
  134.0 1.0 convolution_add_fusion
  135.1 0.9 broadcast_in_dim.12.count_ref
  136.1 1.1 broadcast_in_dim.13
  137.2 0.8 copy.45.sq_ref
  138.0 0.8 copy.46.eq_ref
  139.3 94.0 %pair_steps.1 = bf16[4,128,128]{2,1,0:T(8,128)(2,1)} custom-call(bf16[4,1024,128]{2,1,0:T(8,128)(2,1)} %bitcast.84, bf16[4,1024,128]{2,1,0:T(8,128)(2,1)} %bitcast.83, bf16[4,4,32,128]{3,2,1,0:T(8,128)(2,1)} %get-tuple-element.15.zblk_ref, f32[512,128]{1,0:T(8,128)} %broadcast_in_dim.12.count_ref, bf16[4096,128]{1,0:T(8,128)(2,1)} %bitcast.82, ...), custom_call_target="tpu_custom_call" | custom-call | tf_op jit(solution)/shard_map/pair_steps/pallas_call | solution.py:629
  233.3 1.6 copy.60
  (55 shorter events, 2.8 us)
Async XLA Ops:
  0.6 3.4 %copy-start = (bf16[128,8]{0,1:T(8,128)(2,1)S(1)}, bf16[128,8]{0,1:T(8,128)(2,1)}, u32[]{:S(2)}) copy-start(bf16[128,8]{0,1:T(8,128)(2,1)} %param.23) | copy-start | bytes 6148
  5.9 19.3 %copy-start.16 = (bf16[8,8,64]{2,1,0:T(8,128)(2,1)S(1)}, bf16[8,8,64]{2,1,0:T(8,128)(2,1)}, u32[]{:S(2)}) copy-start(bf16[8,8,64]{2,1,0:T(8,128)(2,1)} %param.25) | copy-start | bytes 24580
  22.8 2.6 %copy-start.8 = (bf16[64,4,8,8]{0,3,2,1:T(8,128)(2,1)S(1)}, bf16[64,4,8,8]{0,3,2,1:T(8,128)(2,1)}, u32[]{:S(2)}) copy-start(bf16[64,4,8,8]{0,3,2,1:T(8,128)(2,1)} %param.24) | copy-start | bytes 98308
  25.3 1.0 copy-start.2
  68.5 1.3 copy-start.3
  69.9 0.6 copy-start.9
  70.5 26.0 %copy-start.1 = (bf16[16,64,1024]{2,1,0:T(8,128)(2,1)}, bf16[16,64,1024]{2,1,0:T(8,128)(2,1)S(1)}, u32[]{:S(2)}) copy-start(bf16[16,64,1024]{2,1,0:T(8,128)(2,1)S(1)} %get-tuple-element.11.ln_ref) | copy-start | bytes 6291460
  70.5 5.0 %copy-start.17 = (bf16[64,8,8]{0,2,1:T(8,128)(2,1)S(1)}, bf16[64,8,8]{0,2,1:T(8,128)(2,1)}, u32[]{:S(2)}) copy-start(bf16[64,8,8]{0,2,1:T(8,128)(2,1)} %param.26) | copy-start | bytes 24580
  70.5 22.0 %copy-start.11 = (bf16[64,2,8]{0,2,1:T(8,128)(2,1)S(1)}, bf16[64,2,8]{0,2,1:T(8,128)(2,1)}, u32[]{:S(2)}) copy-start(bf16[64,2,8]{0,2,1:T(8,128)(2,1)} %param.27) | copy-start | bytes 6148
  70.5 43.3 %copy-start.18 = (bf16[8,8,64]{2,1,0:T(8,128)(2,1)S(1)}, bf16[8,8,64]{2,1,0:T(8,128)(2,1)}, u32[]{:S(2)}) copy-start(bf16[8,8,64]{2,1,0:T(8,128)(2,1)} %param.29) | copy-start | bytes 24580
  74.9 39.0 %copy-start.19 = (bf16[64,8,8]{0,2,1:T(8,128)(2,1)S(1)}, bf16[64,8,8]{0,2,1:T(8,128)(2,1)}, u32[]{:S(2)}) copy-start(bf16[64,8,8]{0,2,1:T(8,128)(2,1)} %param.28) | copy-start | bytes 24580
  74.9 39.0 %copy-start.10 = (bf16[64,2,32]{0,2,1:T(8,128)(2,1)S(1)}, bf16[64,2,32]{0,2,1:T(8,128)(2,1)}, u32[]{:S(2)}) copy-start(bf16[64,2,32]{0,2,1:T(8,128)(2,1)} %param.30) | copy-start | bytes 24580
  92.5 0.8 copy-start.6
  96.5 0.6 copy-start.5
  113.9 1.6 copy-start.4
  115.5 0.8 copy-start.7
  130.6 3.4 %copy-start.12 = (bf16[4096,128]{1,0:T(8,128)(2,1)S(1)}, bf16[4096,128]{1,0:T(8,128)(2,1)}, u32[]{:S(2)}) copy-start(bf16[4096,128]{1,0:T(8,128)(2,1)} %get-tuple-element.18) | copy-start | bytes 3145732
  131.7 4.3 %copy-start.13 = (bf16[32,32,128]{2,1,0:T(8,128)(2,1)S(1)}, bf16[32,32,128]{2,1,0:T(8,128)(2,1)}, u32[]{:S(2)}) copy-start(bf16[32,32,128]{2,1,0:T(8,128)(2,1)} %param.31) | copy-start | bytes 786436
  134.0 3.2 %copy-start.14 = (bf16[128,4,4,32]{0,3,2,1:T(8,128)(2,1)S(1)}, bf16[128,4,4,32]{0,3,2,1:T(8,128)(2,1)}, u32[]{:S(2)}) copy-start(bf16[128,4,4,32]{0,3,2,1:T(8,128)(2,1)} %param.33) | copy-start | bytes 393220
  134.0 4.0 %copy-start.15 = (bf16[128,4,4,32]{0,3,2,1:T(8,128)(2,1)S(1)}, bf16[128,4,4,32]{0,3,2,1:T(8,128)(2,1)}, u32[]{:S(2)}) copy-start(bf16[128,4,4,32]{0,3,2,1:T(8,128)(2,1)} %param.36) | copy-start | bytes 393220
  134.0 4.8 %copy-start.20 = (s32[128]{0:T(128)S(1)}, s32[128]{0:T(128)}, u32[]{:S(2)}) copy-start(s32[128]{0:T(128)} %param.22) | copy-start | bytes 1540

commit v4 on v0

v4 whole, which is shorter than its diff:
```python
import functools
import math

import jax
import jax.numpy as jnp
from jax import lax
from jax.experimental import pallas as pl
from jax.experimental.pallas import tpu as pltpu
from jax.sharding import PartitionSpec as P

MESH = pl.DeviceIdType.MESH
F32 = jnp.float32
BF16 = jnp.bfloat16
NT = (((1,), (1,)), ((), ()))


def dot(a, b):
    return jnp.dot(a, b, preferred_element_type=F32)


def dot_nt(a, b):
    return lax.dot_general(a, b, NT, preferred_element_type=F32)


LOG2E = 1.4426950408889634
BLOCK = 16


def norm_cols(x):
    mean = jnp.mean(x, axis=0, keepdims=True)
    cen = x - mean
    var = jnp.mean(cen * cen, axis=0, keepdims=True)
    return (cen * lax.rsqrt(var + 1e-5)).astype(BF16)


def wide(ref, g):
    return jnp.concatenate([ref[g * BLOCK + u] for u in range(BLOCK)], axis=1)


def put(ref, g, value):
    res = ref.shape[-1]
    for u in range(BLOCK):
        ref[g * BLOCK + u] = value[:, u * res:(u + 1) * res]


def split_mask(hd):
    whole = jnp.float32(-1e4 * hd ** 0.5)
    high = whole.astype(BF16).astype(F32)
    mid = (whole - high).astype(BF16).astype(F32)
    return high, mid, whole - high - mid


def row_project(heads, hd, m_ref, mask_ref, wt_ref, q_buf, k_buf, v_buf, g_buf):
    seq, ch, res = m_ref.shape
    width = heads * hd
    terms = split_mask(hd)

    def step(g, _):
        proj = jnp.dot(wt_ref[...], norm_cols(wide(m_ref, g).astype(F32)), preferred_element_type=F32)
        put(q_buf, g, proj[:width].astype(BF16))
        put(v_buf, g, proj[2 * width:3 * width].astype(BF16))
        put(g_buf, g, proj[3 * width:].astype(BF16))
        for u in range(BLOCK):
            s = g * BLOCK + u
            off = 1.0 - mask_ref[pl.ds(s, 1), :]
            row = lax.broadcasted_iota(jnp.int32, (16, res), 0)
            extra = jnp.where(row == 0, terms[0], jnp.where(row == 1, terms[1], jnp.where(row == 2, terms[2], 0.0))) * off
            k_buf[s] = jnp.concatenate([proj[width:2 * width, u * res:(u + 1) * res], extra], axis=0).T.astype(BF16)
        return 0
    lax.fori_loop(0, seq // BLOCK, step, 0)


def row_attend(heads, hd, bias_ref, pick_ref, q_buf, k_buf, v_buf, att_buf, raw_buf, w_buf, den_buf):
    seq, width, res = q_buf.shape
    pairs = heads // 2
    scale = LOG2E * hd ** -0.5
    row = lax.broadcasted_iota(jnp.int32, (16, 2 * res), 0)
    ones = jnp.where(row < 3, 1.0, 0.0).astype(BF16)

    def logits(s, b):
        qt = q_buf[s]
        q2 = jnp.concatenate([qt, qt], axis=1)
        keys = k_buf[s]
        for p in range(pairs):
            raw_buf[b, p] = jnp.dot(keys, jnp.concatenate([q2 * pick_ref[p], ones], axis=0), preferred_element_type=F32)

    def weigh(b):
        for p in range(pairs):
            t = raw_buf[b, p] * scale + bias_ref[p]
            w = jnp.exp2(t - jnp.max(t, axis=0, keepdims=True))
            w_buf[b, p] = w.astype(BF16)
            den_buf[b, p] = jnp.broadcast_to(1.0 / jnp.sum(w, axis=0, keepdims=True), (8, 2 * res))

    def values(s, b):
        for p in range(pairs):
            lo = 2 * p * hd
            o = jnp.dot(v_buf[s, lo:lo + 2 * hd], w_buf[b, p], preferred_element_type=F32) * den_buf[b, p, 0:1]
            att_buf[s, lo:lo + hd] = o[:hd, :res]
            att_buf[s, lo + hd:lo + 2 * hd] = o[hd:, res:]

    logits(0, 0)
    logits(1, 1)
    weigh(0)

    def step(t, _):
        s = 2 * t
        logits(jnp.minimum(s + 2, seq - 1), 0)
        weigh(1)
        values(s, 0)
        logits(jnp.minimum(s + 3, seq - 1), 1)
        weigh(0)
        values(s + 1, 1)
        return 0
    lax.fori_loop(0, seq // 2, step, 0)


def row_finish(m_ref, mask_ref, wo_ref, g_buf, att_buf, new_ref, ln_ref):
    seq, ch, res = m_ref.shape

    def step(g, total):
        y = (jax.nn.sigmoid(wide(g_buf, g).astype(F32)) * wide(att_buf, g)).astype(BF16)
        new = (wide(m_ref, g).astype(F32) + jnp.dot(wo_ref[...], y, preferred_element_type=F32)).astype(BF16)
        put(new_ref, g, new)
        ln = norm_cols(new.astype(F32))
        put(ln_ref, g, ln)
        for u in range(BLOCK):
            total += ln[:, u * res:(u + 1) * res].astype(F32) * mask_ref[pl.ds(g * BLOCK + u, 1), :]
        return total
    return lax.fori_loop(0, seq // BLOCK, step, jnp.zeros((ch, res), F32))


def col_sums(query, ln_ref, mask_ref, wkv_ref, logit_buf, val_buf):
    seq, ch, res = ln_ref.shape
    hd, heads = len(query), query[0].shape[0]
    scale = hd ** -0.5

    def first(g, top):
        kv = jnp.dot(wkv_ref[...], wide(ln_ref, g), preferred_element_type=F32).astype(BF16).astype(F32)
        for u in range(BLOCK):
            s = g * BLOCK + u
            k = kv[:hd, u * res:(u + 1) * res]
            logit = query[0] * k[0:1]
            for d in range(1, hd):
                logit += query[d] * k[d:d + 1]
            logit = logit * scale + (mask_ref[pl.ds(s, 1), :] - 1.0) * 1e4
            logit_buf[s] = logit
            val_buf[s] = kv[hd:, u * res:(u + 1) * res]
            top = jnp.maximum(top, logit)
        return top
    top = lax.fori_loop(0, seq // BLOCK, first, jnp.full((heads, res), -jnp.inf, F32))

    def second(g, carry):
        den, acc = carry
        acc = list(acc)
        for u in range(BLOCK):
            s = g * BLOCK + u
            w = jnp.exp(logit_buf[s] - top)
            den = den + w
            wb = w.astype(BF16).astype(F32)
            val = val_buf[s]
            for d in range(hd):
                acc[d] = acc[d] + wb * val[d:d + 1]
        return den, tuple(acc)
    zero = jnp.zeros((heads, res), F32)
    den, acc = lax.fori_loop(0, seq // BLOCK, second, (zero, (zero,) * hd))
    return acc, top, den


def col_finish(att, m_ref, ln_ref, mask_ref, wg_ref, wo_ref, wp_ref, out_ref, proj_ref):
    seq, ch, res = m_ref.shape

    def step(g, _):
        tiled = jnp.concatenate([att] * BLOCK, axis=1)
        gate = jnp.dot(wg_ref[...], wide(ln_ref, g), preferred_element_type=F32).astype(BF16).astype(F32)
        y = (jax.nn.sigmoid(gate) * tiled).astype(BF16)
        new = (wide(m_ref, g).astype(F32) + jnp.dot(wo_ref[...], y, preferred_element_type=F32)).astype(BF16)
        put(out_ref, g, new)
        proj = jnp.dot(wp_ref[...], norm_cols(new.astype(F32)), preferred_element_type=F32).astype(BF16)
        for u in range(BLOCK):
            s = g * BLOCK + u
            proj_ref[s] = (proj[:, u * res:(u + 1) * res].astype(F32) * mask_ref[pl.ds(s, 1), :]).astype(proj_ref.dtype)
        return 0
    lax.fori_loop(0, seq // BLOCK, step, 0)


def remote(src, dst, send_sem, recv_sem, dev):
    return pltpu.make_async_remote_copy(src_ref=src, dst_ref=dst, send_sem=send_sem, recv_sem=recv_sem,
                                        device_id={'dap': dev}, device_id_type=MESH)


def vmem():
    return pl.BlockSpec(memory_space=pltpu.VMEM)


def position(me, side):
    return me // (2 * side), (me // 2) % side, me % 2


def rows_to_block(me, side, rows_ref, block_ref, send_sem, recv_sem):
    y, x, c = position(me, side)
    half = side // 2
    slot = (x % half) * 2 + c
    core = x // half
    for t in range(side):
        dst = y * 2 * side + t * 2 + core

        @pl.when(dst != me)
        def _():
            remote(rows_ref.at[:, t], block_ref.at[slot], send_sem.at[t], recv_sem.at[slot], dst).start()

        @pl.when(dst == me)
        def _():
            block_ref[slot] = rows_ref[:, t]


def rows_to_block_wait(me, side, rows_ref, block_ref, send_sem, recv_sem):
    y, x, c = position(me, side)
    half = side // 2
    core = x // half
    for t in range(side):
        dst = y * 2 * side + t * 2 + core
        src = y * 2 * side + (c * half + t // 2) * 2 + t % 2

        @pl.when(dst != me)
        def _():
            remote(rows_ref.at[:, t], block_ref.at[t], send_sem.at[t], recv_sem.at[t], dst).wait_send()

        @pl.when(src != me)
        def _():
            remote(rows_ref.at[:, 0], block_ref.at[t], send_sem.at[t], recv_sem.at[t], dst).wait_recv()


def norm_rows(x):
    mean = jnp.mean(x, axis=-1, keepdims=True)
    cen = x - mean
    var = jnp.mean(cen * cen, axis=-1, keepdims=True)
    return (cen * lax.rsqrt(var + 1e-5)).astype(BF16)


def triangle(z_ref, bias_ref, maskb, qkvg_ref, out_w_ref, heads):
    rows, res, ch = z_ref.shape
    width = qkvg_ref.shape[0] // 4
    hd = width // heads
    lane_head = lax.broadcasted_iota(jnp.int32, (res, width), 1) // hd
    picks = [(lane_head == h).astype(F32) for h in range(heads)]
    pick_bf = jnp.concatenate(picks, axis=0).astype(BF16)
    bias = bias_ref[...].reshape(heads * res, res) + maskb
    projs = [dot_nt(norm_rows(z_ref[i]), qkvg_ref[...]) for i in range(rows)]
    raws = []
    for i in range(rows):
        q = projs[i][:, :width].astype(BF16)
        k = projs[i][:, width:2 * width].astype(BF16)
        raws.append(lax.dot_general(jnp.concatenate([q] * heads, axis=0) * pick_bf, k, (((1,), (1,)), ((), ())), preferred_element_type=F32))
    outs = []
    for i in range(rows):
        t = raws[i] * hd ** -0.5 + bias
        w = jnp.exp(t - jnp.max(t, axis=-1, keepdims=True))
        den = 1.0 / jnp.sum(w, axis=-1, keepdims=True)
        v = projs[i][:, 2 * width:3 * width].astype(BF16)
        outs.append(jnp.dot(w.astype(BF16), v, preferred_element_type=F32) * den)
    for i in range(rows):
        att = outs[i][:res] * picks[0]
        for h in range(1, heads):
            att += outs[i][h * res:(h + 1) * res] * picks[h]
        gate = projs[i][:, 3 * width:].astype(BF16).astype(F32)
        y = (jax.nn.sigmoid(gate) * att).astype(BF16)
        z_ref[i] = (z_ref[i] + jnp.dot(y, out_w_ref[...], preferred_element_type=F32)).astype(BF16).astype(F32)


def bias_rows(z_f, wb_ref, heads):
    parts = [dot_nt(wb_ref[...], norm_rows(z_f[i]))[:heads] for i in range(z_f.shape[0])]
    return jnp.concatenate(parts, axis=0).astype(BF16)


def combine_sum(got):
    return jnp.sum(got[:, 0], axis=0)


def combine_softmax(got):
    acc, top, den = got[:, 0], got[:, 1], got[:, 2]
    scale = jnp.exp(top - jnp.max(top, axis=0, keepdims=True))
    return jnp.sum(acc * scale, axis=0) / jnp.sum(den * scale, axis=0)


def block_kernel(n, side, dims, m_ref, z_ref, mask_ref, resm_ref, rb_ref, rw_ref, ro_ref, cq_ref, ckv_ref, cg_ref, co_ref, op_ref, ow_ref,
                 sb_ref, sq_ref, so_ref, eb_ref, eq_ref, eo_ref, m_out, z_out,
                 smask, q_buf, k_buf, v_buf, g_buf, att_buf, raw_buf, w_buf, den_buf, rbias, pick, rbox, rflat, wt_row, wt_col,
                 part, cut, got1, mine, back, small, logit_buf, val_buf, a_f32, a_send, c_send, zblk, opm_f32, opmw_buf, count_buf, pairs_buf,
                 a_buf, c_buf, acc, got, terms, zsend, zrows, z_f, bias, msg, inbox, flat,
                 sa, ra, sb, rb, sc1, rc1, sc2, rc2, sd1, rd1, sd2, rd2,
                 s1, r1, s2, r2, s3, r3, s4, r4, s5, r5, s6, r6, s7, r7, s8, r8):
    mh, md, heads = dims
    me = lax.axis_index('dap')
    y, x, c = position(me, side)
    half = side // 2
    seq, ch, res = m_ref.shape
    r, _, w, pc = z_ref.shape
    blk = a_buf.shape[2]
    width = mh * md
    e = op_ref.shape[0] // 2

    def dev(yy, xx, cc):
        return (yy * side + xx) * 2 + cc

    def exchange_all(box, src_of, send_sem, recv_sem):
        copies = []
        for k in range(1, n):
            dst = lax.rem(me + k, n)
            cp = remote(src_of(dst), box.at[me], send_sem.at[k], recv_sem.at[k], dst)
            cp.start()
            copies.append(cp)
        box[me] = src_of(me)[...]
        return copies

    barrier = pltpu.get_barrier_semaphore()
    for k in range(1, n):
        pl.semaphore_signal(barrier, inc=1, device_id={'dap': lax.rem(me + k, n)}, device_id_type=MESH)

    for i in range(r):
        for t in range(side):
            z_f[i, t * w:(t + 1) * w, :] = z_ref[i, t].astype(F32)
    rmsg = rbox.at[n]
    rmsg[...] = bias_rows(z_f, rb_ref, mh)
    pl.semaphore_wait(barrier, n - 1)
    gathers = exchange_all(rbox, lambda p: rmsg, sa, ra)
    rows_to_block(me, side, z_ref, zblk, sb, rb)

    smask[...] = mask_ref[pl.ds(pl.multiple_of(me * seq, seq), seq), :].astype(F32)
    wt_row[...] = ro_ref[...].astype(F32).T.astype(BF16)
    wt_col[...] = co_ref[...].astype(F32).T.astype(BF16)
    row_id = lax.broadcasted_iota(jnp.int32, (width, 2 * res), 0) // md
    lane_id = lax.broadcasted_iota(jnp.int32, (width, 2 * res), 1) // res
    for p in range(mh // 2):
        pick[p] = jnp.where(row_id == 2 * p + lane_id, 1.0, 0.0).astype(BF16)
    row_project(mh, md, m_ref, smask, rw_ref, q_buf, k_buf, v_buf, g_buf)

    for cp in gathers:
        cp.wait()
    rflat[...] = rbox[:n].astype(F32).reshape(n * r * mh, res)
    for h in range(mh):
        rbias[h // 2, :, (h % 2) * res:(h % 2 + 1) * res] = rflat[pl.ds(h, res, stride=mh), :].T * LOG2E
    row_attend(mh, md, rbias, pick, q_buf, k_buf, v_buf, att_buf, raw_buf, w_buf, den_buf)
    new_buf, ln_buf = q_buf, v_buf
    part[0] = row_finish(m_ref, smask, wt_row, g_buf, att_buf, new_buf, ln_buf)

    def all_reduce(terms_n, combine, send1, recv1, send2, recv2):
        own = res // n
        for t in range(terms_n):
            turned = part[t].T
            for p in range(n):
                cut[p, t] = turned[p * own:(p + 1) * own]
        copies = []
        for k in range(1, n):
            dst = lax.rem(me + k, n)
            cp = remote(cut.at[dst, :terms_n], got1.at[me, :terms_n], send1.at[k], recv1.at[k], dst)
            cp.start()
            copies.append(cp)
        got1[me, :terms_n] = cut[me, :terms_n]
        for cp in copies:
            cp.wait()
        total = combine(got1[...])
        slot_id = 0 if terms_n == 1 else 1
        mine[slot_id] = total
        back[slot_id, me] = total
        copies = []
        for k in range(1, n):
            cp = remote(mine.at[slot_id], back.at[slot_id, me], send2.at[k], recv2.at[k], lax.rem(me + k, n))
            cp.start()
            copies.append(cp)
        for cp in copies:
            cp.wait()
        return jnp.concatenate([back[slot_id, p] for p in range(n)], axis=0).T

    count = jnp.sum(mask_ref[...].astype(F32), axis=0, keepdims=True) + 1e-10
    qsum = all_reduce(1, combine_sum, sc1, rc1, sc2, rc2)
    small[...] = dot(cq_ref[...], (qsum / count).astype(BF16)).astype(BF16).astype(F32)
    query = [small[pl.ds(d, mh, stride=md), :] for d in range(md)]
    sums, top, den = col_sums(query, ln_buf, smask, ckv_ref, logit_buf, val_buf)
    for d in range(md):
        part[0, pl.ds(d, mh, stride=md), :] = sums[d]
        part[1, pl.ds(d, mh, stride=md), :] = top
        part[2, pl.ds(d, mh, stride=md), :] = den
    attended = all_reduce(3, combine_softmax, sd1, rd1, sd2, rd2)
    proj = att_buf
    col_finish(attended, new_buf, ln_buf, smask, cg_ref, wt_col, op_ref, m_out, proj)

    planes = proj.reshape(seq * 2 * e, res)

    def turn(t, _):
        a_f32[pl.ds(t, res, stride=e), :] = planes[pl.ds(t, seq, stride=2 * e), :].T
        other = planes[pl.ds(e + t, seq, stride=2 * e), :].T.astype(BF16)
        for b in range(side):
            c_send[b, pl.ds(pl.multiple_of(t * w, w), w), :] = other[b * w:(b + 1) * w]
        return 0
    lax.fori_loop(0, e, turn, 0)
    for b in range(side):
        a_send[b] = a_f32[b * blk:(b + 1) * blk].astype(BF16)
    rows_to_block_wait(me, side, z_ref, zblk, sb, rb)

    def count_pairs():
        step = seq

        def add(t, _):
            rows = mask_ref[pl.ds(pl.multiple_of(t * step, step), step), :].astype(F32)
            pairs_buf[...] += dot(rows.T.astype(BF16), rows.astype(BF16))
            return 0
        pairs_buf[...] = jnp.zeros_like(pairs_buf)
        lax.fori_loop(0, mask_ref.shape[0] // step, add, 0)
        size = (w // 2 * w, res)
        row = lax.broadcasted_iota(jnp.int32, size, 0)
        lane = lax.broadcasted_iota(jnp.int32, size, 1)
        pick_i = jnp.where(lane == y * w + c * (w // 2) + row // w, 1.0, 0.0).astype(BF16)
        whole = pairs_buf[...]
        high = jnp.floor(whole * (1.0 / 128.0))
        both = dot(pick_i, high.astype(BF16)) * 128.0 + dot(pick_i, (whole - high * 128.0).astype(BF16))
        one = jnp.sum(jnp.where(lane == x * w + row % w, both, 0.0), axis=1, keepdims=True)
        count_buf[...] = jnp.broadcast_to(1e-3 + one, size)
        opm_f32[...] = ow_ref[...].astype(F32)
        for f in range(e):
            rows_f = opm_f32[pl.ds(f, e, stride=e), :].astype(BF16)
            for i in range(128 // e):
                opmw_buf[(f * (128 // e) + i) * e:(f * (128 // e) + i + 1) * e, :] = rows_f

    def gather_bias(turned):
        for h in range(heads):
            plane = flat[pl.ds(h, res, stride=heads), :]
            bias[h] = plane.T if turned else plane

    def slot(buf, yy, xx, rows=None):
        rows = pl.ds(0, blk) if rows is None else rows
        return buf.at[yy, xx // 2, rows, pl.ds(pl.multiple_of((xx % 2) * seq, seq), seq)]

    order = [0, 1, side - 1] + list(range(2, side - 1))
    first = {}
    for k in [1, side - 1] + list(range(2, side - 1)):
        ty, tx = lax.rem(y + k, side), lax.rem(x + k, side)
        cp = remote(a_send.at[ty], slot(a_buf, y, x), s1.at[0, k], r1.at[0, k], dev(ty, x, c))
        cq = remote(c_send.at[tx], slot(c_buf, y, x), s1.at[1, k], r1.at[1, k], dev(y, tx, c))
        cp.start()
        cq.start()
        first[k] = (cp, cq)
    started = []
    hop = {}
    halves = [pl.ds(0, blk // 2), pl.ds(blk // 2, blk // 2)]
    xn, yn = [lax.rem(x + 1, side), lax.rem(x + side - 1, side)], [lax.rem(y + 1, side), lax.rem(y + side - 1, side)]

    def spread(k):
        sy, sx = lax.rem(y - k + side, side), lax.rem(x - k + side, side)
        for d in range(2):
            src = a_send.at[y] if k == 0 else slot(a_buf, sy, x)
            cp = remote(src, slot(a_buf, sy, x), s2.at[0, k, d], r2.at[0, k, d], dev(y, xn[d], c))
            src = c_send.at[x] if k == 0 else slot(c_buf, y, sx)
            cq = remote(src, slot(c_buf, y, sx), s2.at[1, k, d], r2.at[1, k, d], dev(yn[d], x, c))
            cp.start()
            cq.start()
            hop[k, d] = (cp, cq)

    def relay(k):
        sy, sx = lax.rem(y - k + side, side), lax.rem(x - k + side, side)
        for d in range(2):
            hop[k, d][0].wait_recv()
            fx = xn[1 - d]
            f = remote(slot(a_buf, sy, fx, halves[d]), slot(a_buf, sy, fx, halves[d]), s3.at[0, k, d], r3.at[0, k, d], dev(y, xn[d], c))
            f.start()
            hop[k, d][1].wait_recv()
            fy = yn[1 - d]
            g = remote(slot(c_buf, fy, sx, halves[d]), slot(c_buf, fy, sx, halves[d]), s3.at[1, k, d], r3.at[1, k, d], dev(yn[d], x, c))
            g.start()
            started.extend([f, g])

    lanes = pl.ds(pl.multiple_of((x % 2) * seq, seq), seq)
    for pos, k in enumerate(order):
        if k:
            first[k][0].wait_recv()
            first[k][1].wait_recv()
        spread(k)
        if pos == 0:
            a_buf[y, x // 2, :, lanes] = a_send[y]
            c_buf[y, x // 2, :, lanes] = c_send[x]
        else:
            relay(order[pos - 1])
    relay(order[-1])
    count_pairs()
    for k in order[1:]:
        first[k][0].wait_send()
        first[k][1].wait_send()
    for pair in hop.values():
        pair[0].wait_send()
        pair[1].wait_send()
    for f in started:
        f.wait()

    cols = blk // 2

    def product(base, dst):
        def chunk(t, _):
            yy, xx = t // half, t % half
            part = lax.dot_general(c_buf[yy, xx], a_buf[yy, xx, pl.ds(pl.multiple_of(base, cols), cols), :], NT, preferred_element_type=F32)

            @pl.when(t == 0)
            def _():
                dst[...] = part

            @pl.when(t > 0)
            def _():
                dst[...] += part
            return 0
        lax.fori_loop(0, side * half, chunk, 0)

    product((1 - c) * cols, acc.at[0])
    swap = remote(acc.at[0], got, s4, r4, dev(y, x, 1 - c))
    swap.start()
    product(c * cols, acc.at[1])
    swap.wait()

    per = 128 // e
    lane_i = lax.broadcasted_iota(jnp.int32, (w, 128), 1) // e
    keep = [(lane_i == i).astype(F32) for i in range(per)]

    def place(f, _):
        for g in range(cols // 128):
            rows = pl.ds(pl.multiple_of(f * w, w), w)
            both = acc[1, rows, g * 128:(g + 1) * 128] + got[rows, g * 128:(g + 1) * 128]
            for i in range(per):
                r0 = (g * per + i) * w
                terms[r0:r0 + w, pl.ds(pl.multiple_of(f * 128, 128), 128)] = (both * keep[i]).astype(BF16)
        return 0
    lax.fori_loop(0, blk // w, place, 0)
    update = dot(terms[...], opmw_buf[...]) / count_buf[...]
    fresh = (zblk[...].reshape(side * r * w, pc).astype(F32) + update).astype(BF16)
    zsend[...] = fresh.reshape(side, r, w, pc)

    my_core = x // half
    for t in range(side):
        dst = y * 2 * side + (c * half + t // 2) * 2 + t % 2

        @pl.when(dst != me)
        def _():
            remote(zsend.at[t], zrows.at[x], s5.at[t], r5.at[x], dst).start()

        @pl.when(dst == me)
        def _():
            zrows[x] = zsend[t]
    for t in range(side):
        dst = y * 2 * side + (c * half + t // 2) * 2 + t % 2
        src = y * 2 * side + t * 2 + my_core

        @pl.when(dst != me)
        def _():
            remote(zsend.at[t], zrows.at[x], s5.at[t], r5.at[x], dst).wait_send()

        @pl.when(src != me)
        def _():
            remote(zsend.at[t], zrows.at[t], s5.at[t], r5.at[t], dst).wait_recv()
    for t in range(side):
        z_f[:, t * w:(t + 1) * w, :] = zrows[t].astype(F32)

    nh = r * heads
    msg[0, 0, :nh] = bias_rows(z_f, sb_ref, heads)
    for cp in exchange_all(inbox.at[0, :, :nh], lambda p: msg.at[0, 0, :nh], s6, r6):
        cp.wait()
    flat[...] = inbox[0, :, :nh].astype(F32).reshape(n * nh, res)
    gather_bias(False)
    maskb = (resm_ref[...].astype(F32) - 1.0) * 1e4
    triangle(z_f, bias, maskb, sq_ref, so_ref, heads)

    rr = r * r

    def pack(slot_id):
        for p in range(n):
            msg[slot_id, p, :rr] = jnp.concatenate([z_f[i, p * r:(p + 1) * r, :] for i in range(r)], axis=0).astype(BF16)

    def unpack(slot_id):
        flat[...] = inbox[slot_id, :, :rr].astype(F32).reshape(n * rr, pc)
        for i in range(r):
            z_f[i] = flat[pl.ds(i, res, stride=r), :]

    pack(1)
    rows_b = bias_rows(z_f, eb_ref, heads)
    for p in range(n):
        msg[1, p, rr:] = rows_b
    for cp in exchange_all(inbox.at[1], lambda p: msg.at[1, p], s7, r7):
        cp.wait()
    flat[...] = inbox[1, :, rr:].astype(F32).reshape(n * nh, res)
    gather_bias(True)
    unpack(1)
    triangle(z_f, bias, maskb, eq_ref, eo_ref, heads)
    pack(2)
    for cp in exchange_all(inbox.at[2, :, :rr], lambda p: msg.at[2, p, :rr], s8, r8):
        cp.wait()
    unpack(2)
    z_out[...] = z_f[...].astype(BF16)


def block_call(n, side, dims, ops):
    m, z = ops[0], ops[1]
    seq, ch, res = m.shape
    r, _, w, pc = z.shape
    mh, md, heads = dims
    width, e = mh * md, ops[11].shape[0] // 2
    blk = w * e
    vm, dma = pltpu.VMEM, pltpu.SemaphoreType.DMA
    assert r == heads and res == 128 and seq == 128 and pc == 128
    own = res // n
    buf = vm((side, half_of(side), blk, 2 * seq), BF16)
    tall = vm((seq, width, res), BF16)
    box = vm((3, n, 2 * r * r, pc), BF16)
    scratch = [vm((seq, res), F32), tall, vm((seq, res, width + 16), BF16), tall, tall, vm((seq, width, res), F32),
               vm((2, mh // 2, res, 2 * res), F32), vm((2, mh // 2, res, 2 * res), BF16), vm((2, mh // 2, 8, 2 * res), F32),
               vm((mh // 2, res, 2 * res), F32), vm((mh // 2, width, 2 * res), BF16), vm((n + 1, r * mh, res), BF16), vm((n * r * mh, res), F32),
               vm((ch, width), BF16), vm((ch, width), BF16),
               vm((3, width, res), F32), vm((n, 3, own, width), F32), vm((n, 3, own, width), F32), vm((2, own, width), F32), vm((2, n, own, width), F32),
               vm((width, res), F32), vm((seq, mh, res), F32), vm((seq, md, res), F32), vm((res * e, seq), F32),
               vm((side, blk, seq), BF16), vm((side, blk, seq), BF16), vm((side, r, w, pc), BF16), vm((e * e, pc), F32), vm((e * 128, pc), BF16),
               vm((w // 2 * w, pc), F32), vm((res, res), F32),
               buf, buf, vm((2, blk, blk // 2), F32), vm((blk, blk // 2), F32), vm((w // 2 * w, e * 128), BF16),
               vm((side, r, w, pc), BF16), vm((side, r, w, pc), BF16), vm((r, res, pc), F32),
               vm((heads, res, res), F32), box, box, vm((n * r * r, pc), F32),
               dma((n,)), dma((n,)), dma((side,)), dma((side,))] + [dma((n,))] * 8 + [
               dma((2, side)), dma((2, side)), dma((2, side, 2)), dma((2, side, 2)), dma((2, side, 2)), dma((2, side, 2)),
               dma, dma, dma((side,)), dma((side,))] + [dma((n,))] * 6
    return pl.pallas_call(
        functools.partial(block_kernel, n, side, dims),
        out_shape=[jax.ShapeDtypeStruct((seq, ch, res), BF16), jax.ShapeDtypeStruct((r, res, pc), BF16)],
        in_specs=[vmem()] * len(ops), out_specs=[vmem()] * 2, scratch_shapes=scratch,
        compiler_params=pltpu.CompilerParams(collective_id=0, has_side_effects=True, vmem_limit_bytes=63 * 1024 * 1024),
        name='evoformer_block')(*ops)


def half_of(side):
    return side // 2


def solution(mesh):
    n = mesh.shape['dap']
    side = math.isqrt(n // 2)
    assert 2 * side * side == n

    def block(msa, pair, mask_full, res_mask, row_bias_w, row_qkvg_w, row_out_w, col_query_w, col_kv_w, col_gate_w, col_out_w, opm_proj_w, opm_out_w, start_bias_w, start_qkvg_w, start_out_w, end_bias_w, end_qkvg_w, end_out_w):
        r, res, pc = pair.shape
        ch = msa.shape[-1]
        last = lambda weight: jnp.moveaxis(weight, 0, -1).reshape(-1, weight.shape[0])
        first = lambda weight: weight.reshape(-1, weight.shape[-1])
        ops = [msa.transpose(0, 2, 1), pair.reshape(r, side, res // side, pc), mask_full, res_mask[None],
               row_bias_w.T, last(row_qkvg_w), first(row_out_w), last(col_query_w), last(col_kv_w), last(col_gate_w), first(col_out_w),
               last(opm_proj_w), first(opm_out_w), start_bias_w.T, last(start_qkvg_w), first(start_out_w), end_bias_w.T, last(end_qkvg_w), first(end_out_w)]
        msa_out, pair_out = block_call(n, side, col_gate_w.shape[1:] + (start_bias_w.shape[-1],), ops)
        return msa_out.transpose(0, 2, 1), pair_out

    row_spec = P(('data', 'dap'), None, None)
    in_specs = (row_spec, row_spec, P('data', None), P('data')) + (P(),) * 15
    return jax.shard_map(block, mesh=mesh, in_specs=in_specs, out_specs=(row_spec, row_spec), check_vma=False)
```

time: 460 us -> 186 us (0.40); the launches traced: 454 us -> 186 us
  Pallas kernels: 0 us -> 181 us
  waiting for transfers between devices: 130 us -> 0 us
  blocking collectives: 107 us -> 0 us
  matrix products: 105 us -> 0 us
  local copies, waits for them, and re-layouts: 47.9 us -> 3.77 us
  starting transfers between devices: 36.6 us -> 0 us
  between operations: 15 us -> 0.66 us
  other arithmetic: 12.5 us -> 0 us
    pallas_call x0 -> x1, Pallas kernels: none -> 181 us  [block_call(): pl.pallas_call(functools.partial(block_kernel, n, side, dims), out_shape=...]
    all_gather x1 -> x0, waiting for transfers between devices: 108 us -> none  [evoformer_block(): right_full = lax.all_gather(projected[1], 'dap', axis=1, tiled=True)]
    all_gather x3 -> x0, blocking collectives: 107 us -> none  [the longest x1 46.7 us: evoformer_block(): lax.all_gather(matmul_bf('ijc,ch->hji', cols_ln, end_bias_w), 'dap', axis...]
    dot_general x18 -> x0, matrix products: 67.8 us -> none  [the longest x10 33.6 us: matmul_bf(): jnp.einsum(einsum_form, left_arr, right_arr, preferred_element_type=jnp.f...]
    sub x4 -> x0, matrix products: 37.3 us -> none  [the longest x1 32.8 us: row_attention(): attn_probs = jax.nn.softmax(logits, axis=-1).astype(jnp.bfloat16)]
    all_to_all x4 -> x0, starting transfers between devices: 36.3 us -> none  [the longest x1 10.6 us: evoformer_block(): pair_out = lax.all_to_all(pair_cols, 'dap', 0, 1, tiled=True)]
    all_to_all x4 -> x0, waiting for transfers between devices: 21.6 us -> none  [the longest x1 21.6 us: evoformer_block(): value_a8 = lax.all_to_all(value_a7, 'dap', 1, 0, tiled=True)]
    convert_element_type x9 -> x0, local copies, waits for them, and re-layouts: 19.2 us -> none  [the longest x1 6.98 us: matmul_bf(): jnp.einsum(einsum_form, left_arr, right_arr, preferred_element_type=jnp.f...]
  transfers between devices with their start and end apart: 5 -> 0, of which waited for: 2 -> 0; matrix products, arithmetic and copies ran while one was open for 9% -> 0% of each run, Pallas kernels for 0% -> 0%
where the time goes in v4:
time: 186 us
  Pallas kernels  181 us (97%)
  local copies, waits for them, and re-layouts  3.77 us (2%)
    pallas_call x1, Pallas kernels, block_call(): pl.pallas_call(functools.partial(block_kernel, n, side, dims), out_shape=...  181 us
    unnamed x4, local copies, waits for them, and re-layouts  3.77 us

profile of v4, /device:TPU:97, one launch (start us, length us, event | category | flops | bytes accessed | tf_op | source)
XLA Modules:
  0.0 185.7 jit_solution(9359512019725163371)
XLA Ops:
  0.6 181.3 %evoformer_block.1 = (bf16[128,64,128]{2,1,0:T(8,128)(2,1)}, bf16[4,128,128]{2,1,0:T(8,128)(2,1)}) custom-call(bf16[128,64,128]{2,1,0:T(8,128)(2,1)} %bitcast.33, bf16[4,4,32,128]{3,2,1,0:T(8,128)(2,1)} %bitcast.36, s32[4096,128]{1,0:T(8,128)} %mask_ref.1, s32[1,128]{1,0:T(1,128)} %bitcast.51, bf16[8,128]{1,0:T(8,128)(2,1)} %bitcast.48, ...), custom_call_target="tpu_custom_call" | custom-call | tf_op jit(solution)/shard_map/evoformer_block/pallas_call | solution.py:622
  181.9 0.0 copy-start
  182.0 3.1 %copy.23 = bf16[128,128,64]{1,2,0:T(8,128)(2,1)} copy(bf16[128,128,64]{1,2,0:T(8,128)(2,1)} %bitcast.34) | data formatting | bytes 4194304
  185.1 0.0 copy-done
  185.1 0.7 copy.24
Async XLA Ops:
  181.9 3.1 %copy-start = (bf16[4,128,128]{2,1,0:T(8,128)(2,1)S(1)}, bf16[4,128,128]{2,1,0:T(8,128)(2,1)}, u32[]{:S(2)}) copy-start(bf16[4,128,128]{2,1,0:T(8,128)(2,1)} %get-tuple-element.9) | copy-start | bytes 393220

commit v5 on v4

--- a/solution.py
+++ b/solution.py
@@ -282,8 +282,9 @@
     return jnp.sum(acc * scale, axis=0) / jnp.sum(den * scale, axis=0)
 
 
-def block_kernel(n, side, dims, m_ref, z_ref, mask_ref, resm_ref, rb_ref, rw_ref, ro_ref, cq_ref, ckv_ref, cg_ref, co_ref, op_ref, ow_ref,
-                 sb_ref, sq_ref, so_ref, eb_ref, eq_ref, eo_ref, m_out, z_out,
+def block_kernel(n, side, dims, m_hbm, z_ref, mask_hbm, resm_ref, rb_ref, rw_ref, ro_ref, cq_ref, ckv_ref, cg_ref, co_ref, op_ref, ow_hbm,
+                 sb_ref, sq_hbm, so_ref, eb_ref, eq_hbm, eo_ref, m_out, z_out,
+                 m_ref, mask_ref, ow_ref, sq_ref, eq_ref, load_sem,
                  smask, q_buf, k_buf, v_buf, g_buf, att_buf, raw_buf, w_buf, den_buf, rbias, pick, rbox, rflat, wt_row, wt_col,
                  part, cut, got1, mine, back, small, logit_buf, val_buf, a_f32, a_send, c_send, zblk, opm_f32, opmw_buf, count_buf, pairs_buf,
                  a_buf, c_buf, acc, got, terms, zsend, zrows, z_f, bias, msg, inbox, flat,
@@ -315,6 +316,10 @@
     barrier = pltpu.get_barrier_semaphore()
     for k in range(1, n):
         pl.semaphore_signal(barrier, inc=1, device_id={'dap': lax.rem(me + k, n)}, device_id_type=MESH)
+    loads = [pltpu.make_async_copy(src, dst, load_sem.at[i]) for i, (src, dst) in enumerate(
+        [(m_hbm, m_ref), (mask_hbm, mask_ref), (ow_hbm, ow_ref), (sq_hbm, sq_ref), (eq_hbm, eq_ref)])]
+    for load in loads:
+        load.start()
 
     for i in range(r):
         for t in range(side):
@@ -325,6 +330,8 @@
     gathers = exchange_all(rbox, lambda p: rmsg, sa, ra)
     rows_to_block(me, side, z_ref, zblk, sb, rb)
 
+    loads[0].wait()
+    loads[1].wait()
     smask[...] = mask_ref[pl.ds(pl.multiple_of(me * seq, seq), seq), :].astype(F32)
     wt_row[...] = ro_ref[...].astype(F32).T.astype(BF16)
     wt_col[...] = co_ref[...].astype(F32).T.astype(BF16)
@@ -340,7 +347,7 @@
     for h in range(mh):
         rbias[h // 2, :, (h % 2) * res:(h % 2 + 1) * res] = rflat[pl.ds(h, res, stride=mh), :].T * LOG2E
     row_attend(mh, md, rbias, pick, q_buf, k_buf, v_buf, att_buf, raw_buf, w_buf, den_buf)
-    new_buf, ln_buf = q_buf, v_buf
+    new_buf, ln_buf, last_buf = q_buf, v_buf, g_buf
     part[0] = row_finish(m_ref, smask, wt_row, g_buf, att_buf, new_buf, ln_buf)
 
     def all_reduce(terms_n, combine, send1, recv1, send2, recv2):
@@ -382,21 +389,31 @@
         part[2, pl.ds(d, mh, stride=md), :] = den
     attended = all_reduce(3, combine_softmax, sd1, rd1, sd2, rd2)
     proj = att_buf
-    col_finish(attended, new_buf, ln_buf, smask, cg_ref, wt_col, op_ref, m_out, proj)
+    col_finish(attended, new_buf, ln_buf, smask, cg_ref, wt_col, op_ref, last_buf, proj)
+    store = pltpu.make_async_copy(last_buf, m_out, load_sem.at[len(loads)])
+    store.start()
+    for load in loads[2:]:
+        load.wait()
 
     planes = proj.reshape(seq * 2 * e, res)
 
-    def turn(t, _):
-        a_f32[pl.ds(t, res, stride=e), :] = planes[pl.ds(t, seq, stride=2 * e), :].T
-        other = planes[pl.ds(e + t, seq, stride=2 * e), :].T.astype(BF16)
-        for b in range(side):
-            c_send[b, pl.ds(pl.multiple_of(t * w, w), w), :] = other[b * w:(b + 1) * w]
+    eye = jnp.where(lax.broadcasted_iota(jnp.int32, (res, res), 0) == lax.broadcasted_iota(jnp.int32, (res, res), 1), 1.0, 0.0).astype(BF16)
+
+    def turned(t):
+        return dot_nt(eye, planes[pl.ds(t, seq, stride=2 * e), :].astype(BF16))
+
+    def turn_a(t, _):
+        for u in range(4):
+            a_f32[pl.ds(4 * t + u, res, stride=e), :] = turned(4 * t + u)
         return 0
-    lax.fori_loop(0, e, turn, 0)
-    for b in range(side):
-        a_send[b] = a_f32[b * blk:(b + 1) * blk].astype(BF16)
-    rows_to_block_wait(me, side, z_ref, zblk, sb, rb)
-
+
+    def turn_c(t, _):
+        for u in range(4):
+            f = 4 * t + u
+            other = turned(e + f).astype(BF16)
+            for b in range(side):
+                c_send[b, pl.ds(pl.multiple_of(f * w, w), w), :] = other[b * w:(b + 1) * w]
+        return 0
     def count_pairs():
         step = seq
 
@@ -426,91 +443,121 @@
             plane = flat[pl.ds(h, res, stride=heads), :]
             bias[h] = plane.T if turned else plane
 
-    def slot(buf, yy, xx, rows=None):
-        rows = pl.ds(0, blk) if rows is None else rows
-        return buf.at[yy, xx // 2, rows, pl.ds(pl.multiple_of((xx % 2) * seq, seq), seq)]
-
-    order = [0, 1, side - 1] + list(range(2, side - 1))
-    first = {}
-    for k in [1, side - 1] + list(range(2, side - 1)):
-        ty, tx = lax.rem(y + k, side), lax.rem(x + k, side)
-        cp = remote(a_send.at[ty], slot(a_buf, y, x), s1.at[0, k], r1.at[0, k], dev(ty, x, c))
-        cq = remote(c_send.at[tx], slot(c_buf, y, x), s1.at[1, k], r1.at[1, k], dev(y, tx, c))
-        cp.start()
-        cq.start()
-        first[k] = (cp, cq)
-    started = []
-    hop = {}
+    places = {0: (0, 0), 1: (0, 1), side - 1: (1, 0), 2: (1, 1)}
+
+    def slot(buf, k, l, rows=None):
+        pair_id, part_id = places[l]
+        return buf.at[k, pair_id, pl.ds(0, blk) if rows is None else rows, pl.ds(part_id * seq, seq)]
+
+    order = [0, 1, side - 1, 2]
+    assert side == len(order)
+    xn, yn = [lax.rem(x + 1, side), lax.rem(x + side - 1, side)], [lax.rem(y + 1, side), lax.rem(y + side - 1, side)]
+    back_by = [1, side - 1]
     halves = [pl.ds(0, blk // 2), pl.ds(blk // 2, blk // 2)]
-    xn, yn = [lax.rem(x + 1, side), lax.rem(x + side - 1, side)], [lax.rem(y + 1, side), lax.rem(y + side - 1, side)]
-
-    def spread(k):
-        sy, sx = lax.rem(y - k + side, side), lax.rem(x - k + side, side)
+    first, hop, passed = [{}, {}], {}, {}
+
+    def send_first(which):
+        for k in order[1:]:
+            ty, tx = lax.rem(y + k, side), lax.rem(x + k, side)
+            if which == 0:
+                cp = remote(a_send.at[ty], slot(a_buf, k, 0), s1.at[0, k], r1.at[0, k], dev(ty, x, c))
+            else:
+                cp = remote(c_send.at[tx], slot(c_buf, 0, k), s1.at[1, k], r1.at[1, k], dev(y, tx, c))
+            cp.start()
+            first[which][k] = cp
+
+    def spread(which, k):
         for d in range(2):
-            src = a_send.at[y] if k == 0 else slot(a_buf, sy, x)
-            cp = remote(src, slot(a_buf, sy, x), s2.at[0, k, d], r2.at[0, k, d], dev(y, xn[d], c))
-            src = c_send.at[x] if k == 0 else slot(c_buf, y, sx)
-            cq = remote(src, slot(c_buf, y, sx), s2.at[1, k, d], r2.at[1, k, d], dev(yn[d], x, c))
+            if which == 0:
+                cp = remote(a_send.at[y] if k == 0 else slot(a_buf, k, 0), slot(a_buf, k, back_by[d]), s2.at[0, k, d], r2.at[0, k, d], dev(y, xn[d], c))
+            else:
+                cp = remote(c_send.at[x] if k == 0 else slot(c_buf, 0, k), slot(c_buf, back_by[d], k), s2.at[1, k, d], r2.at[1, k, d], dev(yn[d], x, c))
             cp.start()
-            cq.start()
-            hop[k, d] = (cp, cq)
+            hop[which, k, d] = cp
 
     def relay(k):
-        sy, sx = lax.rem(y - k + side, side), lax.rem(x - k + side, side)
         for d in range(2):
-            hop[k, d][0].wait_recv()
-            fx = xn[1 - d]
-            f = remote(slot(a_buf, sy, fx, halves[d]), slot(a_buf, sy, fx, halves[d]), s3.at[0, k, d], r3.at[0, k, d], dev(y, xn[d], c))
+            hop[0, k, d].wait_recv()
+            f = remote(slot(a_buf, k, back_by[d], halves[d]), slot(a_buf, k, 2, halves[d]), s3.at[0, k, d], r3.at[0, k, d], dev(y, xn[d], c))
             f.start()
-            hop[k, d][1].wait_recv()
-            fy = yn[1 - d]
-            g = remote(slot(c_buf, fy, sx, halves[d]), slot(c_buf, fy, sx, halves[d]), s3.at[1, k, d], r3.at[1, k, d], dev(yn[d], x, c))
+            hop[1, k, d].wait_recv()
+            g = remote(slot(c_buf, back_by[d], k, halves[d]), slot(c_buf, 2, k, halves[d]), s3.at[1, k, d], r3.at[1, k, d], dev(yn[d], x, c))
             g.start()
-            started.extend([f, g])
-
-    lanes = pl.ds(pl.multiple_of((x % 2) * seq, seq), seq)
-    for pos, k in enumerate(order):
-        if k:
-            first[k][0].wait_recv()
-            first[k][1].wait_recv()
-        spread(k)
-        if pos == 0:
-            a_buf[y, x // 2, :, lanes] = a_send[y]
-            c_buf[y, x // 2, :, lanes] = c_send[x]
+            passed[k, d] = (f, g)
+
+    def wait_passed(k):
+        for d in range(2):
+            for f in passed[k, d]:
+                f.wait_recv()
+
+    cols = blk // 2
+
+    def product(chunk, dst_id, fresh=False):
+        k, p = chunk
+        base = jnp.where(dst_id == 0, 1 - c, c) * cols
+        part_sum = dot_nt(c_buf[k, p], a_buf[k, p, pl.ds(pl.multiple_of(base, cols), cols), :])
+        if fresh:
+            acc[dst_id] = part_sum
         else:
-            relay(order[pos - 1])
-    relay(order[-1])
+            acc[dst_id] += part_sum
+
+    def products(chunk, fresh=False):
+        product(chunk, 0, fresh)
+        product(chunk, 1, fresh)
+
+    lax.fori_loop(0, e // 4, turn_a, 0)
+    for b in range(side):
+        a_send[b] = a_f32[b * blk:(b + 1) * blk].astype(BF16)
+    send_first(0)
+    spread(0, 0)
+    lax.fori_loop(0, e // 4, turn_c, 0)
+    send_first(1)
+    spread(1, 0)
+    a_buf[0, 0, :, :seq] = a_send[y]
+    c_buf[0, 0, :, :seq] = c_send[x]
+    rows_to_block_wait(me, side, z_ref, zblk, sb, rb)
     count_pairs()
-    for k in order[1:]:
-        first[k][0].wait_send()
-        first[k][1].wait_send()
-    for pair in hop.values():
-        pair[0].wait_send()
-        pair[1].wait_send()
-    for f in started:
-        f.wait()
-
-    cols = blk // 2
-
-    def product(base, dst):
-        def chunk(t, _):
-            yy, xx = t // half, t % half
-            part = lax.dot_general(c_buf[yy, xx], a_buf[yy, xx, pl.ds(pl.multiple_of(base, cols), cols), :], NT, preferred_element_type=F32)
-
-            @pl.when(t == 0)
-            def _():
-                dst[...] = part
-
-            @pl.when(t > 0)
-            def _():
-                dst[...] += part
-            return 0
-        lax.fori_loop(0, side * half, chunk, 0)
-
-    product((1 - c) * cols, acc.at[0])
+    one, three, two = order[1:]
+    first[0][one].wait_recv()
+    first[1][one].wait_recv()
+    spread(0, one)
+    spread(1, one)
+    relay(0)
+    first[0][three].wait_recv()
+    first[1][three].wait_recv()
+    spread(0, three)
+    spread(1, three)
+    relay(one)
+    products((0, 0), True)
+    first[0][two].wait_recv()
+    first[1][two].wait_recv()
+    spread(0, two)
+    spread(1, two)
+    products((one, 0))
+    relay(three)
+    products((three, 0))
+    wait_passed(0)
+    products((0, 1))
+    relay(two)
+    wait_passed(one)
+    products((two, 0))
+    rest = [(one, 1), (three, 1), (two, 1)]
+    wait_passed(three)
+    wait_passed(two)
+    for chunk in rest:
+        product(chunk, 0)
     swap = remote(acc.at[0], got, s4, r4, dev(y, x, 1 - c))
     swap.start()
-    product(c * cols, acc.at[1])
+    for chunk in rest:
+        product(chunk, 1)
+    for k in order[1:]:
+        first[0][k].wait_send()
+        first[1][k].wait_send()
+    for cp in hop.values():
+        cp.wait_send()
+    for pair in passed.values():
+        for f in pair:
+            f.wait_send()
     swap.wait()
 
     per = 128 // e
@@ -590,6 +637,7 @@
         cp.wait()
     unpack(2)
     z_out[...] = z_f[...].astype(BF16)
+    store.wait()
 
 
 def block_call(n, side, dims, ops):
@@ -605,7 +653,9 @@
     buf = vm((side, half_of(side), blk, 2 * seq), BF16)
     tall = vm((seq, width, res), BF16)
     box = vm((3, n, 2 * r * r, pc), BF16)
-    scratch = [vm((seq, res), F32), tall, vm((seq, res, width + 16), BF16), tall, tall, vm((seq, width, res), F32),
+    large = [0, 2, 12, 14, 17]
+    scratch = [vm(ops[i].shape, ops[i].dtype) for i in large] + [dma((len(large) + 1,))]
+    scratch += [vm((seq, res), F32), tall, vm((seq, res, width + 16), BF16), tall, tall, vm((seq, width, res), F32),
                vm((2, mh // 2, res, 2 * res), F32), vm((2, mh // 2, res, 2 * res), BF16), vm((2, mh // 2, 8, 2 * res), F32),
                vm((mh // 2, res, 2 * res), F32), vm((mh // 2, width, 2 * res), BF16), vm((n + 1, r * mh, res), BF16), vm((n * r * mh, res), F32),
                vm((ch, width), BF16), vm((ch, width), BF16),
@@ -622,7 +672,8 @@
     return pl.pallas_call(
         functools.partial(block_kernel, n, side, dims),
         out_shape=[jax.ShapeDtypeStruct((seq, ch, res), BF16), jax.ShapeDtypeStruct((r, res, pc), BF16)],
-        in_specs=[vmem()] * len(ops), out_specs=[vmem()] * 2, scratch_shapes=scratch,
+        in_specs=[pl.BlockSpec(memory_space=pl.ANY) if i in large else vmem() for i in range(len(ops))],
+        out_specs=[pl.BlockSpec(memory_space=pl.ANY), vmem()], scratch_shapes=scratch,
         compiler_params=pltpu.CompilerParams(collective_id=0, has_side_effects=True, vmem_limit_bytes=63 * 1024 * 1024),
         name='evoformer_block')(*ops)
 

time: 186 us -> 171 us (0.919)
  Pallas kernels: 181 us -> 166 us
    pallas_call x1, Pallas kernels: 181 us -> 166 us  [block_call(): pl.pallas_call(functools.partial(block_kernel, n, side, dims), out_shape=...]
where the time goes in v5:
time: 171 us
  Pallas kernels  166 us (97%)
  local copies, waits for them, and re-layouts  3.77 us (2%)
    pallas_call x1, Pallas kernels, block_call(): pl.pallas_call(functools.partial(block_kernel, n, side, dims), out_shape=...  166 us
    unnamed x4, local copies, waits for them, and re-layouts  3.77 us

profile of v5, /device:TPU:97, one launch (start us, length us, event | category | flops | bytes accessed | tf_op | source)
XLA Modules:
  0.0 170.7 jit_solution(3824862760640306585)
XLA Ops:
  0.6 166.3 %evoformer_block.1 = (bf16[128,64,128]{2,1,0:T(8,128)(2,1)}, bf16[4,128,128]{2,1,0:T(8,128)(2,1)}) custom-call(bf16[128,64,128]{2,1,0:T(8,128)(2,1)} %bitcast.33, bf16[4,4,32,128]{3,2,1,0:T(8,128)(2,1)} %bitcast.36, s32[4096,128]{1,0:T(8,128)} %mask_hbm.1, s32[1,128]{1,0:T(1,128)} %bitcast.51, bf16[8,128]{1,0:T(8,128)(2,1)} %bitcast.48, ...), custom_call_target="tpu_custom_call" | custom-call | tf_op jit(solution)/shard_map/evoformer_block/pallas_call | solution.py:672
  166.9 0.0 copy-start
  166.9 3.1 %copy.23 = bf16[128,128,64]{1,2,0:T(8,128)(2,1)} copy(bf16[128,128,64]{1,2,0:T(8,128)(2,1)} %bitcast.34) | data formatting | bytes 4194304
  170.0 0.0 copy-done
  170.0 0.7 copy.24
Async XLA Ops:
  166.9 3.1 %copy-start = (bf16[4,128,128]{2,1,0:T(8,128)(2,1)S(1)}, bf16[4,128,128]{2,1,0:T(8,128)(2,1)}, u32[]{:S(2)}) copy-start(bf16[4,128,128]{2,1,0:T(8,128)(2,1)} %get-tuple-element.9) | copy-start | bytes 393220

commit v6 on v5

--- a/solution.py
+++ b/solution.py
@@ -77,41 +77,38 @@
     row = lax.broadcasted_iota(jnp.int32, (16, 2 * res), 0)
     ones = jnp.where(row < 3, 1.0, 0.0).astype(BF16)
 
-    def logits(s, b):
+    def logits(s, b, p):
         qt = q_buf[s]
         q2 = jnp.concatenate([qt, qt], axis=1)
-        keys = k_buf[s]
-        for p in range(pairs):
-            raw_buf[b, p] = jnp.dot(keys, jnp.concatenate([q2 * pick_ref[p], ones], axis=0), preferred_element_type=F32)
-
-    def weigh(b):
-        for p in range(pairs):
-            t = raw_buf[b, p] * scale + bias_ref[p]
-            w = jnp.exp2(t - jnp.max(t, axis=0, keepdims=True))
-            w_buf[b, p] = w.astype(BF16)
-            den_buf[b, p] = jnp.broadcast_to(1.0 / jnp.sum(w, axis=0, keepdims=True), (8, 2 * res))
-
-    def values(s, b):
-        for p in range(pairs):
-            lo = 2 * p * hd
-            o = jnp.dot(v_buf[s, lo:lo + 2 * hd], w_buf[b, p], preferred_element_type=F32) * den_buf[b, p, 0:1]
-            att_buf[s, lo:lo + hd] = o[:hd, :res]
-            att_buf[s, lo + hd:lo + 2 * hd] = o[hd:, res:]
-
-    logits(0, 0)
-    logits(1, 1)
-    weigh(0)
+        raw_buf[b, p] = jnp.dot(k_buf[s], jnp.concatenate([q2 * pick_ref[p], ones], axis=0), preferred_element_type=F32)
+
+    def weigh(b, p):
+        t = raw_buf[b, p] * scale + bias_ref[p]
+        w = jnp.exp2(t - jnp.max(t, axis=0, keepdims=True))
+        w_buf[b, p] = w.astype(BF16)
+        den_buf[b, p] = jnp.broadcast_to(1.0 / jnp.sum(w, axis=0, keepdims=True), (8, 2 * res))
+
+    def values(s, b, p):
+        lo = 2 * p * hd
+        o = jnp.dot(v_buf[s, lo:lo + 2 * hd], w_buf[b, p], preferred_element_type=F32) * den_buf[b, p, 0:1]
+        att_buf[s, lo:lo + hd] = o[:hd, :res]
+        att_buf[s, lo + hd:lo + 2 * hd] = o[hd:, res:]
+
+    for p in range(pairs):
+        logits(0, 0, p)
+    for p in range(pairs):
+        logits(1, 1, p)
+        weigh(0, p)
 
     def step(t, _):
-        s = 2 * t
-        logits(jnp.minimum(s + 2, seq - 1), 0)
-        weigh(1)
-        values(s, 0)
-        logits(jnp.minimum(s + 3, seq - 1), 1)
-        weigh(0)
-        values(s + 1, 1)
+        for u in range(4):
+            s = 4 * t + u
+            for p in range(pairs):
+                logits(jnp.minimum(s + 2, seq - 1), u % 2, p)
+                weigh((u + 1) % 2, p)
+                values(s, u % 2, p)
         return 0
-    lax.fori_loop(0, seq // 2, step, 0)
+    lax.fori_loop(0, seq // 4, step, 0)
 
 
 def row_finish(m_ref, mask_ref, wo_ref, g_buf, att_buf, new_ref, ln_ref):
@@ -129,22 +126,42 @@
     return lax.fori_loop(0, seq // BLOCK, step, jnp.zeros((ch, res), F32))
 
 
-def col_sums(query, ln_ref, mask_ref, wkv_ref, logit_buf, val_buf):
+def col_project(ln_ref, wkv_ref, key_buf, val_buf):
     seq, ch, res = ln_ref.shape
-    hd, heads = len(query), query[0].shape[0]
+    hd = key_buf.shape[1]
+
+    def step(g, _):
+        kv = jnp.dot(wkv_ref[...], wide(ln_ref, g), preferred_element_type=F32).astype(BF16).astype(F32)
+        put(key_buf, g, kv[:hd])
+        put(val_buf, g, kv[hd:])
+        return 0
+    lax.fori_loop(0, seq // BLOCK, step, 0)
+
+
+def col_gates(ln_ref, wg_ref, gate_buf):
+    seq, ch, res = ln_ref.shape
+
+    def step(g, _):
+        gate = jnp.dot(wg_ref[...], wide(ln_ref, g), preferred_element_type=F32).astype(BF16).astype(F32)
+        put(gate_buf, g, jax.nn.sigmoid(gate))
+        return 0
+    lax.fori_loop(0, seq // BLOCK, step, 0)
+
+
+def col_sums(query, mask_ref, key_buf, val_buf):
+    seq, hd, res = val_buf.shape
+    heads = query[0].shape[0]
     scale = hd ** -0.5
 
     def first(g, top):
-        kv = jnp.dot(wkv_ref[...], wide(ln_ref, g), preferred_element_type=F32).astype(BF16).astype(F32)
         for u in range(BLOCK):
             s = g * BLOCK + u
-            k = kv[:hd, u * res:(u + 1) * res]
+            k = key_buf[s]
             logit = query[0] * k[0:1]
             for d in range(1, hd):
                 logit += query[d] * k[d:d + 1]
             logit = logit * scale + (mask_ref[pl.ds(s, 1), :] - 1.0) * 1e4
-            logit_buf[s] = logit
-            val_buf[s] = kv[hd:, u * res:(u + 1) * res]
+            key_buf[s] = logit
             top = jnp.maximum(top, logit)
         return top
     top = lax.fori_loop(0, seq // BLOCK, first, jnp.full((heads, res), -jnp.inf, F32))
@@ -154,7 +171,7 @@
         acc = list(acc)
         for u in range(BLOCK):
             s = g * BLOCK + u
-            w = jnp.exp(logit_buf[s] - top)
+            w = jnp.exp(key_buf[s] - top)
             den = den + w
             wb = w.astype(BF16).astype(F32)
             val = val_buf[s]
@@ -166,13 +183,12 @@
     return acc, top, den
 
 
-def col_finish(att, m_ref, ln_ref, mask_ref, wg_ref, wo_ref, wp_ref, out_ref, proj_ref):
+def col_finish(att, m_ref, mask_ref, wo_ref, wp_ref, out_ref, proj_ref):
     seq, ch, res = m_ref.shape
 
     def step(g, _):
         tiled = jnp.concatenate([att] * BLOCK, axis=1)
-        gate = jnp.dot(wg_ref[...], wide(ln_ref, g), preferred_element_type=F32).astype(BF16).astype(F32)
-        y = (jax.nn.sigmoid(gate) * tiled).astype(BF16)
+        y = (wide(proj_ref, g) * tiled).astype(BF16)
         new = (wide(m_ref, g).astype(F32) + jnp.dot(wo_ref[...], y, preferred_element_type=F32)).astype(BF16)
         put(out_ref, g, new)
         proj = jnp.dot(wp_ref[...], norm_cols(new.astype(F32)), preferred_element_type=F32).astype(BF16)
@@ -350,7 +366,7 @@
     new_buf, ln_buf, last_buf = q_buf, v_buf, g_buf
     part[0] = row_finish(m_ref, smask, wt_row, g_buf, att_buf, new_buf, ln_buf)
 
-    def all_reduce(terms_n, combine, send1, recv1, send2, recv2):
+    def all_reduce(terms_n, combine, send1, recv1, send2, recv2, beside1, beside2):
         own = res // n
         for t in range(terms_n):
             turned = part[t].T
@@ -363,6 +379,7 @@
             cp.start()
             copies.append(cp)
         got1[me, :terms_n] = cut[me, :terms_n]
+        beside1()
         for cp in copies:
             cp.wait()
         total = combine(got1[...])
@@ -374,46 +391,11 @@
             cp = remote(mine.at[slot_id], back.at[slot_id, me], send2.at[k], recv2.at[k], lax.rem(me + k, n))
             cp.start()
             copies.append(cp)
+        beside2()
         for cp in copies:
             cp.wait()
         return jnp.concatenate([back[slot_id, p] for p in range(n)], axis=0).T
 
-    count = jnp.sum(mask_ref[...].astype(F32), axis=0, keepdims=True) + 1e-10
-    qsum = all_reduce(1, combine_sum, sc1, rc1, sc2, rc2)
-    small[...] = dot(cq_ref[...], (qsum / count).astype(BF16)).astype(BF16).astype(F32)
-    query = [small[pl.ds(d, mh, stride=md), :] for d in range(md)]
-    sums, top, den = col_sums(query, ln_buf, smask, ckv_ref, logit_buf, val_buf)
-    for d in range(md):
-        part[0, pl.ds(d, mh, stride=md), :] = sums[d]
-        part[1, pl.ds(d, mh, stride=md), :] = top
-        part[2, pl.ds(d, mh, stride=md), :] = den
-    attended = all_reduce(3, combine_softmax, sd1, rd1, sd2, rd2)
-    proj = att_buf
-    col_finish(attended, new_buf, ln_buf, smask, cg_ref, wt_col, op_ref, last_buf, proj)
-    store = pltpu.make_async_copy(last_buf, m_out, load_sem.at[len(loads)])
-    store.start()
-    for load in loads[2:]:
-        load.wait()
-
-    planes = proj.reshape(seq * 2 * e, res)
-
-    eye = jnp.where(lax.broadcasted_iota(jnp.int32, (res, res), 0) == lax.broadcasted_iota(jnp.int32, (res, res), 1), 1.0, 0.0).astype(BF16)
-
-    def turned(t):
-        return dot_nt(eye, planes[pl.ds(t, seq, stride=2 * e), :].astype(BF16))
-
-    def turn_a(t, _):
-        for u in range(4):
-            a_f32[pl.ds(4 * t + u, res, stride=e), :] = turned(4 * t + u)
-        return 0
-
-    def turn_c(t, _):
-        for u in range(4):
-            f = 4 * t + u
-            other = turned(e + f).astype(BF16)
-            for b in range(side):
-                c_send[b, pl.ds(pl.multiple_of(f * w, w), w), :] = other[b * w:(b + 1) * w]
-        return 0
     def count_pairs():
         step = seq
 
@@ -438,6 +420,47 @@
             for i in range(128 // e):
                 opmw_buf[(f * (128 // e) + i) * e:(f * (128 // e) + i + 1) * e, :] = rows_f
 
+    for load in loads[2:]:
+        load.wait()
+    proj = att_buf
+    count = []
+
+    def project():
+        count.append(jnp.sum(mask_ref[...].astype(F32), axis=0, keepdims=True) + 1e-10)
+        col_project(ln_buf, ckv_ref, logit_buf, val_buf)
+
+    qsum = all_reduce(1, combine_sum, sc1, rc1, sc2, rc2, project, lambda: col_gates(ln_buf, cg_ref, proj))
+    small[...] = dot(cq_ref[...], (qsum / count[0]).astype(BF16)).astype(BF16).astype(F32)
+    query = [small[pl.ds(d, mh, stride=md), :] for d in range(md)]
+    sums, top, den = col_sums(query, smask, logit_buf, val_buf)
+    for d in range(md):
+        part[0, pl.ds(d, mh, stride=md), :] = sums[d]
+        part[1, pl.ds(d, mh, stride=md), :] = top
+        part[2, pl.ds(d, mh, stride=md), :] = den
+    attended = all_reduce(3, combine_softmax, sd1, rd1, sd2, rd2, count_pairs, lambda: None)
+    col_finish(attended, new_buf, smask, wt_col, op_ref, last_buf, proj)
+    store = pltpu.make_async_copy(last_buf, m_out, load_sem.at[len(loads)])
+    store.start()
+
+    planes = proj.reshape(seq * 2 * e, res)
+
+    eye = jnp.where(lax.broadcasted_iota(jnp.int32, (res, res), 0) == lax.broadcasted_iota(jnp.int32, (res, res), 1), 1.0, 0.0).astype(BF16)
+
+    def turned(t):
+        return dot_nt(eye, planes[pl.ds(t, seq, stride=2 * e), :].astype(BF16))
+
+    def turn_a(t, _):
+        for u in range(4):
+            a_f32[pl.ds(4 * t + u, res, stride=e), :] = turned(4 * t + u)
+        return 0
+
+    def turn_c(t, _):
+        for u in range(4):
+            f = 4 * t + u
+            other = turned(e + f).astype(BF16)
+            for b in range(side):
+                c_send[b, pl.ds(pl.multiple_of(f * w, w), w), :] = other[b * w:(b + 1) * w]
+        return 0
     def gather_bias(turned):
         for h in range(heads):
             plane = flat[pl.ds(h, res, stride=heads), :]
@@ -516,7 +539,6 @@
     a_buf[0, 0, :, :seq] = a_send[y]
     c_buf[0, 0, :, :seq] = c_send[x]
     rows_to_block_wait(me, side, z_ref, zblk, sb, rb)
-    count_pairs()
     one, three, two = order[1:]
     first[0][one].wait_recv()
     first[1][one].wait_recv()
@@ -577,6 +599,11 @@
     fresh = (zblk[...].reshape(side * r * w, pc).astype(F32) + update).astype(BF16)
     zsend[...] = fresh.reshape(side, r, w, pc)
 
+    nh = r * heads
+    groups = (w // 2) * w // 128
+    part_bias = dot_nt(sb_ref[...], norm_rows(fresh.astype(F32)))[:heads]
+    msg[0, 0, :nh] = jnp.concatenate([part_bias[:, g * 128:(g + 1) * 128] for g in range(groups)], axis=0).astype(BF16)
+    gathers = exchange_all(inbox.at[0, :, :nh], lambda p: msg.at[0, 0, :nh], s6, r6)
     my_core = x // half
     for t in range(side):
         dst = y * 2 * side + (c * half + t // 2) * 2 + t % 2
@@ -602,12 +629,15 @@
     for t in range(side):
         z_f[:, t * w:(t + 1) * w, :] = zrows[t].astype(F32)
 
-    nh = r * heads
-    msg[0, 0, :nh] = bias_rows(z_f, sb_ref, heads)
-    for cp in exchange_all(inbox.at[0, :, :nh], lambda p: msg.at[0, 0, :nh], s6, r6):
+    for cp in gathers:
         cp.wait()
     flat[...] = inbox[0, :, :nh].astype(F32).reshape(n * nh, res)
-    gather_bias(False)
+    per_y = 2 * groups
+    for yy in range(side):
+        for h in range(heads):
+            pieces = [flat[pl.ds((yy * side + xx) * per_y * heads + h, per_y, stride=heads), :] for xx in range(side)]
+            for i in range(128 // w):
+                bias[h, pl.ds(yy * w + i, per_y, stride=128 // w), :] = jnp.concatenate([piece[:, i * w:(i + 1) * w] for piece in pieces], axis=1)
     maskb = (resm_ref[...].astype(F32) - 1.0) * 1e4
     triangle(z_f, bias, maskb, sq_ref, so_ref, heads)
 
@@ -648,7 +678,7 @@
     width, e = mh * md, ops[11].shape[0] // 2
     blk = w * e
     vm, dma = pltpu.VMEM, pltpu.SemaphoreType.DMA
-    assert r == heads and res == 128 and seq == 128 and pc == 128
+    assert r == heads and mh == md and res == 128 and seq == 128 and pc == 128
     own = res // n
     buf = vm((side, half_of(side), blk, 2 * seq), BF16)
     tall = vm((seq, width, res), BF16)

time: 171 us -> 163 us (0.953)
  Pallas kernels: 166 us -> 159 us
    pallas_call x1, Pallas kernels: 166 us -> 159 us  [block_call(): pl.pallas_call(functools.partial(block_kernel, n, side, dims), out_shape=...]
where the time goes in v6:
time: 163 us
  Pallas kernels  159 us (98%)
  local copies, waits for them, and re-layouts  3.77 us (2%)
    pallas_call x1, Pallas kernels, block_call(): pl.pallas_call(functools.partial(block_kernel, n, side, dims), out_shape=...  159 us
    unnamed x4, local copies, waits for them, and re-layouts  3.77 us

profile of v6, /device:TPU:97, one launch (start us, length us, event | category | flops | bytes accessed | tf_op | source)
XLA Modules:
  0.0 163.1 jit_solution(5217274291617260210)
XLA Ops:
  0.6 158.7 %evoformer_block.1 = (bf16[128,64,128]{2,1,0:T(8,128)(2,1)}, bf16[4,128,128]{2,1,0:T(8,128)(2,1)}) custom-call(bf16[128,64,128]{2,1,0:T(8,128)(2,1)} %bitcast.33, bf16[4,4,32,128]{3,2,1,0:T(8,128)(2,1)} %bitcast.36, s32[4096,128]{1,0:T(8,128)} %mask_hbm.1, s32[1,128]{1,0:T(1,128)} %bitcast.51, bf16[8,128]{1,0:T(8,128)(2,1)} %bitcast.48, ...), custom_call_target="tpu_custom_call" | custom-call | tf_op jit(solution)/shard_map/evoformer_block/pallas_call | solution.py:702
  159.3 0.0 copy-start
  159.4 3.1 %copy.23 = bf16[128,128,64]{1,2,0:T(8,128)(2,1)} copy(bf16[128,128,64]{1,2,0:T(8,128)(2,1)} %bitcast.34) | data formatting | bytes 4194304
  162.5 0.0 copy-done
  162.5 0.7 copy.24
Async XLA Ops:
  159.3 3.1 %copy-start = (bf16[4,128,128]{2,1,0:T(8,128)(2,1)S(1)}, bf16[4,128,128]{2,1,0:T(8,128)(2,1)}, u32[]{:S(2)}) copy-start(bf16[4,128,128]{2,1,0:T(8,128)(2,1)} %get-tuple-element.9) | copy-start | bytes 393220

commit v7 on v6

--- a/solution.py
+++ b/solution.py
@@ -67,7 +67,7 @@
             extra = jnp.where(row == 0, terms[0], jnp.where(row == 1, terms[1], jnp.where(row == 2, terms[2], 0.0))) * off
             k_buf[s] = jnp.concatenate([proj[width:2 * width, u * res:(u + 1) * res], extra], axis=0).T.astype(BF16)
         return 0
-    lax.fori_loop(0, seq // BLOCK, step, 0)
+    lax.fori_loop(0, seq // BLOCK, step, 0, unroll=2)
 
 
 def row_attend(heads, hd, bias_ref, pick_ref, q_buf, k_buf, v_buf, att_buf, raw_buf, w_buf, den_buf):
@@ -123,7 +123,7 @@
         for u in range(BLOCK):
             total += ln[:, u * res:(u + 1) * res].astype(F32) * mask_ref[pl.ds(g * BLOCK + u, 1), :]
         return total
-    return lax.fori_loop(0, seq // BLOCK, step, jnp.zeros((ch, res), F32))
+    return lax.fori_loop(0, seq // BLOCK, step, jnp.zeros((ch, res), F32), unroll=2)
 
 
 def col_project(ln_ref, wkv_ref, key_buf, val_buf):
@@ -135,7 +135,7 @@
         put(key_buf, g, kv[:hd])
         put(val_buf, g, kv[hd:])
         return 0
-    lax.fori_loop(0, seq // BLOCK, step, 0)
+    lax.fori_loop(0, seq // BLOCK, step, 0, unroll=2)
 
 
 def col_gates(ln_ref, wg_ref, gate_buf):
@@ -145,7 +145,7 @@
         gate = jnp.dot(wg_ref[...], wide(ln_ref, g), preferred_element_type=F32).astype(BF16).astype(F32)
         put(gate_buf, g, jax.nn.sigmoid(gate))
         return 0
-    lax.fori_loop(0, seq // BLOCK, step, 0)
+    lax.fori_loop(0, seq // BLOCK, step, 0, unroll=2)
 
 
 def col_sums(query, mask_ref, key_buf, val_buf):
@@ -196,7 +196,7 @@
             s = g * BLOCK + u
             proj_ref[s] = (proj[:, u * res:(u + 1) * res].astype(F32) * mask_ref[pl.ds(s, 1), :]).astype(proj_ref.dtype)
         return 0
-    lax.fori_loop(0, seq // BLOCK, step, 0)
+    lax.fori_loop(0, seq // BLOCK, step, 0, unroll=2)
 
 
 def remote(src, dst, send_sem, recv_sem, dev):
@@ -298,14 +298,15 @@
     return jnp.sum(acc * scale, axis=0) / jnp.sum(den * scale, axis=0)
 
 
-def block_kernel(n, side, dims, m_hbm, z_ref, mask_hbm, resm_ref, rb_ref, rw_ref, ro_ref, cq_ref, ckv_ref, cg_ref, co_ref, op_ref, ow_hbm,
-                 sb_ref, sq_hbm, so_ref, eb_ref, eq_hbm, eo_ref, m_out, z_out,
-                 m_ref, mask_ref, ow_ref, sq_ref, eq_ref, load_sem,
+def block_kernel(n, side, dims, n_ops, *refs):
+    operands, (m_out, z_out), loaded, load_sem, rest = refs[:n_ops], refs[n_ops:n_ops + 2], refs[n_ops + 2:2 * n_ops + 2], refs[2 * n_ops + 2], refs[2 * n_ops + 3:]
+    m_ref, z_ref, mask_ref, resm_ref, rb_ref, rw_ref, ro_ref, cq_ref, ckv_ref, cg_ref, co_ref, op_ref, ow_ref, sb_ref, sq_ref, so_ref, eb_ref, eq_ref, eo_ref = loaded
+    (
                  smask, q_buf, k_buf, v_buf, g_buf, att_buf, raw_buf, w_buf, den_buf, rbias, pick, rbox, rflat, wt_row, wt_col,
                  part, cut, got1, mine, back, small, logit_buf, val_buf, a_f32, a_send, c_send, zblk, opm_f32, opmw_buf, count_buf, pairs_buf,
                  a_buf, c_buf, acc, got, terms, zsend, zrows, z_f, bias, msg, inbox, flat,
                  sa, ra, sb, rb, sc1, rc1, sc2, rc2, sd1, rd1, sd2, rd2,
-                 s1, r1, s2, r2, s3, r3, s4, r4, s5, r5, s6, r6, s7, r7, s8, r8):
+                 s1, r1, s2, r2, s3, r3, s4, r4, s5, r5, s6, r6, s7, r7, s8, r8) = rest
     mh, md, heads = dims
     me = lax.axis_index('dap')
     y, x, c = position(me, side)
@@ -332,10 +333,15 @@
     barrier = pltpu.get_barrier_semaphore()
     for k in range(1, n):
         pl.semaphore_signal(barrier, inc=1, device_id={'dap': lax.rem(me + k, n)}, device_id_type=MESH)
-    loads = [pltpu.make_async_copy(src, dst, load_sem.at[i]) for i, (src, dst) in enumerate(
-        [(m_hbm, m_ref), (mask_hbm, mask_ref), (ow_hbm, ow_ref), (sq_hbm, sq_ref), (eq_hbm, eq_ref)])]
-    for load in loads:
-        load.start()
+    loads = [pltpu.make_async_copy(src, dst, load_sem.at[i]) for i, (src, dst) in enumerate(zip(operands, loaded))]
+    urgent = [1, 4]
+    for i in urgent:
+        loads[i].start()
+    for i in range(n_ops):
+        if i not in urgent:
+            loads[i].start()
+    for i in urgent:
+        loads[i].wait()
 
     for i in range(r):
         for t in range(side):
@@ -346,8 +352,9 @@
     gathers = exchange_all(rbox, lambda p: rmsg, sa, ra)
     rows_to_block(me, side, z_ref, zblk, sb, rb)
 
-    loads[0].wait()
-    loads[1].wait()
+    for i in range(n_ops):
+        if i not in urgent:
+            loads[i].wait()
     smask[...] = mask_ref[pl.ds(pl.multiple_of(me * seq, seq), seq), :].astype(F32)
     wt_row[...] = ro_ref[...].astype(F32).T.astype(BF16)
     wt_col[...] = co_ref[...].astype(F32).T.astype(BF16)
@@ -399,12 +406,10 @@
     def count_pairs():
         step = seq
 
-        def add(t, _):
+        def add(t, total):
             rows = mask_ref[pl.ds(pl.multiple_of(t * step, step), step), :].astype(F32)
-            pairs_buf[...] += dot(rows.T.astype(BF16), rows.astype(BF16))
-            return 0
-        pairs_buf[...] = jnp.zeros_like(pairs_buf)
-        lax.fori_loop(0, mask_ref.shape[0] // step, add, 0)
+            return total + dot(rows.T.astype(BF16), rows.astype(BF16))
+        pairs_buf[...] = lax.fori_loop(0, mask_ref.shape[0] // step, add, jnp.zeros((res, res), F32), unroll=8)
         size = (w // 2 * w, res)
         row = lax.broadcasted_iota(jnp.int32, size, 0)
         lane = lax.broadcasted_iota(jnp.int32, size, 1)
@@ -420,8 +425,6 @@
             for i in range(128 // e):
                 opmw_buf[(f * (128 // e) + i) * e:(f * (128 // e) + i + 1) * e, :] = rows_f
 
-    for load in loads[2:]:
-        load.wait()
     proj = att_buf
     count = []
 
@@ -528,12 +531,12 @@
         product(chunk, 0, fresh)
         product(chunk, 1, fresh)
 
-    lax.fori_loop(0, e // 4, turn_a, 0)
+    lax.fori_loop(0, e // 4, turn_a, 0, unroll=2)
     for b in range(side):
         a_send[b] = a_f32[b * blk:(b + 1) * blk].astype(BF16)
     send_first(0)
     spread(0, 0)
-    lax.fori_loop(0, e // 4, turn_c, 0)
+    lax.fori_loop(0, e // 4, turn_c, 0, unroll=2)
     send_first(1)
     spread(1, 0)
     a_buf[0, 0, :, :seq] = a_send[y]
@@ -563,15 +566,14 @@
     relay(two)
     wait_passed(one)
     products((two, 0))
-    rest = [(one, 1), (three, 1), (two, 1)]
+    products((one, 1))
     wait_passed(three)
+    products((three, 1))
     wait_passed(two)
-    for chunk in rest:
-        product(chunk, 0)
+    product((two, 1), 0)
     swap = remote(acc.at[0], got, s4, r4, dev(y, x, 1 - c))
     swap.start()
-    for chunk in rest:
-        product(chunk, 1)
+    product((two, 1), 1)
     for k in order[1:]:
         first[0][k].wait_send()
         first[1][k].wait_send()
@@ -683,8 +685,7 @@
     buf = vm((side, half_of(side), blk, 2 * seq), BF16)
     tall = vm((seq, width, res), BF16)
     box = vm((3, n, 2 * r * r, pc), BF16)
-    large = [0, 2, 12, 14, 17]
-    scratch = [vm(ops[i].shape, ops[i].dtype) for i in large] + [dma((len(large) + 1,))]
+    scratch = [vm(op.shape, op.dtype) for op in ops] + [dma((len(ops) + 1,))]
     scratch += [vm((seq, res), F32), tall, vm((seq, res, width + 16), BF16), tall, tall, vm((seq, width, res), F32),
                vm((2, mh // 2, res, 2 * res), F32), vm((2, mh // 2, res, 2 * res), BF16), vm((2, mh // 2, 8, 2 * res), F32),
                vm((mh // 2, res, 2 * res), F32), vm((mh // 2, width, 2 * res), BF16), vm((n + 1, r * mh, res), BF16), vm((n * r * mh, res), F32),
@@ -700,9 +701,9 @@
                dma((2, side)), dma((2, side)), dma((2, side, 2)), dma((2, side, 2)), dma((2, side, 2)), dma((2, side, 2)),
                dma, dma, dma((side,)), dma((side,))] + [dma((n,))] * 6
     return pl.pallas_call(
-        functools.partial(block_kernel, n, side, dims),
+        functools.partial(block_kernel, n, side, dims, len(ops)),
         out_shape=[jax.ShapeDtypeStruct((seq, ch, res), BF16), jax.ShapeDtypeStruct((r, res, pc), BF16)],
-        in_specs=[pl.BlockSpec(memory_space=pl.ANY) if i in large else vmem() for i in range(len(ops))],
+        in_specs=[pl.BlockSpec(memory_space=pl.ANY)] * len(ops),
         out_specs=[pl.BlockSpec(memory_space=pl.ANY), vmem()], scratch_shapes=scratch,
         compiler_params=pltpu.CompilerParams(collective_id=0, has_side_effects=True, vmem_limit_bytes=63 * 1024 * 1024),
         name='evoformer_block')(*ops)

time: 163 us -> 159 us (0.975)
  Pallas kernels: 159 us -> 154 us
    pallas_call x1, Pallas kernels: 159 us -> 154 us  [block_call(): pl.pallas_call(functools.partial(block_kernel, n, side, dims, len(ops)),...]
where the time goes in v7:
time: 159 us; the launch traced here: 158 us
  Pallas kernels  154 us (97%)
  local copies, waits for them, and re-layouts  3.77 us (2%)
    pallas_call x1, Pallas kernels, block_call(): pl.pallas_call(functools.partial(block_kernel, n, side, dims, len(ops)),...  154 us
    unnamed x4, local copies, waits for them, and re-layouts  3.77 us

profile of v7, /device:TPU:97, one launch (start us, length us, event | category | flops | bytes accessed | tf_op | source)
XLA Modules:
  0.0 158.5 jit_solution(16845719831527568890)
XLA Ops:
  0.6 154.1 %evoformer_block.1 = (bf16[128,64,128]{2,1,0:T(8,128)(2,1)}, bf16[4,128,128]{2,1,0:T(8,128)(2,1)}) custom-call(bf16[128,64,128]{2,1,0:T(8,128)(2,1)} %bitcast.33, bf16[4,4,32,128]{3,2,1,0:T(8,128)(2,1)} %bitcast.36, s32[4096,128]{1,0:T(8,128)} %refs_2_.1, s32[1,128]{1,0:T(1,128)} %bitcast.51, bf16[8,128]{1,0:T(8,128)(2,1)} %bitcast.48, ...), custom_call_target="tpu_custom_call" | custom-call | tf_op jit(solution)/shard_map/evoformer_block/pallas_call | solution.py:703
  154.7 0.0 copy-start
  154.7 3.1 %copy.23 = bf16[128,128,64]{1,2,0:T(8,128)(2,1)} copy(bf16[128,128,64]{1,2,0:T(8,128)(2,1)} %bitcast.34) | data formatting | bytes 4194304
  157.8 0.0 copy-done
  157.8 0.7 copy.24
Async XLA Ops:
  154.7 3.1 %copy-start = (bf16[4,128,128]{2,1,0:T(8,128)(2,1)S(1)}, bf16[4,128,128]{2,1,0:T(8,128)(2,1)}, u32[]{:S(2)}) copy-start(bf16[4,128,128]{2,1,0:T(8,128)(2,1)} %get-tuple-element.9) | copy-start | bytes 393220

commit v8 on v7

--- a/solution.py
+++ b/solution.py
@@ -67,7 +67,7 @@
             extra = jnp.where(row == 0, terms[0], jnp.where(row == 1, terms[1], jnp.where(row == 2, terms[2], 0.0))) * off
             k_buf[s] = jnp.concatenate([proj[width:2 * width, u * res:(u + 1) * res], extra], axis=0).T.astype(BF16)
         return 0
-    lax.fori_loop(0, seq // BLOCK, step, 0, unroll=2)
+    lax.fori_loop(0, seq // BLOCK, step, 0, unroll=4)
 
 
 def row_attend(heads, hd, bias_ref, pick_ref, q_buf, k_buf, v_buf, att_buf, raw_buf, w_buf, den_buf):
@@ -101,14 +101,14 @@
         weigh(0, p)
 
     def step(t, _):
-        for u in range(4):
-            s = 4 * t + u
+        for u in range(8):
+            s = 8 * t + u
             for p in range(pairs):
                 logits(jnp.minimum(s + 2, seq - 1), u % 2, p)
                 weigh((u + 1) % 2, p)
                 values(s, u % 2, p)
         return 0
-    lax.fori_loop(0, seq // 4, step, 0)
+    lax.fori_loop(0, seq // 8, step, 0)
 
 
 def row_finish(m_ref, mask_ref, wo_ref, g_buf, att_buf, new_ref, ln_ref):
@@ -135,7 +135,7 @@
         put(key_buf, g, kv[:hd])
         put(val_buf, g, kv[hd:])
         return 0
-    lax.fori_loop(0, seq // BLOCK, step, 0, unroll=2)
+    lax.fori_loop(0, seq // BLOCK, step, 0, unroll=4)
 
 
 def col_gates(ln_ref, wg_ref, gate_buf):
@@ -145,7 +145,7 @@
         gate = jnp.dot(wg_ref[...], wide(ln_ref, g), preferred_element_type=F32).astype(BF16).astype(F32)
         put(gate_buf, g, jax.nn.sigmoid(gate))
         return 0
-    lax.fori_loop(0, seq // BLOCK, step, 0, unroll=2)
+    lax.fori_loop(0, seq // BLOCK, step, 0, unroll=4)
 
 
 def col_sums(query, mask_ref, key_buf, val_buf):
@@ -196,7 +196,7 @@
             s = g * BLOCK + u
             proj_ref[s] = (proj[:, u * res:(u + 1) * res].astype(F32) * mask_ref[pl.ds(s, 1), :]).astype(proj_ref.dtype)
         return 0
-    lax.fori_loop(0, seq // BLOCK, step, 0, unroll=2)
+    lax.fori_loop(0, seq // BLOCK, step, 0, unroll=4)
 
 
 def remote(src, dst, send_sem, recv_sem, dev):
@@ -320,10 +320,16 @@
     def dev(yy, xx, cc):
         return (yy * side + xx) * 2 + cc
 
+    def ring(d):
+        return min(d, side - d)
+
+    steps = [(dy, dx, dc) for dy in range(side) for dx in range(side) for dc in range(2) if dy + dx + dc]
+    steps.sort(key=lambda t: -(ring(t[0]) + ring(t[1])))
+    peers = [((dy * side + dx) * 2 + dc, dev(lax.rem(y + dy, side), lax.rem(x + dx, side), lax.rem(c + dc, 2))) for dy, dx, dc in steps]
+
     def exchange_all(box, src_of, send_sem, recv_sem):
         copies = []
-        for k in range(1, n):
-            dst = lax.rem(me + k, n)
+        for k, dst in peers:
             cp = remote(src_of(dst), box.at[me], send_sem.at[k], recv_sem.at[k], dst)
             cp.start()
             copies.append(cp)
@@ -331,8 +337,8 @@
         return copies
 
     barrier = pltpu.get_barrier_semaphore()
-    for k in range(1, n):
-        pl.semaphore_signal(barrier, inc=1, device_id={'dap': lax.rem(me + k, n)}, device_id_type=MESH)
+    for _, dst in peers:
+        pl.semaphore_signal(barrier, inc=1, device_id={'dap': dst}, device_id_type=MESH)
     loads = [pltpu.make_async_copy(src, dst, load_sem.at[i]) for i, (src, dst) in enumerate(zip(operands, loaded))]
     urgent = [1, 4]
     for i in urgent:
@@ -380,8 +386,7 @@
             for p in range(n):
                 cut[p, t] = turned[p * own:(p + 1) * own]
         copies = []
-        for k in range(1, n):
-            dst = lax.rem(me + k, n)
+        for k, dst in peers:
             cp = remote(cut.at[dst, :terms_n], got1.at[me, :terms_n], send1.at[k], recv1.at[k], dst)
             cp.start()
             copies.append(cp)
@@ -394,8 +399,8 @@
         mine[slot_id] = total
         back[slot_id, me] = total
         copies = []
-        for k in range(1, n):
-            cp = remote(mine.at[slot_id], back.at[slot_id, me], send2.at[k], recv2.at[k], lax.rem(me + k, n))
+        for k, dst in peers:
+            cp = remote(mine.at[slot_id], back.at[slot_id, me], send2.at[k], recv2.at[k], dst)
             cp.start()
             copies.append(cp)
         beside2()

time: 159 us -> 155 us (0.975)
  Pallas kernels: 154 us -> 150 us
    pallas_call x1, Pallas kernels: 154 us -> 150 us  [block_call(): pl.pallas_call(functools.partial(block_kernel, n, side, dims, len(ops)),...]
where the time goes in v8:
time: 155 us
  Pallas kernels  150 us (97%)
  local copies, waits for them, and re-layouts  3.77 us (2%)
    pallas_call x1, Pallas kernels, block_call(): pl.pallas_call(functools.partial(block_kernel, n, side, dims, len(ops)),...  150 us
    unnamed x4, local copies, waits for them, and re-layouts  3.77 us

profile of v8, /device:TPU:97, one launch (start us, length us, event | category | flops | bytes accessed | tf_op | source)
XLA Modules:
  0.0 154.8 jit_solution(12094385776971533736)
XLA Ops:
  0.6 150.3 %evoformer_block.1 = (bf16[128,64,128]{2,1,0:T(8,128)(2,1)}, bf16[4,128,128]{2,1,0:T(8,128)(2,1)}) custom-call(bf16[128,64,128]{2,1,0:T(8,128)(2,1)} %bitcast.33, bf16[4,4,32,128]{3,2,1,0:T(8,128)(2,1)} %bitcast.36, s32[4096,128]{1,0:T(8,128)} %refs_2_.1, s32[1,128]{1,0:T(1,128)} %bitcast.51, bf16[8,128]{1,0:T(8,128)(2,1)} %bitcast.48, ...), custom_call_target="tpu_custom_call" | custom-call | tf_op jit(solution)/shard_map/evoformer_block/pallas_call | solution.py:708
  151.0 0.0 copy-start
  151.0 3.1 %copy.23 = bf16[128,128,64]{1,2,0:T(8,128)(2,1)} copy(bf16[128,128,64]{1,2,0:T(8,128)(2,1)} %bitcast.34) | data formatting | bytes 4194304
  154.1 0.0 copy-done
  154.1 0.7 copy.24
Async XLA Ops:
  151.0 3.1 %copy-start = (bf16[4,128,128]{2,1,0:T(8,128)(2,1)S(1)}, bf16[4,128,128]{2,1,0:T(8,128)(2,1)}, u32[]{:S(2)}) copy-start(bf16[4,128,128]{2,1,0:T(8,128)(2,1)} %get-tuple-element.9) | copy-start | bytes 393220

commit v9 on v8

--- a/solution.py
+++ b/solution.py
@@ -101,14 +101,14 @@
         weigh(0, p)
 
     def step(t, _):
-        for u in range(8):
-            s = 8 * t + u
+        for u in range(16):
+            s = 16 * t + u
             for p in range(pairs):
                 logits(jnp.minimum(s + 2, seq - 1), u % 2, p)
                 weigh((u + 1) % 2, p)
                 values(s, u % 2, p)
         return 0
-    lax.fori_loop(0, seq // 8, step, 0)
+    lax.fori_loop(0, seq // 16, step, 0)
 
 
 def row_finish(m_ref, mask_ref, wo_ref, g_buf, att_buf, new_ref, ln_ref):

time: 155 us -> 154 us (level)
  no operation moved by 1% of the time
where the time goes in v9:
time: 154 us; the launch traced here: 153 us
  Pallas kernels  149 us (97%)
  local copies, waits for them, and re-layouts  3.77 us (2%)
    pallas_call x1, Pallas kernels, block_call(): pl.pallas_call(functools.partial(block_kernel, n, side, dims, len(ops)),...  149 us
    unnamed x4, local copies, waits for them, and re-layouts  3.77 us

profile of v9, /device:TPU:97, one launch (start us, length us, event | category | flops | bytes accessed | tf_op | source)
XLA Modules:
  0.0 153.5 jit_solution(7486134221246803135)
XLA Ops:
  0.6 149.1 %evoformer_block.1 = (bf16[128,64,128]{2,1,0:T(8,128)(2,1)}, bf16[4,128,128]{2,1,0:T(8,128)(2,1)}) custom-call(bf16[128,64,128]{2,1,0:T(8,128)(2,1)} %bitcast.33, bf16[4,4,32,128]{3,2,1,0:T(8,128)(2,1)} %bitcast.36, s32[4096,128]{1,0:T(8,128)} %refs_2_.1, s32[1,128]{1,0:T(1,128)} %bitcast.51, bf16[8,128]{1,0:T(8,128)(2,1)} %bitcast.48, ...), custom_call_target="tpu_custom_call" | custom-call | tf_op jit(solution)/shard_map/evoformer_block/pallas_call | solution.py:708
  149.7 0.0 copy-start
  149.7 3.1 %copy.23 = bf16[128,128,64]{1,2,0:T(8,128)(2,1)} copy(bf16[128,128,64]{1,2,0:T(8,128)(2,1)} %bitcast.34) | data formatting | bytes 4194304
  152.8 0.0 copy-done
  152.8 0.7 copy.24
Async XLA Ops:
  149.7 3.1 %copy-start = (bf16[4,128,128]{2,1,0:T(8,128)(2,1)S(1)}, bf16[4,128,128]{2,1,0:T(8,128)(2,1)}, u32[]{:S(2)}) copy-start(bf16[4,128,128]{2,1,0:T(8,128)(2,1)} %get-tuple-element.9) | copy-start | bytes 393220
